TPU v7x, 256 devices: a whole 4x4x8 slice. The times are simulated.
256 devices in a mesh: row: 8 (over y, core), col: 32 (over x, z).
Axes of the slice: x: 4, y: 4, z: 8, core: 2. Of those that a mesh axis runs over, the one named last changes fastest.
Arguments:
- residual: bfloat16 [2048, 32768], P('row', 'col'), may hold values from -6 to 6
- strip_weights: bfloat16 [2048, 512], P('row'), may hold values from -0.375 to 0.375
- bin_weights: bfloat16 [8, 32768, 4096], P('row', 'col'), may hold values from -0.375 to 0.375
- touched: int32 [8, 32, 32], P('row', 'col'), may hold values 0 or 1
- image: float32 [4096, 4096], P('row', 'col'), may hold values from -6 to 6
- precond: float32 [4096, 4096], P('row', 'col'), may hold values from 0.05 to 1.35, as said below
Outputs:
- updated: float32 [4096, 4096], P('row', 'col')
- mean_change: float32 [], replicated
Inputs may be any that keep to these rules, and one draw needn't show every extreme that they name: `precond`: positive.
All inputs are finite; a program needn't handle non-finite values. No bound on the sum of `touched` on one device may be relied on, other than what follows from the above.
Results may differ from a plain program's by a relative error of at most 0.0023.
Values sent between devices are 32-bit elements; how exact they have to be, the bound alone decides.
No kernel may reach another device: no remote copies, remote signals or barrier semaphores. Data moves between devices by JAX's collectives and lax.ppermute only.
A program may use at most 64 MiB of HBM per device.

v0:
```python
import functools

import jax
import jax.numpy as jnp
from jax import lax
from jax.sharding import Mesh
from jax.sharding import PartitionSpec as P

ITERS = 10
COL = ("col_0", "col_1")
ROW = ("row_0", "row_1")
ROW_COL = ("row_0", "row_1", "col_0", "col_1")


tv_weight = 0.25
dual_step = 0.125
radius = 0.25
epsilon = 1e-06


def sum_by_axis(so_far, axes):
    for axis in axes:
        so_far = lax.psum_scatter(so_far, axis, scatter_dimension=0, tiled=True)
    return so_far


def over_axes(array, axes):
    return functools.reduce(lax.psum, axes, array)


def padded_2(array, sides, width):
    for axis, dim in sides:
        peers, length = (lax.axis_size(axis), array.shape[dim])
        up = [(i, (i + 1) % peers) for i in range(peers - 1)]
        down = [(j, i) for i, j in up]
        last = lax.slice_in_dim(array, length - width, length, axis=dim)
        initial = lax.slice_in_dim(array, 0, width, axis=dim)
        before = lax.ppermute(last, axis, up)
        after = lax.ppermute(initial, axis, down)
        array = jnp.concatenate([before, array, after], axis=dim)
    return array


def passed_along(value, axis, steps):
    count = lax.axis_size(axis)
    initial, last = (max(0, -steps), min(count, count - steps))
    return lax.ppermute(value, axis, [(source, source + steps) for source in range(initial, last)])


def advance(dual, value_band, first_row, first_col, total_rows, total_cols):
    height = dual.shape[1]
    breadth = dual.shape[2]
    potential = (
        dual[0, 1:, 1:]
        - dual[0, :-1, 1:]
        + (dual[1, 1:, 1:] - dual[1, 1:, :-1])
        - value_band[1:, 1:]
    )
    grad_down = potential[1:, :-1] - potential[:-1, :-1]
    grad_right = potential[:-1, 1:] - potential[:-1, :-1]
    row_ids = first_row + 1 + lax.broadcasted_iota(jnp.int32, (height - 2, breadth - 2), 0)
    col_ids = first_col + 1 + lax.broadcasted_iota(jnp.int32, (height - 2, breadth - 2), 1)
    inside = (row_ids >= 0) & (row_ids < total_rows) & (col_ids >= 0) & (col_ids < total_cols)
    grad_down = jnp.where(inside & (row_ids < total_rows - 1), grad_down, 0.0)
    grad_right = jnp.where(inside & (col_ids < total_cols - 1), grad_right, 0.0)
    magnitude = jnp.sqrt(grad_down * grad_down + grad_right * grad_right)
    divisor = 1.0 + dual_step * magnitude
    interior = dual[:, 1:-1, 1:-1]
    return (interior + dual_step * jnp.stack([grad_down, grad_right])) / divisor


def local(residual, strip_weights, bin_weights, touched, image, precond):
    tile_rows = image.shape[0]
    tile_cols = image.shape[1]
    weights_flat = bin_weights[0]
    tile_marks = touched[0, 0].astype(jnp.float32)
    chosen = weights_flat
    chosen = chosen.reshape(chosen.shape[0], 1 * lax.axis_size(COL), tile_cols)
    product = jnp.einsum("ad,dct->cat", residual, chosen, preferred_element_type=jnp.float32)
    summed = sum_by_axis(product * tile_marks[:, None, None], COL)[0]
    strip_float = strip_weights.astype(jnp.float32)
    gradient = jnp.einsum("ar,at->rt", strip_float, summed, precision=lax.Precision.HIGHEST)
    total_rows = tile_rows * lax.axis_size(ROW)
    total_cols = tile_cols * lax.axis_size(COL)
    cell_total = float(total_rows * total_cols)
    step_dir = precond * gradient
    square_sum = over_axes(jnp.sum(step_dir * step_dir), ROW_COL)
    spread = jnp.sqrt(square_sum / cell_total + epsilon)
    factor = jnp.minimum(1.0, radius / spread)
    source = image - factor * step_dir
    scaled = source / tv_weight
    row_first = lax.axis_index(ROW) * tile_rows
    col_first = lax.axis_index(COL) * tile_cols
    starting = jnp.zeros((2, tile_rows, tile_cols), jnp.float32)
    scaled_band = padded_2(scaled, ((ROW, 0), (COL, 1)), 2)

    def deep_turn(turn_index, dual):
        padded = padded_2(dual, ((ROW, 1), (COL, 2)), 2)
        middle = advance(padded, scaled_band, row_first - 2, col_first - 2, total_rows, total_cols)
        return advance(
            middle, scaled_band[1:-1, 1:-1], row_first - 1, col_first - 1, total_rows, total_cols
        )

    dual = lax.fori_loop(0, ITERS // 2, deep_turn, starting)
    upper = passed_along(dual[0, -1:, :], ROW, 1)
    leftward = passed_along(dual[1, :, -1:], COL, 1)
    above = jnp.concatenate([upper, dual[0, :-1, :]], 0)
    beside = jnp.concatenate([leftward, dual[1, :, :-1]], 1)
    divergence = dual[0] - above + (dual[1] - beside)
    updated = source - tv_weight * divergence
    change = updated - image
    mean_change = over_axes(jnp.sum(change * change), ROW_COL) / cell_total
    return (updated, mean_change)


def solution(mesh):
    split = Mesh(mesh.devices.reshape(4, 2, 4, 8), ("row_0", "row_1", "col_0", "col_1"))
    placed = (
        P(ROW, COL),
        P(ROW, None),
        P(ROW, COL, None),
        P(ROW, COL, None),
        P(ROW, COL),
        P(ROW, COL),
    )
    return jax.shard_map(
        local, mesh=split, in_specs=placed, out_specs=(P(ROW, COL), P()), check_vma=False
    )
```

profile of v0, /device:TPU:32, one launch (start us, length us, event | category | flops | bytes accessed | tf_op | source)
XLA Modules:
  0.0 343.4 jit_solution(9859548678065450244)
XLA Ops:
  7.2 12.0 %copy.42 = bf16[1,1024,4096]{1,2,0:T(8,128)(2,1)} copy(bf16[1,1024,4096]{2,1,0:T(8,128)(2,1)} %param.10) | data formatting | bytes 16777216 | tf_op jit(solution)/shard_map/reshape;squeeze | solution.py:78
  19.3 7.8 %multiply_bitcast_fusion = f32[32,256,128]{1,2,0:T(8,128)} fusion(bf16[1024,32,128]{0,2,1:T(8,128)(2,1)} %bitcast.53, f32[32]{0:T(128)S(1)} %convert_bitcast_fusion, bf16[256,1024]{1,0:T(8,128)(2,1)S(1)} %copy-done), kind=kOutput, calls=%fused_computation.55 | convolution fusion | flops 2148532224 | bytes 13107328 | tf_op jit(solution)/shard_map/ad,dct->cat/dot_general | solution.py:79
  27.2 52.1 %reduce-scatter.3.cloned.1.call-done = f32[8,256,128]{1,2,0:T(8,128)} async-done(((f32[32,256,128]{1,2,0:T(8,128)}), f32[8,256,128]{1,2,0:T(8,128)}) %reduce-scatter.3.cloned.1.call-update) | async-done | bytes 1048592 | tf_op jit(solution)/shard_map/reduce_scatter | solution.py:23
  79.4 40.5 %reduce-scatter.5.cloned.1.call-done = f32[1,256,128]{1,2,0:T(8,128)} async-done(((f32[8,256,128]{1,2,0:T(8,128)}), f32[1,256,128]{1,2,0:T(8,128)}) %reduce-scatter.5.cloned.1.call-update) | async-done | bytes 131088 | tf_op jit(solution)/shard_map/reduce_scatter | solution.py:23
  121.8 11.1 %psum.56 = f32[]{:T(128)} all-reduce(f32[]{:T(128)} %get-tuple-element.234), channel_id=1, replica_groups=mesh['row_0'=4,'row_1'=2,'col_0'=4,'col_1'=8] {'row_0'}, use_global_device_ids=true, to_apply=%region_3.0 | all-reduce | flops 1 | bytes 8 | tf_op jit(solution)/shard_map/psum | solution.py:28
  132.8 3.1 psum.57
  135.9 11.0 %psum.58 = f32[]{:T(128)} all-reduce(f32[]{:T(128)} %psum.57), channel_id=1, replica_groups=mesh['row_0'=4,'row_1'=2,'col_0'=4,'col_1'=8] {'col_0'}, use_global_device_ids=true, to_apply=%region_5.0 | all-reduce | flops 1 | bytes 8 | tf_op jit(solution)/shard_map/psum | solution.py:28
  147.1 15.9 %psum.59 = f32[]{:T(128)} all-reduce(f32[]{:T(128)} %psum.58), channel_id=1, replica_groups=mesh['row_0'=4,'row_1'=2,'col_0'=4,'col_1'=8] {'col_1'}, use_global_device_ids=true, to_apply=%region_6.0 | all-reduce | flops 1 | bytes 8 | tf_op jit(solution)/shard_map/psum | solution.py:28
  168.3 2.8 collective-permute-start.6
  171.1 3.1 collective-permute-start.7
  174.2 2.4 collective-permute-done.7
  176.8 92.5 %while.15 = (s32[]{:T(128)}, f32[2,512,128]{1,2,0:T(8,128)S(1)}, s32[]{:T(128)}, s32[]{:T(128)}, f32[516,132]{0,1:T(8,128)S(1)}, /*index=5*/s32[]{:T(128)}, s32[]{:T(128)}, s32[]{:T(128)}, s32[]{:T(128)}) while((s32[]{:T(128)}, f32[2,512,128]{1,2,0:T(8,128)S(1)}, s32[]{:T(128)}, s32[]{:T(128)}, f32[516,132]{0,1:T(8,128)S(1)}, ...), condition=%wide.region_8.9_spmd.clone, body=%wide.region_7.8_spmd.clone.sunk | while | flops 4004691 | bytes 12869747 | solution.py:104
  178.3 3.9 %collective-permute-start.1 = (f32[2,2,128]{1,2,0:T(8,128)S(1)}, f32[2,2,128]{1,2,0:T(8,128)S(1)}, u32[]{:S(2)}, u32[]{:S(2)}) collective-permute-start(f32[2,2,128]{1,2,0:T(8,128)S(1)} %get-tuple-element.298), channel_id=1, source_target_pairs={{0,32},{32,64},{64,96},{96,128},{128,160},{160,192},{192,224},{1,3... | collective-permute-start | bytes 6152 | tf_op jit(solution)/shard_map/while/body/eval_jaxpr/ppermute | solution.py:38
  183.2 3.1 collective-permute-start.2
  186.3 3.5 %collective-permute-start.3 = (f32[2,516,2]{1,2,0:T(2,128)S(1)}, f32[2,516,2]{1,2,0:T(2,128)S(1)}, u32[]{:S(2)}, u32[]{:S(2)}) collective-permute-start(f32[2,516,2]{1,2,0:T(2,128)S(1)} %get-tuple-element.300), channel_id=1, source_target_pairs={{0,1},{1,2},{2,3},{3,4},{4,5},{5,6},{6,7},{7,8},{8,9},{9,10},{10,1... | collective-permute-start | bytes 24776 | tf_op jit(solution)/shard_map/while/body/eval_jaxpr/ppermute | solution.py:38
  189.8 2.1 collective-permute-done.3
  195.7 3.8 %collective-permute-start.1 = (f32[2,2,128]{1,2,0:T(8,128)S(1)}, f32[2,2,128]{1,2,0:T(8,128)S(1)}, u32[]{:S(2)}, u32[]{:S(2)}) collective-permute-start(f32[2,2,128]{1,2,0:T(8,128)S(1)} %get-tuple-element.298), channel_id=1, source_target_pairs={{0,32},{32,64},{64,96},{96,128},{128,160},{160,192},{192,224},{1,3... | collective-permute-start | bytes 6152 | tf_op jit(solution)/shard_map/while/body/eval_jaxpr/ppermute | solution.py:38
  200.6 1.9 collective-permute-start.2
  202.5 4.7 %collective-permute-start.3 = (f32[2,516,2]{1,2,0:T(2,128)S(1)}, f32[2,516,2]{1,2,0:T(2,128)S(1)}, u32[]{:S(2)}, u32[]{:S(2)}) collective-permute-start(f32[2,516,2]{1,2,0:T(2,128)S(1)} %get-tuple-element.300), channel_id=1, source_target_pairs={{0,1},{1,2},{2,3},{3,4},{4,5},{5,6},{6,7},{7,8},{8,9},{9,10},{10,1... | collective-permute-start | bytes 24776 | tf_op jit(solution)/shard_map/while/body/eval_jaxpr/ppermute | solution.py:38
  212.4 5.9 %collective-permute-start.1 = (f32[2,2,128]{1,2,0:T(8,128)S(1)}, f32[2,2,128]{1,2,0:T(8,128)S(1)}, u32[]{:S(2)}, u32[]{:S(2)}) collective-permute-start(f32[2,2,128]{1,2,0:T(8,128)S(1)} %get-tuple-element.298), channel_id=1, source_target_pairs={{0,32},{32,64},{64,96},{96,128},{128,160},{160,192},{192,224},{1,3... | collective-permute-start | bytes 6152 | tf_op jit(solution)/shard_map/while/body/eval_jaxpr/ppermute | solution.py:38
  221.4 5.1 %collective-permute-start.3 = (f32[2,516,2]{1,2,0:T(2,128)S(1)}, f32[2,516,2]{1,2,0:T(2,128)S(1)}, u32[]{:S(2)}, u32[]{:S(2)}) collective-permute-start(f32[2,516,2]{1,2,0:T(2,128)S(1)} %get-tuple-element.300), channel_id=1, source_target_pairs={{0,1},{1,2},{2,3},{3,4},{4,5},{5,6},{6,7},{7,8},{8,9},{9,10},{10,1... | collective-permute-start | bytes 24776 | tf_op jit(solution)/shard_map/while/body/eval_jaxpr/ppermute | solution.py:38
  231.7 5.9 %collective-permute-start.1 = (f32[2,2,128]{1,2,0:T(8,128)S(1)}, f32[2,2,128]{1,2,0:T(8,128)S(1)}, u32[]{:S(2)}, u32[]{:S(2)}) collective-permute-start(f32[2,2,128]{1,2,0:T(8,128)S(1)} %get-tuple-element.298), channel_id=1, source_target_pairs={{0,32},{32,64},{64,96},{96,128},{128,160},{160,192},{192,224},{1,3... | collective-permute-start | bytes 6152 | tf_op jit(solution)/shard_map/while/body/eval_jaxpr/ppermute | solution.py:38
  238.7 1.9 collective-permute-start.2
  240.7 5.4 %collective-permute-start.3 = (f32[2,516,2]{1,2,0:T(2,128)S(1)}, f32[2,516,2]{1,2,0:T(2,128)S(1)}, u32[]{:S(2)}, u32[]{:S(2)}) collective-permute-start(f32[2,516,2]{1,2,0:T(2,128)S(1)} %get-tuple-element.300), channel_id=1, source_target_pairs={{0,1},{1,2},{2,3},{3,4},{4,5},{5,6},{6,7},{7,8},{8,9},{9,10},{10,1... | collective-permute-start | bytes 24776 | tf_op jit(solution)/shard_map/while/body/eval_jaxpr/ppermute | solution.py:38
  251.3 5.9 %collective-permute-start.1 = (f32[2,2,128]{1,2,0:T(8,128)S(1)}, f32[2,2,128]{1,2,0:T(8,128)S(1)}, u32[]{:S(2)}, u32[]{:S(2)}) collective-permute-start(f32[2,2,128]{1,2,0:T(8,128)S(1)} %get-tuple-element.298), channel_id=1, source_target_pairs={{0,32},{32,64},{64,96},{96,128},{128,160},{160,192},{192,224},{1,3... | collective-permute-start | bytes 6152 | tf_op jit(solution)/shard_map/while/body/eval_jaxpr/ppermute | solution.py:38
  260.2 5.4 %collective-permute-start.3 = (f32[2,516,2]{1,2,0:T(2,128)S(1)}, f32[2,516,2]{1,2,0:T(2,128)S(1)}, u32[]{:S(2)}, u32[]{:S(2)}) collective-permute-start(f32[2,516,2]{1,2,0:T(2,128)S(1)} %get-tuple-element.300), channel_id=1, source_target_pairs={{0,1},{1,2},{2,3},{3,4},{4,5},{5,6},{6,7},{7,8},{8,9},{9,10},{10,1... | collective-permute-start | bytes 24776 | tf_op jit(solution)/shard_map/while/body/eval_jaxpr/ppermute | solution.py:38
  269.5 5.3 %collective-permute-start.8 = (f32[1,128]{0,1:T(8,128)S(1)}, f32[1,128]{0,1:T(8,128)S(1)}, u32[]{:S(2)}, u32[]{:S(2)}) collective-permute-start(f32[1,128]{0,1:T(8,128)S(1)} %slice_bitcast_fusion.2), channel_id=1, source_target_pairs={{0,32},{32,64},{64,96},{96,128},{128,160},{160,192},{192,224},{1,3... | collective-permute-start | bytes 1544 | tf_op jit(solution)/shard_map/ppermute | solution.py:47
  274.8 5.4 %collective-permute-start.9 = (f32[512,1]{0,1:T(1,128)S(1)}, f32[512,1]{0,1:T(1,128)S(1)}, u32[]{:S(2)}, u32[]{:S(2)}) collective-permute-start(f32[512,1]{0,1:T(1,128)S(1)} %slice_bitcast_fusion.3), channel_id=1, source_target_pairs={{0,1},{1,2},{2,3},{3,4},{4,5},{5,6},{6,7},{7,8},{8,9},{9,10},{10,1... | collective-permute-start | bytes 6152 | tf_op jit(solution)/shard_map/ppermute | solution.py:47
  282.3 11.9 %psum.60 = f32[]{:T(128)} all-reduce(f32[]{:T(128)} %get-tuple-element.210), channel_id=1, replica_groups=mesh['row_0'=4,'row_1'=2,'col_0'=4,'col_1'=8] {'row_0'}, use_global_device_ids=true, to_apply=%region_10.11 | all-reduce | flops 1 | bytes 8 | tf_op jit(solution)/shard_map/psum | solution.py:28
  294.2 3.1 psum.61
  297.3 17.8 %psum.62 = f32[]{:T(128)} all-reduce(f32[]{:T(128)} %psum.61), channel_id=1, replica_groups=mesh['row_0'=4,'row_1'=2,'col_0'=4,'col_1'=8] {'col_0'}, use_global_device_ids=true, to_apply=%region_12.13 | all-reduce | flops 1 | bytes 8 | tf_op jit(solution)/shard_map/psum | solution.py:28
  315.9 18.9 %psum.63 = f32[]{:T(128)} all-reduce(f32[]{:T(128)} %psum.62), channel_id=1, replica_groups=mesh['row_0'=4,'row_1'=2,'col_0'=4,'col_1'=8] {'col_1'}, use_global_device_ids=true, to_apply=%region_13.14 | all-reduce | flops 1 | bytes 8 | tf_op jit(solution)/shard_map/psum | solution.py:28
  (142 shorter events, 43.1 us)
Async XLA Ops:
  7.2 12.1 %copy-start = (bf16[256,1024]{1,0:T(8,128)(2,1)S(1)}, bf16[256,1024]{1,0:T(8,128)(2,1)}, u32[]{:S(2)}) copy-start(bf16[256,1024]{1,0:T(8,128)(2,1)} %param.8) | copy-start | bytes 1572868
  7.2 72.1 %reduce-scatter.3.cloned.1.call-start = ((), (), s32[]{:S(2)}) async-start(), calls=%async_computation.2 | async-start | bytes 5242880 | tf_op jit(solution)/shard_map/reduce_scatter | solution.py:23
  19.3 60.0 %copy-start.2 = (f32[512,128]{1,0:T(8,128)S(1)}, f32[512,128]{1,0:T(8,128)}, u32[]{:S(2)}) copy-start(f32[512,128]{1,0:T(8,128)} %param.13) | copy-start | bytes 786436
  19.3 100.7 %copy-start.1 = (bf16[256,512]{1,0:T(8,128)(2,1)S(1)}, bf16[256,512]{1,0:T(8,128)(2,1)}, u32[]{:S(2)}) copy-start(bf16[256,512]{1,0:T(8,128)(2,1)} %param.9) | copy-start | bytes 786436
  19.3 127.7 %copy-start.3 = (f32[512,128]{1,0:T(8,128)S(1)}, f32[512,128]{1,0:T(8,128)}, u32[]{:S(2)}) copy-start(f32[512,128]{1,0:T(8,128)} %param.12) | copy-start | bytes 786436
  27.1 92.8 %reduce-scatter.5.cloned.1.call-start = ((), (), s32[]{:S(2)}) async-start(), calls=%async_computation.3 | async-start | bytes 1179648 | tf_op jit(solution)/shard_map/reduce_scatter | solution.py:23
  163.8 2.6 collective-permute-start.4
  165.1 3.1 collective-permute-start.5
  168.3 5.9 %collective-permute-start.6 = (f32[516,2]{0,1:T(2,128)S(1)}, f32[516,2]{0,1:T(2,128)S(1)}, u32[]{:S(2)}, u32[]{:S(2)}) collective-permute-start(f32[516,2]{0,1:T(2,128)S(1)} %get-tuple-element.230), channel_id=1, source_target_pairs={{0,1},{1,2},{2,3},{3,4},{4,5},{5,6},{6,7},{7,8},{8,9},{9,10},{10,1... | collective-permute-start | bytes 12392 | tf_op jit(solution)/shard_map/ppermute | solution.py:38
  171.1 5.5 %collective-permute-start.7 = (f32[516,2]{0,1:T(2,128)S(1)}, f32[516,2]{0,1:T(2,128)S(1)}, u32[]{:S(2)}, u32[]{:S(2)}) collective-permute-start(f32[516,2]{0,1:T(2,128)S(1)} %get-tuple-element.231), channel_id=1, source_target_pairs={{1,0},{2,1},{3,2},{4,3},{5,4},{6,5},{7,6},{8,7},{9,8},{10,9},{11,1... | collective-permute-start | bytes 12392 | tf_op jit(solution)/shard_map/ppermute | solution.py:39
  177.0 5.3 %collective-permute-start = (f32[2,2,128]{1,2,0:T(8,128)S(1)}, f32[2,2,128]{1,2,0:T(8,128)S(1)}, u32[]{:S(2)}, u32[]{:S(2)}) collective-permute-start(f32[2,2,128]{1,2,0:T(8,128)S(1)} %get-tuple-element.297), channel_id=1, source_target_pairs={{32,0},{64,32},{96,64},{128,96},{160,128},{192,160},{224,192},{33,... | collective-permute-start | bytes 6152 | tf_op jit(solution)/shard_map/while/body/eval_jaxpr/ppermute | solution.py:39
  178.3 4.9 %collective-permute-start.1 = (f32[2,2,128]{1,2,0:T(8,128)S(1)}, f32[2,2,128]{1,2,0:T(8,128)S(1)}, u32[]{:S(2)}, u32[]{:S(2)}) collective-permute-start(f32[2,2,128]{1,2,0:T(8,128)S(1)} %get-tuple-element.298), channel_id=1, source_target_pairs={{0,32},{32,64},{64,96},{96,128},{128,160},{160,192},{192,224},{1,3... | collective-permute-start | bytes 6152 | tf_op jit(solution)/shard_map/while/body/eval_jaxpr/ppermute | solution.py:38
  183.2 6.6 %collective-permute-start.2 = (f32[2,516,2]{1,2,0:T(2,128)S(1)}, f32[2,516,2]{1,2,0:T(2,128)S(1)}, u32[]{:S(2)}, u32[]{:S(2)}) collective-permute-start(f32[2,516,2]{1,2,0:T(2,128)S(1)} %get-tuple-element.299), channel_id=1, source_target_pairs={{1,0},{2,1},{3,2},{4,3},{5,4},{6,5},{7,6},{8,7},{9,8},{10,9},{11,1... | collective-permute-start | bytes 24776 | tf_op jit(solution)/shard_map/while/body/eval_jaxpr/ppermute | solution.py:39
  186.3 5.6 %collective-permute-start.3 = (f32[2,516,2]{1,2,0:T(2,128)S(1)}, f32[2,516,2]{1,2,0:T(2,128)S(1)}, u32[]{:S(2)}, u32[]{:S(2)}) collective-permute-start(f32[2,516,2]{1,2,0:T(2,128)S(1)} %get-tuple-element.300), channel_id=1, source_target_pairs={{0,1},{1,2},{2,3},{3,4},{4,5},{5,6},{6,7},{7,8},{8,9},{9,10},{10,1... | collective-permute-start | bytes 24776 | tf_op jit(solution)/shard_map/while/body/eval_jaxpr/ppermute | solution.py:38
  194.4 5.2 %collective-permute-start = (f32[2,2,128]{1,2,0:T(8,128)S(1)}, f32[2,2,128]{1,2,0:T(8,128)S(1)}, u32[]{:S(2)}, u32[]{:S(2)}) collective-permute-start(f32[2,2,128]{1,2,0:T(8,128)S(1)} %get-tuple-element.297), channel_id=1, source_target_pairs={{32,0},{64,32},{96,64},{128,96},{160,128},{192,160},{224,192},{33,... | collective-permute-start | bytes 6152 | tf_op jit(solution)/shard_map/while/body/eval_jaxpr/ppermute | solution.py:39
  195.7 4.8 %collective-permute-start.1 = (f32[2,2,128]{1,2,0:T(8,128)S(1)}, f32[2,2,128]{1,2,0:T(8,128)S(1)}, u32[]{:S(2)}, u32[]{:S(2)}) collective-permute-start(f32[2,2,128]{1,2,0:T(8,128)S(1)} %get-tuple-element.298), channel_id=1, source_target_pairs={{0,32},{32,64},{64,96},{96,128},{128,160},{160,192},{192,224},{1,3... | collective-permute-start | bytes 6152 | tf_op jit(solution)/shard_map/while/body/eval_jaxpr/ppermute | solution.py:38
  200.6 6.7 %collective-permute-start.2 = (f32[2,516,2]{1,2,0:T(2,128)S(1)}, f32[2,516,2]{1,2,0:T(2,128)S(1)}, u32[]{:S(2)}, u32[]{:S(2)}) collective-permute-start(f32[2,516,2]{1,2,0:T(2,128)S(1)} %get-tuple-element.299), channel_id=1, source_target_pairs={{1,0},{2,1},{3,2},{4,3},{5,4},{6,5},{7,6},{8,7},{9,8},{10,9},{11,1... | collective-permute-start | bytes 24776 | tf_op jit(solution)/shard_map/while/body/eval_jaxpr/ppermute | solution.py:39
  202.5 6.1 %collective-permute-start.3 = (f32[2,516,2]{1,2,0:T(2,128)S(1)}, f32[2,516,2]{1,2,0:T(2,128)S(1)}, u32[]{:S(2)}, u32[]{:S(2)}) collective-permute-start(f32[2,516,2]{1,2,0:T(2,128)S(1)} %get-tuple-element.300), channel_id=1, source_target_pairs={{0,1},{1,2},{2,3},{3,4},{4,5},{5,6},{6,7},{7,8},{8,9},{9,10},{10,1... | collective-permute-start | bytes 24776 | tf_op jit(solution)/shard_map/while/body/eval_jaxpr/ppermute | solution.py:38
  211.1 7.3 %collective-permute-start = (f32[2,2,128]{1,2,0:T(8,128)S(1)}, f32[2,2,128]{1,2,0:T(8,128)S(1)}, u32[]{:S(2)}, u32[]{:S(2)}) collective-permute-start(f32[2,2,128]{1,2,0:T(8,128)S(1)} %get-tuple-element.297), channel_id=1, source_target_pairs={{32,0},{64,32},{96,64},{128,96},{160,128},{192,160},{224,192},{33,... | collective-permute-start | bytes 6152 | tf_op jit(solution)/shard_map/while/body/eval_jaxpr/ppermute | solution.py:39
  212.4 6.9 %collective-permute-start.1 = (f32[2,2,128]{1,2,0:T(8,128)S(1)}, f32[2,2,128]{1,2,0:T(8,128)S(1)}, u32[]{:S(2)}, u32[]{:S(2)}) collective-permute-start(f32[2,2,128]{1,2,0:T(8,128)S(1)} %get-tuple-element.298), channel_id=1, source_target_pairs={{0,32},{32,64},{64,96},{96,128},{128,160},{160,192},{192,224},{1,3... | collective-permute-start | bytes 6152 | tf_op jit(solution)/shard_map/while/body/eval_jaxpr/ppermute | solution.py:38
  219.4 7.1 %collective-permute-start.2 = (f32[2,516,2]{1,2,0:T(2,128)S(1)}, f32[2,516,2]{1,2,0:T(2,128)S(1)}, u32[]{:S(2)}, u32[]{:S(2)}) collective-permute-start(f32[2,516,2]{1,2,0:T(2,128)S(1)} %get-tuple-element.299), channel_id=1, source_target_pairs={{1,0},{2,1},{3,2},{4,3},{5,4},{6,5},{7,6},{8,7},{9,8},{10,9},{11,1... | collective-permute-start | bytes 24776 | tf_op jit(solution)/shard_map/while/body/eval_jaxpr/ppermute | solution.py:39
  221.4 6.5 %collective-permute-start.3 = (f32[2,516,2]{1,2,0:T(2,128)S(1)}, f32[2,516,2]{1,2,0:T(2,128)S(1)}, u32[]{:S(2)}, u32[]{:S(2)}) collective-permute-start(f32[2,516,2]{1,2,0:T(2,128)S(1)} %get-tuple-element.300), channel_id=1, source_target_pairs={{0,1},{1,2},{2,3},{3,4},{4,5},{5,6},{6,7},{7,8},{8,9},{9,10},{10,1... | collective-permute-start | bytes 24776 | tf_op jit(solution)/shard_map/while/body/eval_jaxpr/ppermute | solution.py:38
  230.4 7.3 %collective-permute-start = (f32[2,2,128]{1,2,0:T(8,128)S(1)}, f32[2,2,128]{1,2,0:T(8,128)S(1)}, u32[]{:S(2)}, u32[]{:S(2)}) collective-permute-start(f32[2,2,128]{1,2,0:T(8,128)S(1)} %get-tuple-element.297), channel_id=1, source_target_pairs={{32,0},{64,32},{96,64},{128,96},{160,128},{192,160},{224,192},{33,... | collective-permute-start | bytes 6152 | tf_op jit(solution)/shard_map/while/body/eval_jaxpr/ppermute | solution.py:39
  231.7 6.9 %collective-permute-start.1 = (f32[2,2,128]{1,2,0:T(8,128)S(1)}, f32[2,2,128]{1,2,0:T(8,128)S(1)}, u32[]{:S(2)}, u32[]{:S(2)}) collective-permute-start(f32[2,2,128]{1,2,0:T(8,128)S(1)} %get-tuple-element.298), channel_id=1, source_target_pairs={{0,32},{32,64},{64,96},{96,128},{128,160},{160,192},{192,224},{1,3... | collective-permute-start | bytes 6152 | tf_op jit(solution)/shard_map/while/body/eval_jaxpr/ppermute | solution.py:38
  238.7 7.4 %collective-permute-start.2 = (f32[2,516,2]{1,2,0:T(2,128)S(1)}, f32[2,516,2]{1,2,0:T(2,128)S(1)}, u32[]{:S(2)}, u32[]{:S(2)}) collective-permute-start(f32[2,516,2]{1,2,0:T(2,128)S(1)} %get-tuple-element.299), channel_id=1, source_target_pairs={{1,0},{2,1},{3,2},{4,3},{5,4},{6,5},{7,6},{8,7},{9,8},{10,9},{11,1... | collective-permute-start | bytes 24776 | tf_op jit(solution)/shard_map/while/body/eval_jaxpr/ppermute | solution.py:39
  240.7 6.8 %collective-permute-start.3 = (f32[2,516,2]{1,2,0:T(2,128)S(1)}, f32[2,516,2]{1,2,0:T(2,128)S(1)}, u32[]{:S(2)}, u32[]{:S(2)}) collective-permute-start(f32[2,516,2]{1,2,0:T(2,128)S(1)} %get-tuple-element.300), channel_id=1, source_target_pairs={{0,1},{1,2},{2,3},{3,4},{4,5},{5,6},{6,7},{7,8},{8,9},{9,10},{10,1... | collective-permute-start | bytes 24776 | tf_op jit(solution)/shard_map/while/body/eval_jaxpr/ppermute | solution.py:38
  250.0 7.3 %collective-permute-start = (f32[2,2,128]{1,2,0:T(8,128)S(1)}, f32[2,2,128]{1,2,0:T(8,128)S(1)}, u32[]{:S(2)}, u32[]{:S(2)}) collective-permute-start(f32[2,2,128]{1,2,0:T(8,128)S(1)} %get-tuple-element.297), channel_id=1, source_target_pairs={{32,0},{64,32},{96,64},{128,96},{160,128},{192,160},{224,192},{33,... | collective-permute-start | bytes 6152 | tf_op jit(solution)/shard_map/while/body/eval_jaxpr/ppermute | solution.py:39
  251.3 6.9 %collective-permute-start.1 = (f32[2,2,128]{1,2,0:T(8,128)S(1)}, f32[2,2,128]{1,2,0:T(8,128)S(1)}, u32[]{:S(2)}, u32[]{:S(2)}) collective-permute-start(f32[2,2,128]{1,2,0:T(8,128)S(1)} %get-tuple-element.298), channel_id=1, source_target_pairs={{0,32},{32,64},{64,96},{96,128},{128,160},{160,192},{192,224},{1,3... | collective-permute-start | bytes 6152 | tf_op jit(solution)/shard_map/while/body/eval_jaxpr/ppermute | solution.py:38
  258.3 7.4 %collective-permute-start.2 = (f32[2,516,2]{1,2,0:T(2,128)S(1)}, f32[2,516,2]{1,2,0:T(2,128)S(1)}, u32[]{:S(2)}, u32[]{:S(2)}) collective-permute-start(f32[2,516,2]{1,2,0:T(2,128)S(1)} %get-tuple-element.299), channel_id=1, source_target_pairs={{1,0},{2,1},{3,2},{4,3},{5,4},{6,5},{7,6},{8,7},{9,8},{10,9},{11,1... | collective-permute-start | bytes 24776 | tf_op jit(solution)/shard_map/while/body/eval_jaxpr/ppermute | solution.py:39
  260.2 6.8 %collective-permute-start.3 = (f32[2,516,2]{1,2,0:T(2,128)S(1)}, f32[2,516,2]{1,2,0:T(2,128)S(1)}, u32[]{:S(2)}, u32[]{:S(2)}) collective-permute-start(f32[2,516,2]{1,2,0:T(2,128)S(1)} %get-tuple-element.300), channel_id=1, source_target_pairs={{0,1},{1,2},{2,3},{3,4},{4,5},{5,6},{6,7},{7,8},{8,9},{9,10},{10,1... | collective-permute-start | bytes 24776 | tf_op jit(solution)/shard_map/while/body/eval_jaxpr/ppermute | solution.py:38
  269.5 10.8 %collective-permute-start.8 = (f32[1,128]{0,1:T(8,128)S(1)}, f32[1,128]{0,1:T(8,128)S(1)}, u32[]{:S(2)}, u32[]{:S(2)}) collective-permute-start(f32[1,128]{0,1:T(8,128)S(1)} %slice_bitcast_fusion.2), channel_id=1, source_target_pairs={{0,32},{32,64},{64,96},{96,128},{128,160},{160,192},{192,224},{1,3... | collective-permute-start | bytes 1544 | tf_op jit(solution)/shard_map/ppermute | solution.py:47
  274.8 6.7 %collective-permute-start.9 = (f32[512,1]{0,1:T(1,128)S(1)}, f32[512,1]{0,1:T(1,128)S(1)}, u32[]{:S(2)}, u32[]{:S(2)}) collective-permute-start(f32[512,1]{0,1:T(1,128)S(1)} %slice_bitcast_fusion.3), channel_id=1, source_target_pairs={{0,1},{1,2},{2,3},{3,4},{4,5},{5,6},{6,7},{7,8},{8,9},{9,10},{10,1... | collective-permute-start | bytes 6152 | tf_op jit(solution)/shard_map/ppermute | solution.py:47
  (1 other events, 12.1 us)
Sparse Core Ops, SparseCore 0:
  27.2 51.9 reduce-scatter.2
  81.8 38.0 reduce-scatter.4
where the time goes:
time: 345 us; the launch traced here: 343 us
  waiting for transfers between devices  110 us (32%)
  blocking collectives  92.8 us (27%)
  starting transfers between devices  86.1 us (25%)
  between operations  16.7 us (5%)
  local copies, waits for them, and re-layouts  13.8 us (4%)
  other arithmetic  13.7 us (4%)
  matrix products  9.64 us (3%)
    psum x8, blocking collectives, over_axes(): return functools.reduce(lax.psum, axes, array)  92.8 us
    reduce_scatter x2, waiting for transfers between devices, sum_by_axis(): so_far = lax.psum_scatter(so_far, axis, scatter_dimension=0, tiled=True)  92.6 us
    ppermute x12, starting transfers between devices, padded_2(): before = lax.ppermute(last, axis, up)  53.7 us
    ppermute x12, starting transfers between devices, padded_2(): after = lax.ppermute(initial, axis, down)  21.6 us
    another operation x1, local copies, waits for them, and re-layouts, local(): chosen = chosen.reshape(chosen.shape[0], 1 * lax.axis_size(COL), tile_cols)  12 us
    ppermute x12, waiting for transfers between devices, padded_2(): before = lax.ppermute(last, axis, up)  11.8 us
    ppermute x2, starting transfers between devices, passed_along(): lax.ppermute(value, axis, [(source, source + steps) for source in range(i...  10.7 us
    dot_general x1, matrix products, local(): jnp.einsum('ad,dct->cat', residual, chosen, preferred_element_type=jnp.fl...  7.81 us
  transfers between devices with their start and end apart: 28, of which 15 were waited for; matrix products, arithmetic and copies ran while one was open for 0% of the time, Pallas kernels for 0%

commit v1 on v0

v1 whole, which is shorter than its diff:
```python
import functools

import jax
import jax.numpy as jnp
from jax import lax
from jax.experimental import pallas as pl
from jax.experimental.pallas import tpu as pltpu
from jax.sharding import Mesh
from jax.sharding import PartitionSpec as P

ITERS = 10
COL = ("col_0", "col_1")
ROW = ("row_0", "row_1")
ROW_COL = ("row_0", "row_1", "col_0", "col_1")

tv_weight = 0.25
dual_step = 0.125
radius = 0.25
epsilon = 1e-06

HALO = 16
LANES = 128
BASE = 8


def vmem():
    return pl.BlockSpec(memory_space=pltpu.VMEM)


def smem():
    return pl.BlockSpec(memory_space=pltpu.SMEM)


def back_project_kernel(marks, residual, weights, out, *, tiles, per_x):
    first = (pl.program_id(0) * per_x) + pl.program_id(1) * tiles
    product = jnp.dot(residual[...], weights[...], preferred_element_type=jnp.float32)
    for k in range(tiles):
        mark = marks[0, first + k].astype(jnp.float32)
        out[k, 0] = product[:, k * LANES:(k + 1) * LANES] * mark


def back_project(residual, weights, marks, n_x, n_z):
    angles, bins = residual.shape
    tiles = 4
    return pl.pallas_call(
        functools.partial(back_project_kernel, tiles=tiles, per_x=n_z),
        grid=(n_x, n_z // tiles),
        in_specs=[
            smem(),
            pl.BlockSpec((angles, bins), lambda x, h: (0, 0)),
            pl.BlockSpec((None, bins, tiles * LANES), lambda x, h: (0, 0, x * (n_z // tiles) + h)),
        ],
        out_specs=pl.BlockSpec((tiles, 1, angles, LANES), lambda x, h: (h, x, 0, 0)),
        out_shape=jax.ShapeDtypeStruct((n_z, n_x, angles, LANES), jnp.float32),
    )(marks, residual, weights)


def exact_parts(value):
    high = value.astype(jnp.bfloat16)
    rest = value - high.astype(jnp.float32)
    middle = rest.astype(jnp.bfloat16)
    low = (rest - middle.astype(jnp.float32)).astype(jnp.bfloat16)
    return high, middle, low


def gradient_kernel(place, parts, strip, precond, step_dir, slots, *, n_row):
    summed = parts[0]
    for k in range(1, parts.shape[0]):
        summed = summed + parts[k]
    gradient = None
    for piece in reversed(exact_parts(summed)):
        term = jnp.dot(strip[...], piece, preferred_element_type=jnp.float32)
        gradient = term if gradient is None else gradient + term
    value = precond[...] * gradient
    step_dir[...] = value
    rows = value.shape[0]
    squares = value * value
    partial = squares[0:8]
    for k in range(1, rows // 8):
        partial = partial + squares[8 * k:8 * k + 8]
    own = place[0]
    initial = value[0:HALO]
    last = value[rows - HALO:rows]
    for k in range(n_row):
        slots[k, 0:HALO] = jnp.where(own < k, last, initial)
        slots[k, HALO:HALO + 8] = partial


def make_gradient(place, parts, strip, precond, n_row):
    rows = strip.shape[0]
    return pl.pallas_call(
        functools.partial(gradient_kernel, n_row=n_row),
        in_specs=[smem(), vmem(), vmem(), vmem()],
        out_specs=[vmem(), vmem()],
        out_shape=[
            jax.ShapeDtypeStruct((rows, LANES), jnp.float32),
            jax.ShapeDtypeStruct((n_row, HALO + 8, LANES), jnp.float32),
        ],
    )(place, parts, strip, precond)


def edges_kernel(place, received, step_dir, leftward, rightward, slots, padded, *, n_row):
    own = place[0]
    rows = step_dir.shape[0]
    padded[0:HALO] = received[jnp.maximum(own - 1, 0), 0:HALO]
    padded[HALO:HALO + rows] = step_dir[...]
    padded[HALO + rows:rows + 2 * HALO] = received[jnp.minimum(own + 1, n_row - 1), 0:HALO]
    padded[rows + 2 * HALO:] = jnp.zeros((padded.shape[0] - rows - 2 * HALO, LANES), jnp.float32)
    for k in range(padded.shape[0] // LANES):
        block = padded[k * LANES:(k + 1) * LANES].T
        leftward[:, k * LANES:(k + 1) * LANES] = block[0:HALO]
        rightward[:, k * LANES:(k + 1) * LANES] = block[LANES - HALO:]
    partial = received[0, HALO:HALO + 8]
    for k in range(1, n_row):
        partial = partial + received[k, HALO:HALO + 8]
    total = jnp.sum(partial, axis=0, keepdims=True)
    slots[...] = jnp.broadcast_to(total[None], slots.shape)


def make_edges(place, received, step_dir, n_row, n_col):
    rows = step_dir.shape[0]
    length = -(-(rows + 2 * HALO) // LANES) * LANES
    edge = jax.ShapeDtypeStruct((HALO, length), jnp.float32)
    return pl.pallas_call(
        functools.partial(edges_kernel, n_row=n_row),
        in_specs=[smem(), vmem(), vmem()],
        out_specs=[vmem(), vmem(), vmem()],
        out_shape=[edge, edge, jax.ShapeDtypeStruct((n_col, 1, LANES), jnp.float32)],
        scratch_shapes=[pltpu.VMEM((length, LANES), jnp.float32)],
    )(place, received, step_dir)


def denoise_kernel(
    place, sums, received, step_dir, from_right, from_left, image_main, image_side,
    updated, slots, scaled, down, right, potential, down_mask, right_mask,
    *, n_row, n_col,
):
    own_row, own_col = place[0], place[1]
    rows = step_dir.shape[0]
    band = rows + 2 * HALO
    cells = float(n_row * rows * n_col * LANES)
    square_sum = jnp.sum(jnp.sum(sums[...], axis=0), axis=1, keepdims=True)
    spread = jnp.sqrt(square_sum / cells + epsilon)
    factor = jnp.minimum(1.0, radius / spread)

    zero = jnp.zeros((2, 8, LANES), jnp.float32)
    for plane in (scaled, down, right, potential):
        plane[:, 0:BASE] = zero
        plane[:, BASE + band:BASE + band + 8] = zero

    lane = lax.broadcasted_iota(jnp.int32, (8, LANES), 1)
    sub = lax.broadcasted_iota(jnp.int32, (8, LANES), 0)
    first_lane = lane == 0
    last_lane = lane == LANES - 1
    total_rows = n_row * rows
    total_cols = n_col * LANES
    columns = (
        own_col * LANES + lane,
        own_col * LANES + lane + jnp.where(lane < LANES // 2, LANES, -LANES),
    )
    column_in = [(c >= 0) & (c < total_cols) for c in columns]
    column_not_last = [(c >= 0) & (c < total_cols - 1) for c in columns]
    for at in range(BASE, BASE + band, 8):
        row = own_row * rows + (at - BASE - HALO) + sub
        row_in = (row >= 0) & (row < total_rows)
        row_not_last = (row >= 0) & (row < total_rows - 1)
        for t in range(2):
            down_mask[t, at:at + 8] = jnp.where(row_not_last & column_in[t], dual_step, 0.0)
            right_mask[t, at:at + 8] = jnp.where(row_in & column_not_last[t], dual_step, 0.0)
            down[t, at:at + 8] = zero[0]
            right[t, at:at + 8] = zero[0]

    scaled[0, BASE:BASE + HALO] = received[jnp.maximum(own_row - 1, 0), 0:HALO]
    scaled[0, BASE + HALO + rows:BASE + band] = received[jnp.minimum(own_row + 1, n_row - 1), 0:HALO]
    gap = jnp.zeros((LANES - 2 * HALO, LANES), jnp.float32)
    for k in range(from_right.shape[1] // LANES):
        here = slice(k * LANES, (k + 1) * LANES)
        block = jnp.concatenate([from_right[:, here], gap, from_left[:, here]], axis=0).T
        count = min(LANES, band - k * LANES)
        scaled[1, BASE + k * LANES:BASE + k * LANES + count] = block[0:count]
    for at in range(BASE, BASE + band, 8):
        from_tile = BASE + HALO <= at < BASE + HALO + rows
        direction = step_dir[at - BASE - HALO:at - BASE - HALO + 8] if from_tile else scaled[0, at:at + 8]
        scaled[0, at:at + 8] = (image_main[at - BASE:at - BASE + 8] - factor * direction) / tv_weight
        scaled[1, at:at + 8] = (image_side[at - BASE:at - BASE + 8] - factor * scaled[1, at:at + 8]) / tv_weight

    def right_divergence(at, t):
        mine = right[t, at:at + 8]
        rolled = pltpu.roll(mine, 1, 1)
        across = pltpu.roll(right[1 - t, at:at + 8], 1, 1)
        return mine - jnp.where(first_lane, across, rolled)

    def turn(_, carry):
        for at in range(BASE, BASE + band, 8):
            rolled = [pltpu.roll(right[t, at:at + 8], 1, 1) for t in range(2)]
            for t in range(2):
                beside = jnp.where(first_lane, rolled[1 - t], rolled[t])
                potential[t, at:at + 8] = (
                    (down[t, at:at + 8] - down[t, at - 1:at + 7])
                    + (right[t, at:at + 8] - beside)
                    - scaled[t, at:at + 8]
                )
        for at in range(BASE, BASE + band, 8):
            here = [potential[t, at:at + 8] for t in range(2)]
            rolled = [pltpu.roll(here[t], LANES - 1, 1) for t in range(2)]
            for t in range(2):
                beside = jnp.where(last_lane, rolled[1 - t], rolled[t])
                step_down = (potential[t, at + 1:at + 9] - here[t]) * down_mask[t, at:at + 8]
                step_right = (beside - here[t]) * right_mask[t, at:at + 8]
                square = step_down * step_down + step_right * step_right
                size = square * lax.rsqrt(jnp.maximum(square, 1e-36))
                inverse = 1.0 / (1.0 + size)
                down[t, at:at + 8] = (down[t, at:at + 8] + step_down) * inverse
                right[t, at:at + 8] = (right[t, at:at + 8] + step_right) * inverse
        return carry

    lax.fori_loop(0, ITERS, turn, 0)

    change_sum = jnp.zeros((8, LANES), jnp.float32)
    for at in range(BASE + HALO, BASE + HALO + rows, 8):
        inner = at - BASE - HALO
        picture = image_main[at - BASE:at - BASE + 8]
        source = picture - factor * step_dir[inner:inner + 8]
        divergence = (down[0, at:at + 8] - down[0, at - 1:at + 7]) + right_divergence(at, 0)
        result = source - tv_weight * divergence
        updated[inner:inner + 8] = result
        change = result - picture
        change_sum = change_sum + change * change
    total = jnp.sum(change_sum, axis=0, keepdims=True)
    slots[...] = jnp.broadcast_to(total[None], slots.shape)


def denoise(place, sums, received, step_dir, from_right, from_left, image_main, image_side, n_row, n_col):
    rows = step_dir.shape[0]
    plane = pltpu.VMEM((2, BASE + rows + 2 * HALO + 8, LANES), jnp.float32)
    return pl.pallas_call(
        functools.partial(denoise_kernel, n_row=n_row, n_col=n_col),
        in_specs=[smem()] + [vmem()] * 7,
        out_specs=[vmem(), vmem()],
        out_shape=[
            jax.ShapeDtypeStruct((rows, LANES), jnp.float32),
            jax.ShapeDtypeStruct((n_row * n_col, 1, LANES), jnp.float32),
        ],
        scratch_shapes=[plane] * 6,
    )(place, sums, received, step_dir, from_right, from_left, image_main, image_side)


def neighbours(count):
    forward = [(i, i + 1) for i in range(count - 1)]
    return forward, [(j, i) for i, j in forward]


def image_bands(image, n_row, n_col):
    later, earlier = neighbours(n_row)
    above = lax.ppermute(image[-HALO:], ROW, later)
    below = lax.ppermute(image[:HALO], ROW, earlier)
    main = jnp.concatenate([above, image, below], axis=0)
    later, earlier = neighbours(n_col)
    left = lax.ppermute(main[:, -HALO:], COL, later)
    right = lax.ppermute(main[:, :HALO], COL, earlier)
    gap = jnp.zeros((main.shape[0], LANES - 2 * HALO), jnp.float32)
    return main, jnp.concatenate([right, gap, left], axis=1)


def local(residual, strip_weights, bin_weights, touched, image, precond):
    n_row = lax.axis_size(ROW)
    n_col = lax.axis_size(COL)
    n_x = lax.axis_size("col_0")
    n_z = lax.axis_size("col_1")
    place = jnp.stack([lax.axis_index(ROW), lax.axis_index(COL)]).astype(jnp.int32)
    angles = residual.shape[0]
    product = back_project(residual, bin_weights, touched[0], n_x, n_z)
    product, image, strip_weights = lax.optimization_barrier((product, image, strip_weights))
    by_z = lax.psum_scatter(
        product.reshape(n_z * n_x, angles, LANES), "col_1", scatter_dimension=0, tiled=True
    )
    image_main, image_side = image_bands(image, n_row, n_col)
    strip = strip_weights.T
    parts = lax.all_to_all(by_z, "col_0", 0, 0, tiled=True)
    step_dir, row_slots = make_gradient(place, parts, strip, precond, n_row)
    received = lax.all_to_all(row_slots, ROW, 0, 0, tiled=True)
    leftward, rightward, sum_slots = make_edges(place, received, step_dir, n_row, n_col)
    later, earlier = neighbours(n_col)
    from_right = lax.ppermute(leftward, COL, earlier)
    from_left = lax.ppermute(rightward, COL, later)
    sums = lax.all_to_all(sum_slots, COL, 0, 0, tiled=True)
    updated, change_slots = denoise(
        place, sums, received, step_dir, from_right, from_left, image_main, image_side, n_row, n_col
    )
    changes = lax.all_to_all(change_slots, ROW_COL, 0, 0, tiled=True)
    cells = float(n_row * image.shape[0] * n_col * image.shape[1])
    return updated, jnp.sum(changes) / cells


def solution(mesh):
    split = Mesh(mesh.devices.reshape(4, 2, 4, 8), ("row_0", "row_1", "col_0", "col_1"))
    placed = (
        P(ROW, COL),
        P(ROW, None),
        P(ROW, COL, None),
        P(ROW, COL, None),
        P(ROW, COL),
        P(ROW, COL),
    )
    return jax.shard_map(
        local, mesh=split, in_specs=placed, out_specs=(P(ROW, COL), P()), check_vma=False
    )
```

time: 345 us -> 167 us (0.48)
  blocking collectives: 92.8 us -> 26.2 us
  starting transfers between devices: 86.1 us -> 31.8 us
  waiting for transfers between devices: 110 us -> 63.2 us
  Pallas kernels: 0 us -> 21.4 us
  other arithmetic: 13.7 us -> 2.3 us
  local copies, waits for them, and re-layouts: 13.8 us -> 3.76 us
  matrix products: 9.64 us -> 0 us
    psum x8 -> x0, blocking collectives: 92.8 us -> none  [over_axes(): return functools.reduce(lax.psum, axes, array)]
    ppermute x26 -> x6, starting transfers between devices: 86 us -> 14.7 us  [the longest x1 3.7 us: local(): from_left = lax.ppermute(rightward, COL, later)]
    reduce_scatter x2 -> x1, waiting for transfers between devices: 92.6 us -> 53.3 us  [local(): lax.psum_scatter(product.reshape(n_z * n_x, angles, LANES), 'col_1', scat...]
    all_to_all x0 -> x1, blocking collectives: none -> 26.2 us  [local(): changes = lax.all_to_all(change_slots, ROW_COL, 0, 0, tiled=True)]
    pallas_call x0 -> x4, Pallas kernels: none -> 21.4 us  [the longest x1 9.2 us: back_project(): pl.pallas_call(functools.partial(back_project_kernel, tiles=tiles, per_x=...]
    ppermute x26 -> x6, waiting for transfers between devices: 17.3 us -> 0.02 us  [the longest x1 0.01 us: image_bands(): above = lax.ppermute(image[-HALO:], ROW, later)]
    all_to_all x0 -> x3, starting transfers between devices: none -> 17.1 us  [the longest x1 8.54 us: local(): sums = lax.all_to_all(sum_slots, COL, 0, 0, tiled=True)]
    another operation x1 -> x0, local copies, waits for them, and re-layouts: 12 us -> none  [local(): chosen = chosen.reshape(chosen.shape[0], 1 * lax.axis_size(COL), tile_cols)]
  transfers between devices with their start and end apart: 28 -> 10, of which waited for: 15 -> 3; matrix products, arithmetic and copies ran while one was open for 0% -> 2% of each run, Pallas kernels for 0% -> 1%
where the time goes in v1:
time: 167 us; the launch traced here: 165 us
  waiting for transfers between devices  63.2 us (38%)
  starting transfers between devices  31.8 us (19%)
  blocking collectives  26.2 us (16%)
  Pallas kernels  21.4 us (13%)
  between operations  16 us (10%)
  local copies, waits for them, and re-layouts  3.76 us (2%)
  other arithmetic  2.3 us (1%)
    reduce_scatter x1, waiting for transfers between devices, local(): lax.psum_scatter(product.reshape(n_z * n_x, angles, LANES), 'col_1', scat...  53.3 us
    all_to_all x1, blocking collectives, local(): changes = lax.all_to_all(change_slots, ROW_COL, 0, 0, tiled=True)  26.2 us
    pallas_call x1, Pallas kernels, back_project(): pl.pallas_call(functools.partial(back_project_kernel, tiles=tiles, per_x=...  9.2 us
    all_to_all x1, starting transfers between devices, local(): sums = lax.all_to_all(sum_slots, COL, 0, 0, tiled=True)  8.54 us
    pallas_call x1, Pallas kernels, denoise(): pl.pallas_call(functools.partial(denoise_kernel, n_row=n_row, n_col=n_col...  8.03 us
    all_to_all x1, waiting for transfers between devices, local(): parts = lax.all_to_all(by_z, 'col_0', 0, 0, tiled=True)  7.93 us
    all_to_all x1, starting transfers between devices, local(): received = lax.all_to_all(row_slots, ROW, 0, 0, tiled=True)  4.28 us
    all_to_all x1, starting transfers between devices, local(): parts = lax.all_to_all(by_z, 'col_0', 0, 0, tiled=True)  4.24 us
  transfers between devices with their start and end apart: 10, of which 3 were waited for; matrix products, arithmetic and copies ran while one was open for 2% of the time, Pallas kernels for 1%

profile of v1, /device:TPU:32, one launch (start us, length us, event | category | flops | bytes accessed | tf_op | source)
XLA Modules:
  0.0 164.6 jit_solution(11917056231632076144)
XLA Ops:
  7.2 0.0 reduce-scatter.2.cloned.1.call-start
  7.2 9.2 %shard_map.77 = f32[8,4,256,128]{3,2,1,0:T(8,128)} custom-call(s32[1,32]{1,0:T(1,128)} %bitcast.7, bf16[256,1024]{1,0:T(8,128)(2,1)} %residual.1, bf16[1,1024,4096]{2,1,0:T(8,128)(2,1)} %weights.1), custom_call_target="tpu_custom_call" | custom-call | tf_op jit(solution)/shard_map/pallas_call | solution.py:45
  16.4 0.0 reduce-scatter.2.cloned.1.call-update
  16.5 1.7 %collective-permute-start.2 = (f32[16,128]{1,0:T(8,128)S(1)}, f32[16,128]{1,0:T(8,128)S(1)}, u32[]{:S(2)}, u32[]{:S(2)}) collective-permute-start(f32[16,128]{1,0:T(8,128)S(1)} %get-tuple-element.25), channel_id=1, source_target_pairs={{0,32},{32,64},{64,96},{96,128},{128,160},{160,192},{192,224},{1,3... | collective-permute-start | bytes 24584 | tf_op jit(solution)/shard_map/ppermute | solution.py:255
  18.2 1.3 collective-permute-start.3
  19.5 53.3 %reduce-scatter.2.cloned.1.call-done = f32[4,256,128]{2,1,0:T(8,128)} async-done(((f32[32,256,128]{2,1,0:T(8,128)}), f32[4,256,128]{2,1,0:T(8,128)}) %reduce-scatter.2.cloned.1.call-update) | async-done | bytes 524304 | tf_op jit(solution)/shard_map/reduce_scatter | solution.py:274
  72.8 4.2 %all-to-all-start = ((f32[4,256,128]{2,1,0:T(8,128)}), f32[4,256,128]{2,1,0:T(8,128)S(1)}, u32[]{:S(2)}, u32[]{:S(2)}) async-start(f32[4,256,128]{2,1,0:T(8,128)} %reduce-scatter.2.cloned.1.call-done), calls=%async_computation.1 | async-start | bytes 1048576 | tf_op jit(solution)/shard_map/all_to_all | solution.py:279
  77.0 0.6 pad_add_fusion.place
  77.6 0.8 copy.8
  78.5 0.0 collective-permute-done.2
  78.5 7.9 %all-to-all-done.parts = f32[4,256,128]{2,1,0:T(8,128)S(1)} async-done(((f32[4,256,128]{2,1,0:T(8,128)}), f32[4,256,128]{2,1,0:T(8,128)S(1)}, u32[]{:S(2)}, u32[]{:S(2)}) %all-to-all-start) | async-done | bytes 524320 | tf_op jit(solution)/shard_map/all_to_all | solution.py:279
  86.4 0.8 copy-done.1
  87.3 2.3 %shard_map.78 = (f32[512,128]{1,0:T(8,128)}, f32[8,24,128]{2,1,0:T(8,128)}) custom-call(s32[2]{0:T(128)} %pad_add_fusion.place, f32[4,256,128]{2,1,0:T(8,128)} %copy-done.1, bf16[512,256]{1,0:T(8,128)(2,1)} %bitcast.6, f32[512,128]{1,0:T(8,128)} %precond.1), custom_call_target="tpu_custom_call" | custom-call | tf_op jit(solution)/shard_map/pallas_call | solution.py:91
  89.6 4.3 %all-to-all-start.1 = ((f32[8,24,128]{2,1,0:T(8,128)}), f32[8,24,128]{2,1,0:T(8,128)S(1)}, u32[]{:S(2)}, u32[]{:S(2)}) async-start(f32[8,24,128]{2,1,0:T(8,128)} %get-tuple-element.14), calls=%async_computation.2 | async-start | bytes 196608 | tf_op jit(solution)/shard_map/all_to_all | solution.py:281
  93.9 0.1 fusion
  94.0 3.3 %collective-permute-start.5 = (f32[544,16]{1,0:T(8,128)S(1)}, f32[544,16]{1,0:T(8,128)S(1)}, u32[]{:S(2)}, u32[]{:S(2)}) collective-permute-start(f32[544,16]{1,0:T(8,128)S(1)} %get-tuple-element.23), channel_id=1, source_target_pairs={{0,1},{1,2},{2,3},{3,4},{4,5},{5,6},{6,7},{7,8},{8,9},{9,10},{10,1... | collective-permute-start | bytes 104456 | tf_op jit(solution)/shard_map/ppermute | solution.py:259
  97.3 2.5 %collective-permute-start.4 = (f32[544,16]{1,0:T(8,128)S(1)}, f32[544,16]{1,0:T(8,128)S(1)}, u32[]{:S(2)}, u32[]{:S(2)}) collective-permute-start(f32[544,16]{1,0:T(8,128)S(1)} %get-tuple-element.22), channel_id=1, source_target_pairs={{1,0},{2,1},{3,2},{4,3},{5,4},{6,5},{7,6},{8,7},{9,8},{10,9},{11,1... | collective-permute-start | bytes 104456 | tf_op jit(solution)/shard_map/ppermute | solution.py:260
  99.9 0.1 pad.1.clone
  100.0 0.0 all-to-all-done.1.received
  100.0 0.6 copy-done.2
  100.6 1.8 %shard_map.79 = (f32[16,640]{1,0:T(8,128)}, f32[16,640]{1,0:T(8,128)}, f32[32,1,128]{2,1,0:T(1,128)}) custom-call(s32[2]{0:T(128)} %pad_add_fusion.place, f32[8,24,128]{2,1,0:T(8,128)} %copy-done.2, f32[512,128]{1,0:T(8,128)} %get-tuple-element.15.step_dir), custom_call_target="tpu_custom_call" | custom-call | tf_op jit(solution)/shard_map/pallas_call | solution.py:124
  102.4 8.5 %all-to-all-start.2 = ((f32[32,1,128]{2,1,0:T(1,128)}), f32[32,1,128]{2,1,0:T(1,128)S(1)}, u32[]{:S(2)}, u32[]{:S(2)}) async-start(f32[32,1,128]{2,1,0:T(1,128)} %get-tuple-element.16), calls=%async_computation.3 | async-start | bytes 32768 | tf_op jit(solution)/shard_map/all_to_all | solution.py:286
  110.9 2.1 %collective-permute-start = (f32[16,640]{1,0:T(8,128)}, f32[16,640]{1,0:T(8,128)S(1)}, u32[]{:S(2)}, u32[]{:S(2)}) collective-permute-start(f32[16,640]{1,0:T(8,128)} %get-tuple-element.17), channel_id=1, source_target_pairs={{1,0},{2,1},{3,2},{4,3},{5,4},{6,5},{7,6},{8,7},{9,8},{10,9},{11,1... | collective-permute-start | bytes 122888 | tf_op jit(solution)/shard_map/ppermute | solution.py:284
  113.1 3.7 %collective-permute-start.1 = (f32[16,640]{1,0:T(8,128)}, f32[16,640]{1,0:T(8,128)S(1)}, u32[]{:S(2)}, u32[]{:S(2)}) collective-permute-start(f32[16,640]{1,0:T(8,128)} %get-tuple-element.18), channel_id=1, source_target_pairs={{0,1},{1,2},{2,3},{3,4},{4,5},{5,6},{6,7},{7,8},{8,9},{9,10},{10,1... | collective-permute-start | bytes 122888 | tf_op jit(solution)/shard_map/ppermute | solution.py:285
  116.8 0.8 pad_maximum_fusion.image_side
  117.7 2.0 %all-to-all-done.2.sums = f32[32,1,128]{2,1,0:T(1,128)S(1)} async-done(((f32[32,1,128]{2,1,0:T(1,128)}), f32[32,1,128]{2,1,0:T(1,128)S(1)}, u32[]{:S(2)}, u32[]{:S(2)}) %all-to-all-start.2) | async-done | bytes 16416 | tf_op jit(solution)/shard_map/all_to_all | solution.py:286
  119.7 0.6 copy-done.5
  120.2 0.0 copy-done.6
  120.3 0.6 copy-done.7
  120.9 8.0 %shard_map.80 = (f32[512,128]{1,0:T(8,128)}, f32[256,1,128]{2,1,0:T(1,128)}) custom-call(s32[2]{0:T(128)} %pad_add_fusion.place, f32[32,1,128]{2,1,0:T(1,128)} %copy-done.5, f32[8,24,128]{2,1,0:T(8,128)} %copy-done.2, f32[512,128]{1,0:T(8,128)} %get-tuple-element.15.step_dir, f32[16,640]{1,0:T(8,128)} %copy-done.6, f32[16,640]{1,0:T(8,128)} %copy-done.7, ...), custom_call_target="tpu_custom_call" | custom-call | tf_op jit(solution)/shard_map/pallas_call | solution.py:236
  128.9 26.2 %all_to_all.20 = f32[256,1,128]{2,1,0:T(1,128)S(1)} all-to-all(f32[256,1,128]{2,1,0:T(1,128)} %get-tuple-element.21), channel_id=1, replica_groups=mesh['row_0'=4,'row_1'=2,'col_0'=4,'col_1'=8] {'row_0','row_1','col_0','..., dimensions={0} | all-to-all | bytes 262144 | tf_op jit(solution)/shard_map/all_to_all | solution.py:290
  155.2 0.9 reduce_sum.9
  (21 shorter events, 0.1 us)
Async XLA Ops:
  7.2 65.6 %reduce-scatter.2.cloned.1.call-start = ((), (), s32[]{:S(2)}) async-start(), calls=%async_computation.5 | async-start | bytes 4718592 | tf_op jit(solution)/shard_map/reduce_scatter | solution.py:274
  7.2 9.2 %copy-start.3 = (f32[512,128]{1,0:T(8,128)S(1)}, f32[512,128]{1,0:T(8,128)}, u32[]{:S(2)}) copy-start(f32[512,128]{1,0:T(8,128)} %param.10) | copy-start | bytes 786436
  7.2 70.4 %copy-start.4 = (bf16[256,512]{1,0:T(8,128)(2,1)S(1)}, bf16[256,512]{1,0:T(8,128)(2,1)}, u32[]{:S(2)}) copy-start(bf16[256,512]{1,0:T(8,128)(2,1)} %param.7) | copy-start | bytes 786436
  16.5 62.0 %collective-permute-start.2 = (f32[16,128]{1,0:T(8,128)S(1)}, f32[16,128]{1,0:T(8,128)S(1)}, u32[]{:S(2)}, u32[]{:S(2)}) collective-permute-start(f32[16,128]{1,0:T(8,128)S(1)} %get-tuple-element.25), channel_id=1, source_target_pairs={{0,32},{32,64},{64,96},{96,128},{128,160},{160,192},{192,224},{1,3... | collective-permute-start | bytes 24584 | tf_op jit(solution)/shard_map/ppermute | solution.py:255
  18.2 60.3 %collective-permute-start.3 = (f32[16,128]{1,0:T(8,128)S(1)}, f32[16,128]{1,0:T(8,128)S(1)}, u32[]{:S(2)}, u32[]{:S(2)}) collective-permute-start(f32[16,128]{1,0:T(8,128)S(1)} %get-tuple-element.24), channel_id=1, source_target_pairs={{32,0},{64,32},{96,64},{128,96},{160,128},{192,160},{224,192},{33,... | collective-permute-start | bytes 24584 | tf_op jit(solution)/shard_map/ppermute | solution.py:256
  72.8 13.7 %all-to-all-start = ((f32[4,256,128]{2,1,0:T(8,128)}), f32[4,256,128]{2,1,0:T(8,128)S(1)}, u32[]{:S(2)}, u32[]{:S(2)}) async-start(f32[4,256,128]{2,1,0:T(8,128)} %reduce-scatter.2.cloned.1.call-done), calls=%async_computation.1 | async-start | bytes 1048576 | tf_op jit(solution)/shard_map/all_to_all | solution.py:279
  78.5 41.1 %copy-start = (f32[544,128]{1,0:T(8,128)}, f32[544,128]{1,0:T(8,128)S(1)}, u32[]{:S(2)}) copy-start(f32[544,128]{1,0:T(8,128)S(1)} %constant_dynamic-update-slice_fusion.image_main) | copy-start | bytes 835588
  86.4 0.8 copy-start.1
  89.6 10.4 %all-to-all-start.1 = ((f32[8,24,128]{2,1,0:T(8,128)}), f32[8,24,128]{2,1,0:T(8,128)S(1)}, u32[]{:S(2)}, u32[]{:S(2)}) async-start(f32[8,24,128]{2,1,0:T(8,128)} %get-tuple-element.14), calls=%async_computation.2 | async-start | bytes 196608 | tf_op jit(solution)/shard_map/all_to_all | solution.py:281
  94.0 22.8 %collective-permute-start.5 = (f32[544,16]{1,0:T(8,128)S(1)}, f32[544,16]{1,0:T(8,128)S(1)}, u32[]{:S(2)}, u32[]{:S(2)}) collective-permute-start(f32[544,16]{1,0:T(8,128)S(1)} %get-tuple-element.23), channel_id=1, source_target_pairs={{0,1},{1,2},{2,3},{3,4},{4,5},{5,6},{6,7},{7,8},{8,9},{9,10},{10,1... | collective-permute-start | bytes 104456 | tf_op jit(solution)/shard_map/ppermute | solution.py:259
  97.3 19.5 %collective-permute-start.4 = (f32[544,16]{1,0:T(8,128)S(1)}, f32[544,16]{1,0:T(8,128)S(1)}, u32[]{:S(2)}, u32[]{:S(2)}) collective-permute-start(f32[544,16]{1,0:T(8,128)S(1)} %get-tuple-element.22), channel_id=1, source_target_pairs={{1,0},{2,1},{3,2},{4,3},{5,4},{6,5},{7,6},{8,7},{9,8},{10,9},{11,1... | collective-permute-start | bytes 104456 | tf_op jit(solution)/shard_map/ppermute | solution.py:260
  100.0 0.6 copy-start.2
  102.4 17.2 %all-to-all-start.2 = ((f32[32,1,128]{2,1,0:T(1,128)}), f32[32,1,128]{2,1,0:T(1,128)S(1)}, u32[]{:S(2)}, u32[]{:S(2)}) async-start(f32[32,1,128]{2,1,0:T(1,128)} %get-tuple-element.16), calls=%async_computation.3 | async-start | bytes 32768 | tf_op jit(solution)/shard_map/all_to_all | solution.py:286
  110.9 8.7 %collective-permute-start = (f32[16,640]{1,0:T(8,128)}, f32[16,640]{1,0:T(8,128)S(1)}, u32[]{:S(2)}, u32[]{:S(2)}) collective-permute-start(f32[16,640]{1,0:T(8,128)} %get-tuple-element.17), channel_id=1, source_target_pairs={{1,0},{2,1},{3,2},{4,3},{5,4},{6,5},{7,6},{8,7},{9,8},{10,9},{11,1... | collective-permute-start | bytes 122888 | tf_op jit(solution)/shard_map/ppermute | solution.py:284
  113.1 6.5 %collective-permute-start.1 = (f32[16,640]{1,0:T(8,128)}, f32[16,640]{1,0:T(8,128)S(1)}, u32[]{:S(2)}, u32[]{:S(2)}) collective-permute-start(f32[16,640]{1,0:T(8,128)} %get-tuple-element.18), channel_id=1, source_target_pairs={{0,1},{1,2},{2,3},{3,4},{4,5},{5,6},{6,7},{7,8},{8,9},{9,10},{10,1... | collective-permute-start | bytes 122888 | tf_op jit(solution)/shard_map/ppermute | solution.py:285
  119.6 0.6 copy-start.5
  119.6 0.6 copy-start.6
  120.3 0.6 copy-start.7
Sparse Core Ops, SparseCore 0:
  16.6 56.1 reduce-scatter.1

commit v2 on v1

v2 whole, which is shorter than its diff:
```python
import functools

import jax
import jax.numpy as jnp
from jax import lax
from jax.experimental import pallas as pl
from jax.experimental.pallas import tpu as pltpu
from jax.sharding import Mesh
from jax.sharding import PartitionSpec as P


ITERS = 10
COL = ("col_0", "col_1")
ROW = ("row_0", "row_1")
ROW_COL = ("row_0", "row_1", "col_0", "col_1")

tv_weight = 0.25
dual_step = 0.125
radius = 0.25
epsilon = 1e-06

HALO = 16
FIRST = 96
LANES = 128
BASE = 8


def vmem():
    return pl.BlockSpec(memory_space=pltpu.VMEM)


def smem():
    return pl.BlockSpec(memory_space=pltpu.SMEM)


def params(mebibytes):
    return pltpu.CompilerParams(vmem_limit_bytes=mebibytes * 1024 * 1024)


def back_project_kernel(marks, residual, weights, *outs, plan, splits, width, n_x, n_z):
    own = lax.axis_index("col_0")
    for o, (step, low, high) in enumerate(plan):
        x = lax.rem(own + step, n_x)
        for z in range(low, high, width):
            tile = x * n_z + z
            columns = pl.ds(pl.multiple_of(tile * LANES, width * LANES), width * LANES)
            product = jnp.dot(
                residual[...], weights[0, :, columns], preferred_element_type=jnp.float32
            )
            for t in range(width):
                mark = marks[0, tile + t].astype(jnp.float32)
                marked = product[:, t * LANES:(t + 1) * LANES] * mark
                for s, (first, last) in enumerate(splits):
                    outs[o * len(splits) + s][z - low + t] = marked[first:last]


def back_project(residual, weights, marks, plan, splits, n_x, n_z):
    outs = pl.pallas_call(
        functools.partial(
            back_project_kernel, plan=plan, splits=splits, width=4, n_x=n_x, n_z=n_z
        ),
        in_specs=[smem(), vmem(), vmem()],
        out_specs=[vmem()] * (len(plan) * len(splits)),
        out_shape=[
            jax.ShapeDtypeStruct((high - low, last - first, LANES), jnp.float32)
            for _, low, high in plan for first, last in splits
        ],
        compiler_params=params(32),
    )(marks, residual, weights)
    return [outs[i:i + len(splits)] for i in range(0, len(outs), len(splits))]


def relay_kernel(ahead, behind, from_behind, from_ahead, to_ahead, to_behind):
    half = ahead.shape[0] // 2
    for k in range(half):
        to_ahead[k] = ahead[k] + from_behind[k]
        to_ahead[half + k] = ahead[half + k]
        to_behind[k] = behind[k]
        to_behind[half + k] = behind[half + k] + from_ahead[k]


def relay(ahead, behind, from_behind, from_ahead):
    shape = jax.ShapeDtypeStruct(ahead.shape, jnp.float32)
    return pl.pallas_call(
        relay_kernel,
        in_specs=[vmem()] * 4,
        out_specs=[vmem()] * 2,
        out_shape=[shape, shape],
        compiler_params=params(8),
    )(ahead, behind, from_behind, from_ahead)


def add_up_kernel(*refs):
    *parts, out = refs
    total = parts[0][...]
    for part in parts[1:]:
        total = total + part[...]
    out[...] = total


def add_up(*parts):
    return pl.pallas_call(
        add_up_kernel,
        in_specs=[vmem()] * len(parts),
        out_specs=vmem(),
        out_shape=jax.ShapeDtypeStruct(parts[0].shape, jnp.float32),
        compiler_params=params(8),
    )(*parts)


def exact_parts(value):
    high = value.astype(jnp.bfloat16)
    rest = value - high.astype(jnp.float32)
    middle = rest.astype(jnp.bfloat16)
    low = (rest - middle.astype(jnp.float32)).astype(jnp.bfloat16)
    return high, middle, low


def gradient_kernel(*refs, n_row):
    *groups, strip, precond, image, step_dir, slots = refs
    sums = []
    for parts in groups:
        total = parts[0]
        for k in range(1, parts.shape[0]):
            total = total + parts[k]
        sums.append(total)
    summed = jnp.concatenate(sums, axis=0)
    gradient = None
    for piece in reversed(exact_parts(summed)):
        term = jnp.dot(strip[...], piece, preferred_element_type=jnp.float32)
        gradient = term if gradient is None else gradient + term
    value = precond[...] * gradient
    step_dir[...] = value
    rows = value.shape[0]
    squares = value * value
    partial = squares[0:8]
    for k in range(1, rows // 8):
        partial = partial + squares[8 * k:8 * k + 8]
    own = lax.axis_index(ROW)
    last = slice(rows - HALO, rows)
    for k in range(n_row):
        below = own < k
        slots[k, 0:HALO] = jnp.where(below, value[last], value[0:HALO])
        slots[k, HALO:2 * HALO] = jnp.where(below, image[last], image[0:HALO])
        slots[k, 2 * HALO:2 * HALO + 8] = partial


def make_gradient(groups, strip, precond, image, n_row):
    rows = strip.shape[0]
    return pl.pallas_call(
        functools.partial(gradient_kernel, n_row=n_row),
        in_specs=[vmem()] * (len(groups) + 3),
        out_specs=[vmem(), vmem()],
        out_shape=[
            jax.ShapeDtypeStruct((rows, LANES), jnp.float32),
            jax.ShapeDtypeStruct((n_row, 2 * HALO + 8, LANES), jnp.float32),
        ],
        compiler_params=params(8),
    )(*groups, strip, precond, image)


def edges_kernel(received, step_dir, image, leftward, rightward, slots, padded, *, n_row):
    own = lax.axis_index(ROW)
    rows = step_dir.shape[0]
    above = jnp.maximum(own - 1, 0)
    below = jnp.minimum(own + 1, n_row - 1)
    padded[rows + 2 * HALO:] = jnp.zeros((padded.shape[0] - rows - 2 * HALO, LANES), jnp.float32)
    for part, tile in enumerate((step_dir, image)):
        layers = slice(part * HALO, (part + 1) * HALO)
        padded[0:HALO] = received[above, layers]
        padded[HALO:HALO + rows] = tile[...]
        padded[HALO + rows:rows + 2 * HALO] = received[below, layers]
        for k in range(padded.shape[0] // LANES):
            here = slice(k * LANES, (k + 1) * LANES)
            block = padded[here].T
            leftward[layers, here] = block[0:HALO]
            rightward[layers, here] = block[LANES - HALO:]
    partial = received[0, 2 * HALO:2 * HALO + 8]
    for k in range(1, n_row):
        partial = partial + received[k, 2 * HALO:2 * HALO + 8]
    total = jnp.sum(partial, axis=0, keepdims=True)
    slots[...] = jnp.broadcast_to(total[None], slots.shape)


def make_edges(received, step_dir, image, n_row, n_col):
    rows = step_dir.shape[0]
    length = -(-(rows + 2 * HALO) // LANES) * LANES
    edge = jax.ShapeDtypeStruct((2 * HALO, length), jnp.float32)
    return pl.pallas_call(
        functools.partial(edges_kernel, n_row=n_row),
        in_specs=[vmem()] * 3,
        out_specs=[vmem(), vmem(), vmem()],
        out_shape=[edge, edge, jax.ShapeDtypeStruct((n_col, 1, LANES), jnp.float32)],
        scratch_shapes=[pltpu.VMEM((length, LANES), jnp.float32)],
        compiler_params=params(4),
    )(received, step_dir, image)


def denoise_kernel(
    sums, received, step_dir, image, from_right, from_left,
    updated, slots, scaled, down, right, potential, down_mask, right_mask,
    *, n_row, n_col,
):
    own_row, own_col = lax.axis_index(ROW), lax.axis_index(COL)
    rows = step_dir.shape[0]
    band = rows + 2 * HALO
    cells = float(n_row * rows * n_col * LANES)
    square_sum = jnp.sum(jnp.sum(sums[...], axis=0), axis=1, keepdims=True)
    spread = jnp.sqrt(square_sum / cells + epsilon)
    factor = jnp.minimum(1.0, radius / spread)

    zero = jnp.zeros((2, 8, LANES), jnp.float32)
    for plane in (scaled, down, right, potential):
        plane[:, 0:BASE] = zero
        plane[:, BASE + band:BASE + band + 8] = zero

    lane = lax.broadcasted_iota(jnp.int32, (8, LANES), 1)
    sub = lax.broadcasted_iota(jnp.int32, (8, LANES), 0)
    first_lane = lane == 0
    last_lane = lane == LANES - 1
    total_rows = n_row * rows
    total_cols = n_col * LANES
    columns = (
        own_col * LANES + lane,
        own_col * LANES + lane + jnp.where(lane < LANES // 2, LANES, -LANES),
    )
    column_in = [(c >= 0) & (c < total_cols) for c in columns]
    column_not_last = [(c >= 0) & (c < total_cols - 1) for c in columns]
    for at in range(BASE, BASE + band, 8):
        row = own_row * rows + (at - BASE - HALO) + sub
        row_in = (row >= 0) & (row < total_rows)
        row_not_last = (row >= 0) & (row < total_rows - 1)
        for t in range(2):
            down_mask[t, at:at + 8] = jnp.where(row_not_last & column_in[t], dual_step, 0.0)
            right_mask[t, at:at + 8] = jnp.where(row_in & column_not_last[t], dual_step, 0.0)
            down[t, at:at + 8] = zero[0]
            right[t, at:at + 8] = zero[0]

    def scale(direction, picture):
        return (picture - factor * direction) / tv_weight

    above = jnp.maximum(own_row - 1, 0)
    below = jnp.minimum(own_row + 1, n_row - 1)
    for there, at in ((above, BASE), (below, BASE + HALO + rows)):
        for k in range(0, HALO, 8):
            scaled[0, at + k:at + k + 8] = scale(
                received[there, k:k + 8], received[there, HALO + k:HALO + k + 8]
            )
    for at in range(0, rows, 8):
        scaled[0, BASE + HALO + at:BASE + HALO + at + 8] = scale(
            step_dir[at:at + 8], image[at:at + 8]
        )
    gap = jnp.zeros((LANES - 2 * HALO, LANES), jnp.float32)
    for k in range(from_right.shape[1] // LANES):
        here = slice(k * LANES, (k + 1) * LANES)
        edges = [
            scale(edge[0:HALO, here], edge[HALO:2 * HALO, here]) for edge in (from_right, from_left)
        ]
        block = jnp.concatenate([edges[0], gap, edges[1]], axis=0).T
        count = min(LANES, band - k * LANES)
        scaled[1, BASE + k * LANES:BASE + k * LANES + count] = block[0:count]

    def right_divergence(at, t):
        mine = right[t, at:at + 8]
        rolled = pltpu.roll(mine, 1, 1)
        across = pltpu.roll(right[1 - t, at:at + 8], 1, 1)
        return mine - jnp.where(first_lane, across, rolled)

    def turn(_, carry):
        for at in range(BASE, BASE + band, 8):
            rolled = [pltpu.roll(right[t, at:at + 8], 1, 1) for t in range(2)]
            for t in range(2):
                beside = jnp.where(first_lane, rolled[1 - t], rolled[t])
                potential[t, at:at + 8] = (
                    (down[t, at:at + 8] - down[t, at - 1:at + 7])
                    + (right[t, at:at + 8] - beside)
                    - scaled[t, at:at + 8]
                )
        for at in range(BASE, BASE + band, 8):
            here = [potential[t, at:at + 8] for t in range(2)]
            rolled = [pltpu.roll(here[t], LANES - 1, 1) for t in range(2)]
            for t in range(2):
                beside = jnp.where(last_lane, rolled[1 - t], rolled[t])
                step_down = (potential[t, at + 1:at + 9] - here[t]) * down_mask[t, at:at + 8]
                step_right = (beside - here[t]) * right_mask[t, at:at + 8]
                square = step_down * step_down + step_right * step_right
                size = square * lax.rsqrt(jnp.maximum(square, 1e-36))
                inverse = 1.0 / (1.0 + size)
                down[t, at:at + 8] = (down[t, at:at + 8] + step_down) * inverse
                right[t, at:at + 8] = (right[t, at:at + 8] + step_right) * inverse
        return carry

    lax.fori_loop(0, ITERS, turn, 0)

    change_sum = jnp.zeros((8, LANES), jnp.float32)
    for at in range(BASE + HALO, BASE + HALO + rows, 8):
        inner = at - BASE - HALO
        picture = image[inner:inner + 8]
        source = picture - factor * step_dir[inner:inner + 8]
        divergence = (down[0, at:at + 8] - down[0, at - 1:at + 7]) + right_divergence(at, 0)
        result = source - tv_weight * divergence
        updated[inner:inner + 8] = result
        change = result - picture
        change_sum = change_sum + change * change
    total = jnp.sum(change_sum, axis=0, keepdims=True)
    slots[...] = jnp.broadcast_to(total[None], slots.shape)


def denoise(sums, received, step_dir, image, from_right, from_left, n_row, n_col):
    rows = step_dir.shape[0]
    plane = pltpu.VMEM((2, BASE + rows + 2 * HALO + 8, LANES), jnp.float32)
    return pl.pallas_call(
        functools.partial(denoise_kernel, n_row=n_row, n_col=n_col),
        in_specs=[vmem()] * 6,
        out_specs=[vmem(), vmem()],
        out_shape=[
            jax.ShapeDtypeStruct((rows, LANES), jnp.float32),
            jax.ShapeDtypeStruct((n_row * n_col, 1, LANES), jnp.float32),
        ],
        scratch_shapes=[plane] * 6,
        compiler_params=params(12),
    )(sums, received, step_dir, image, from_right, from_left)


def neighbours(count):
    forward = [(i, i + 1) for i in range(count - 1)]
    return forward, [(j, i) for i, j in forward]


def step(residual, strip_weights, bin_weights, touched, image, precond):
    n_row = lax.axis_size(ROW)
    n_col = lax.axis_size(COL)
    n_x = lax.axis_size("col_0")
    n_z = lax.axis_size("col_1")
    angles = residual.shape[0]
    splits = ((0, FIRST), (FIRST, angles))
    half = n_z // 2
    marks = touched[0]
    far = back_project(
        residual, bin_weights, marks, ((2, 0, half), (2, half, n_z)), splits, n_x, n_z
    )
    far, residual = lax.optimization_barrier((far, residual))
    ring = [(i, (i + 1) % n_x) for i in range(n_x)]
    back = [(j, i) for i, j in ring]

    def both_ways(forward, backward):
        return lax.ppermute(forward, "col_0", ring), lax.ppermute(backward, "col_0", back)

    relayed = [both_ways(far[0][c], far[1][c]) for c in range(2)]
    ahead, behind, own = back_project(
        residual, bin_weights, marks,
        ((1, 0, n_z), (n_x - 1, 0, n_z), (0, 0, n_z)), splits, n_x, n_z,
    )
    outgoing = [relay(ahead[c], behind[c], *relayed[c]) for c in range(2)]
    incoming = [both_ways(*outgoing[c]) for c in range(2)]
    first = add_up(own[0], *incoming[0])
    by_z = [lax.all_to_all(first, "col_1", 0, 0, tiled=True)]
    last = add_up(own[1], *incoming[1])
    last, by_z[0] = lax.optimization_barrier((last, by_z[0]))
    by_z.append(lax.all_to_all(last, "col_1", 0, 0, tiled=True))
    strip = strip_weights.T
    step_dir, row_slots = make_gradient(by_z, strip, precond, image, n_row)
    received = lax.all_to_all(row_slots, ROW, 0, 0, tiled=True)
    leftward, rightward, sum_slots = make_edges(received, step_dir, image, n_row, n_col)
    later, earlier = neighbours(n_col)
    from_right = lax.ppermute(leftward, COL, earlier)
    from_left = lax.ppermute(rightward, COL, later)
    sums = lax.all_to_all(sum_slots, COL, 0, 0, tiled=True)
    updated, change_slots = denoise(
        sums, received, step_dir, image, from_right, from_left, n_row, n_col
    )
    changes = lax.all_to_all(change_slots, ROW_COL, 0, 0, tiled=True)
    cells = float(n_row * image.shape[0] * n_col * image.shape[1])
    return updated, jnp.sum(changes) / cells


def solution(mesh):
    split = Mesh(mesh.devices.reshape(4, 2, 4, 8), ("row_0", "row_1", "col_0", "col_1"))
    placed = (
        P(ROW, COL),
        P(ROW, None),
        P(ROW, COL, None),
        P(ROW, COL, None),
        P(ROW, COL),
        P(ROW, COL),
    )
    return jax.shard_map(
        step, mesh=split, in_specs=placed, out_specs=(P(ROW, COL), P()), check_vma=False
    )
```

time: 167 us -> 138 us (0.83)
  waiting for transfers between devices: 63.2 us -> 30.7 us
  blocking collectives: 26.2 us -> 46 us
  between operations: 16 us -> 2.5 us
  Pallas kernels: 21.4 us -> 13.9 us
  starting transfers between devices: 31.8 us -> 35.2 us
  local copies, waits for them, and re-layouts: 3.76 us -> 6.16 us
    reduce_scatter x1 -> x0, waiting for transfers between devices: 53.3 us -> none  [local(): lax.psum_scatter(product.reshape(n_z * n_x, angles, LANES), 'col_1', scat...]
    all_to_all x1 -> x3, blocking collectives: 26.2 us -> 46 us  [the longest x1 18.8 us: step(): changes = lax.all_to_all(change_slots, ROW_COL, 0, 0, tiled=True)]
    ppermute x6 -> x10, waiting for transfers between devices: 0.02 us -> 19.2 us  [the longest x4 18.9 us: both_ways(): lax.ppermute(forward, 'col_0', ring)]
    ppermute x6 -> x10, starting transfers between devices: 14.7 us -> 19.4 us  [the longest x4 8.49 us: both_ways(): lax.ppermute(backward, 'col_0', back)]
    pallas_call x2 -> x7, Pallas kernels: 11 us -> 6.55 us  [the longest x2 4.38 us: back_project(): pl.pallas_call(functools.partial(back_project_kernel, plan=plan, splits=s...]
    unnamed x18 -> x11, local copies, waits for them, and re-layouts: 2.7 us -> 6.16 us
    pallas_call x1, Pallas kernels: 2.33 us -> 0.4 us  [make_gradient(): pl.pallas_call(functools.partial(gradient_kernel, n_row=n_row), in_specs=...]
    all_to_all x3 -> x2, waiting for transfers between devices: 9.89 us -> 11.5 us  [the longest x1 11.5 us: step(): by_z.append(lax.all_to_all(last, 'col_1', 0, 0, tiled=True))]
  transfers between devices with their start and end apart: 10 -> 12, of which waited for: 3 -> 5; matrix products, arithmetic and copies ran while one was open for 2% -> 1% of each run, Pallas kernels for 1% -> 3%
where the time goes in v2:
time: 138 us; the launch traced here: 135 us
  blocking collectives  46 us (33%)
  starting transfers between devices  35.2 us (26%)
  waiting for transfers between devices  30.7 us (22%)
  Pallas kernels  13.9 us (10%)
  local copies, waits for them, and re-layouts  6.16 us (4%)
  between operations  2.5 us (2%)
    ppermute x4, waiting for transfers between devices, both_ways(): lax.ppermute(forward, 'col_0', ring)  18.9 us
    all_to_all x1, blocking collectives, step(): changes = lax.all_to_all(change_slots, ROW_COL, 0, 0, tiled=True)  18.8 us
    all_to_all x1, blocking collectives, step(): sums = lax.all_to_all(sum_slots, COL, 0, 0, tiled=True)  16.5 us
    all_to_all x1, waiting for transfers between devices, step(): by_z.append(lax.all_to_all(last, 'col_1', 0, 0, tiled=True))  11.5 us
    all_to_all x1, blocking collectives, step(): received = lax.all_to_all(row_slots, ROW, 0, 0, tiled=True)  10.7 us
    all_to_all x1, starting transfers between devices, step(): by_z = [lax.all_to_all(first, 'col_1', 0, 0, tiled=True)]  8.57 us
    ppermute x4, starting transfers between devices, both_ways(): lax.ppermute(backward, 'col_0', back)  8.49 us
    all_to_all x1, starting transfers between devices, step(): by_z.append(lax.all_to_all(last, 'col_1', 0, 0, tiled=True))  7.21 us
  transfers between devices with their start and end apart: 12, of which 5 were waited for; matrix products, arithmetic and copies ran while one was open for 1% of the time, Pallas kernels for 3%

profile of v2, /device:TPU:32, one launch (start us, length us, event | category | flops | bytes accessed | tf_op | source)
XLA Modules:
  0.0 135.3 jit_solution(14196256386619672150)
XLA Ops:
  0.6 3.4 %copy-done = bf16[1,1024,4096]{2,1,0:T(8,128)(2,1)S(1)} copy-done((bf16[1,1024,4096]{2,1,0:T(8,128)(2,1)S(1)}, bf16[1,1024,4096]{2,1,0:T(8,128)(2,1)}, u32[]{:S(2)}) %copy-start) | copy-done | bytes 8388632
  4.0 1.0 copy-done.2
  5.1 0.7 copy-done.4
  5.7 2.0 %shard_map.77 = (f32[4,96,128]{2,1,0:T(8,128)S(1)}, f32[4,160,128]{2,1,0:T(8,128)}, f32[4,96,128]{2,1,0:T(8,128)S(1)}, f32[4,160,128]{2,1,0:T(8,128)}) custom-call(s32[1,32]{1,0:T(1,128)S(1)} %bitcast.3, bf16[256,1024]{1,0:T(8,128)(2,1)S(1)} %copy-done.2, bf16[1,1024,4096]{2,1,0:T(8,128)(2,1)S(1)} %copy-done), custom_call_target="tpu_custom_call" | custom-call | tf_op jit(solution)/shard_map/pallas_call | solution.py:58
  7.7 1.5 %collective-permute-start.4 = (f32[4,96,128]{2,1,0:T(8,128)S(1)}, f32[4,96,128]{2,1,0:T(8,128)S(1)}, u32[]{:S(2)}, u32[]{:S(2)}) collective-permute-start(f32[4,96,128]{2,1,0:T(8,128)S(1)} %get-tuple-element.45), channel_id=1, source_target_pairs={{0,8},{8,16},{16,24},{24,0},{1,9},{9,17},{17,25},{25,1},{2,10},{10... | collective-permute-start | bytes 589832 | tf_op jit(solution)/shard_map/ppermute | solution.py:347
  9.2 1.7 %collective-permute-start.5 = (f32[4,96,128]{2,1,0:T(8,128)S(1)}, f32[4,96,128]{2,1,0:T(8,128)S(1)}, u32[]{:S(2)}, u32[]{:S(2)}) collective-permute-start(f32[4,96,128]{2,1,0:T(8,128)S(1)} %get-tuple-element.46), channel_id=1, source_target_pairs={{8,0},{16,8},{24,16},{0,24},{9,1},{17,9},{25,17},{1,25},{10,2},{18... | collective-permute-start | bytes 589832 | tf_op jit(solution)/shard_map/ppermute | solution.py:347
  11.0 2.4 %shard_map.78 = (f32[8,96,128]{2,1,0:T(8,128)S(1)}, f32[8,160,128]{2,1,0:T(8,128)S(1)}, f32[8,96,128]{2,1,0:T(8,128)S(1)}, f32[8,160,128]{2,1,0:T(8,128)S(1)}, f...) custom-call(s32[1,32]{1,0:T(1,128)S(1)} %bitcast.4, bf16[256,1024]{1,0:T(8,128)(2,1)S(1)} %copy-done.2, ...), custom_call_target="tpu_custom_call" | custom-call | tf_op jit(solution)/shard_map/pallas_call | solution.py:58
  13.3 2.2 %collective-permute-done.4.from_behind = f32[4,96,128]{2,1,0:T(8,128)S(1)} collective-permute-done((f32[4,96,128]{2,1,0:T(8,128)S(1)}, f32[4,96,128]{2,1,0:T(8,128)S(1)}, u32[]{:S(2)}, u32[]{:S(2)}) %collective-permute-start.4) | collective-permute-done | bytes 196640 | tf_op jit(solution)/shard_map/ppermute | solution.py:347
  15.7 1.6 %collective-permute-start.6 = (f32[8,96,128]{2,1,0:T(8,128)S(1)}, f32[8,96,128]{2,1,0:T(8,128)S(1)}, u32[]{:S(2)}, u32[]{:S(2)}) collective-permute-start(f32[8,96,128]{2,1,0:T(8,128)S(1)} %get-tuple-element.47), channel_id=1, source_target_pairs={{0,8},{8,16},{16,24},{24,0},{1,9},{9,17},{17,25},{25,1},{2,10},{10... | collective-permute-start | bytes 1179656 | tf_op jit(solution)/shard_map/ppermute | solution.py:347
  17.2 1.7 %collective-permute-start.7 = (f32[8,96,128]{2,1,0:T(8,128)S(1)}, f32[8,96,128]{2,1,0:T(8,128)S(1)}, u32[]{:S(2)}, u32[]{:S(2)}) collective-permute-start(f32[8,96,128]{2,1,0:T(8,128)S(1)} %get-tuple-element.48), channel_id=1, source_target_pairs={{8,0},{16,8},{24,16},{0,24},{9,1},{17,9},{25,17},{1,25},{10,2},{18... | collective-permute-start | bytes 1179656 | tf_op jit(solution)/shard_map/ppermute | solution.py:347
  19.0 0.3 collective-permute-start
  19.2 3.0 %collective-permute-start.1 = (f32[4,160,128]{2,1,0:T(8,128)}, f32[4,160,128]{2,1,0:T(8,128)S(1)}, u32[]{:S(2)}, u32[]{:S(2)}) collective-permute-start(f32[4,160,128]{2,1,0:T(8,128)} %get-tuple-element.39), channel_id=1, source_target_pairs={{8,0},{16,8},{24,16},{0,24},{9,1},{17,9},{25,17},{1,25},{10,2},{18... | collective-permute-start | bytes 983048 | tf_op jit(solution)/shard_map/ppermute | solution.py:347
  22.2 6.7 %collective-permute-done.6.refs_1_ = f32[8,96,128]{2,1,0:T(8,128)S(1)} collective-permute-done((f32[8,96,128]{2,1,0:T(8,128)S(1)}, f32[8,96,128]{2,1,0:T(8,128)S(1)}, u32[]{:S(2)}, u32[]{:S(2)}) %collective-permute-start.6) | collective-permute-done | bytes 393248 | tf_op jit(solution)/shard_map/ppermute | solution.py:347
  28.9 0.3 collective-permute-done.7.refs_2_
  29.2 0.8 shard_map.82
  30.0 8.6 %all-to-all-start = ((f32[8,96,128]{2,1,0:T(8,128)}), f32[8,96,128]{2,1,0:T(8,128)S(1)}, u32[]{:S(2)}, u32[]{:S(2)}) async-start(f32[8,96,128]{2,1,0:T(8,128)} %shard_map.82), calls=%async_computation | async-start | bytes 786432 | tf_op jit(solution)/shard_map/all_to_all | solution.py:357
  38.7 1.3 collective-permute-start.2
  40.0 2.0 %collective-permute-start.3 = (f32[8,160,128]{2,1,0:T(8,128)S(1)}, f32[8,160,128]{2,1,0:T(8,128)S(1)}, u32[]{:S(2)}, u32[]{:S(2)}) collective-permute-start(f32[8,160,128]{2,1,0:T(8,128)S(1)} %get-tuple-element.41), channel_id=1, source_target_pairs={{8,0},{16,8},{24,16},{0,24},{9,1},{17,9},{25,17},{1,25},{10,2},{18... | collective-permute-start | bytes 1966088 | tf_op jit(solution)/shard_map/ppermute | solution.py:347
  42.0 9.9 %collective-permute-done.2.refs_1_ = f32[8,160,128]{2,1,0:T(8,128)S(1)} collective-permute-done((f32[8,160,128]{2,1,0:T(8,128)S(1)}, f32[8,160,128]{2,1,0:T(8,128)S(1)}, u32[]{:S(2)}, u32[]{:S(2)}) %collective-permute-start.2) | collective-permute-done | bytes 655392 | tf_op jit(solution)/shard_map/ppermute | solution.py:347
  51.9 1.0 shard_map.80
  52.9 7.2 %all-to-all-start.1 = ((f32[8,160,128]{2,1,0:T(8,128)}), f32[8,160,128]{2,1,0:T(8,128)S(1)}, u32[]{:S(2)}, u32[]{:S(2)}) async-start(f32[8,160,128]{2,1,0:T(8,128)} %shard_map.80), calls=%async_computation.1 | async-start | bytes 1310720 | tf_op jit(solution)/shard_map/all_to_all | solution.py:360
  60.1 1.1 copy.8
  61.2 11.5 %all-to-all-done.1.refs_1_ = f32[8,160,128]{2,1,0:T(8,128)S(1)} async-done(((f32[8,160,128]{2,1,0:T(8,128)}), f32[8,160,128]{2,1,0:T(8,128)S(1)}, u32[]{:S(2)}, u32[]{:S(2)}) %all-to-all-start.1) | async-done | bytes 655392 | tf_op jit(solution)/shard_map/all_to_all | solution.py:360
  72.7 0.4 shard_map.83
  73.2 10.7 %all_to_all.25.received = f32[8,40,128]{2,1,0:T(8,128)S(1)} all-to-all(f32[8,40,128]{2,1,0:T(8,128)S(1)} %get-tuple-element.51), channel_id=1, replica_groups=mesh['row_0'=4,'row_1'=2,'col_0'=4,'col_1'=8] {'row_0','row_1'}, dimensions={0} | all-to-all | bytes 327680 | tf_op jit(solution)/shard_map/all_to_all | solution.py:363
  83.9 0.2 shard_map.84
  84.1 4.4 %collective-permute-start.8 = (f32[32,640]{1,0:T(8,128)S(1)}, f32[32,640]{1,0:T(8,128)S(1)}, u32[]{:S(2)}, u32[]{:S(2)}) collective-permute-start(f32[32,640]{1,0:T(8,128)S(1)} %get-tuple-element.54), channel_id=1, source_target_pairs={{1,0},{2,1},{3,2},{4,3},{5,4},{6,5},{7,6},{8,7},{9,8},{10,9},{11,1... | collective-permute-start | bytes 245768 | tf_op jit(solution)/shard_map/ppermute | solution.py:366
  88.5 1.9 %collective-permute-start.9 = (f32[32,640]{1,0:T(8,128)S(1)}, f32[32,640]{1,0:T(8,128)S(1)}, u32[]{:S(2)}, u32[]{:S(2)}) collective-permute-start(f32[32,640]{1,0:T(8,128)S(1)} %get-tuple-element.55), channel_id=1, source_target_pairs={{0,1},{1,2},{2,3},{3,4},{4,5},{5,6},{6,7},{7,8},{8,9},{9,10},{10,1... | collective-permute-start | bytes 245768 | tf_op jit(solution)/shard_map/ppermute | solution.py:367
  90.4 16.5 %all_to_all.26.sums = f32[32,1,128]{2,1,0:T(1,128)S(1)} all-to-all(f32[32,1,128]{2,1,0:T(1,128)S(1)} %get-tuple-element.53), channel_id=1, replica_groups=mesh['row_0'=4,'row_1'=2,'col_0'=4,'col_1'=8] {'col_0','col_1'}, dimensions={0} | all-to-all | bytes 32768 | tf_op jit(solution)/shard_map/all_to_all | solution.py:368
  106.9 6.9 %shard_map.85 = (f32[512,128]{1,0:T(8,128)}, f32[256,1,128]{2,1,0:T(1,128)S(1)}) custom-call(f32[32,1,128]{2,1,0:T(1,128)S(1)} %all_to_all.26.sums, f32[8,40,128]{2,1,0:T(8,128)S(1)} %all_to_all.25.received, f32[512,128]{1,0:T(8,128)S(1)} %get-tuple-element.52.step_dir, f32[512,128]{1,0:T(8,128)S(1)} %copy-done.1, ...), custom_call_target="tpu_custom_call" | custom-call | tf_op jit(solution)/shard_map/pallas_call | solution.py:312
  113.8 18.8 %all_to_all.27 = f32[256,1,128]{2,1,0:T(1,128)S(1)} all-to-all(f32[256,1,128]{2,1,0:T(1,128)S(1)} %get-tuple-element.57), channel_id=1, replica_groups=mesh['row_0'=4,'row_1'=2,'col_0'=4,'col_1'=8] {'row_0','row_1','col_0','..., dimensions={0} | all-to-all | bytes 262144 | tf_op jit(solution)/shard_map/all_to_all | solution.py:372
  132.6 0.9 reduce_sum.9
  (16 shorter events, 0.2 us)
Async XLA Ops:
  0.6 3.4 %copy-start = (bf16[1,1024,4096]{2,1,0:T(8,128)(2,1)S(1)}, bf16[1,1024,4096]{2,1,0:T(8,128)(2,1)}, u32[]{:S(2)}) copy-start(bf16[1,1024,4096]{2,1,0:T(8,128)(2,1)} %weights.3) | copy-start | bytes 25165828
  4.0 1.0 copy-start.2
  5.1 0.7 copy-start.4
  7.7 65.0 %copy-start.1 = (f32[512,128]{1,0:T(8,128)S(1)}, f32[512,128]{1,0:T(8,128)}, u32[]{:S(2)}) copy-start(f32[512,128]{1,0:T(8,128)} %image.3) | copy-start | bytes 786436
  7.7 65.0 %copy-start.3 = (f32[512,128]{1,0:T(8,128)S(1)}, f32[512,128]{1,0:T(8,128)}, u32[]{:S(2)}) copy-start(f32[512,128]{1,0:T(8,128)} %refs_3_.1) | copy-start | bytes 786436
  7.7 7.9 %collective-permute-start.4 = (f32[4,96,128]{2,1,0:T(8,128)S(1)}, f32[4,96,128]{2,1,0:T(8,128)S(1)}, u32[]{:S(2)}, u32[]{:S(2)}) collective-permute-start(f32[4,96,128]{2,1,0:T(8,128)S(1)} %get-tuple-element.45), channel_id=1, source_target_pairs={{0,8},{8,16},{16,24},{24,0},{1,9},{9,17},{17,25},{25,1},{2,10},{10... | collective-permute-start | bytes 589832 | tf_op jit(solution)/shard_map/ppermute | solution.py:347
  9.2 6.4 %collective-permute-start.5 = (f32[4,96,128]{2,1,0:T(8,128)S(1)}, f32[4,96,128]{2,1,0:T(8,128)S(1)}, u32[]{:S(2)}, u32[]{:S(2)}) collective-permute-start(f32[4,96,128]{2,1,0:T(8,128)S(1)} %get-tuple-element.46), channel_id=1, source_target_pairs={{8,0},{16,8},{24,16},{0,24},{9,1},{17,9},{25,17},{1,25},{10,2},{18... | collective-permute-start | bytes 589832 | tf_op jit(solution)/shard_map/ppermute | solution.py:347
  15.7 13.3 %collective-permute-start.6 = (f32[8,96,128]{2,1,0:T(8,128)S(1)}, f32[8,96,128]{2,1,0:T(8,128)S(1)}, u32[]{:S(2)}, u32[]{:S(2)}) collective-permute-start(f32[8,96,128]{2,1,0:T(8,128)S(1)} %get-tuple-element.47), channel_id=1, source_target_pairs={{0,8},{8,16},{16,24},{24,0},{1,9},{9,17},{17,25},{25,1},{2,10},{10... | collective-permute-start | bytes 1179656 | tf_op jit(solution)/shard_map/ppermute | solution.py:347
  17.2 12.0 %collective-permute-start.7 = (f32[8,96,128]{2,1,0:T(8,128)S(1)}, f32[8,96,128]{2,1,0:T(8,128)S(1)}, u32[]{:S(2)}, u32[]{:S(2)}) collective-permute-start(f32[8,96,128]{2,1,0:T(8,128)S(1)} %get-tuple-element.48), channel_id=1, source_target_pairs={{8,0},{16,8},{24,16},{0,24},{9,1},{17,9},{25,17},{1,25},{10,2},{18... | collective-permute-start | bytes 1179656 | tf_op jit(solution)/shard_map/ppermute | solution.py:347
  19.0 19.6 %collective-permute-start = (f32[4,160,128]{2,1,0:T(8,128)}, f32[4,160,128]{2,1,0:T(8,128)S(1)}, u32[]{:S(2)}, u32[]{:S(2)}) collective-permute-start(f32[4,160,128]{2,1,0:T(8,128)} %get-tuple-element.38), channel_id=1, source_target_pairs={{0,8},{8,16},{16,24},{24,0},{1,9},{9,17},{17,25},{25,1},{2,10},{10... | collective-permute-start | bytes 983048 | tf_op jit(solution)/shard_map/ppermute | solution.py:347
  19.2 19.3 %collective-permute-start.1 = (f32[4,160,128]{2,1,0:T(8,128)}, f32[4,160,128]{2,1,0:T(8,128)S(1)}, u32[]{:S(2)}, u32[]{:S(2)}) collective-permute-start(f32[4,160,128]{2,1,0:T(8,128)} %get-tuple-element.39), channel_id=1, source_target_pairs={{8,0},{16,8},{24,16},{0,24},{9,1},{17,9},{25,17},{1,25},{10,2},{18... | collective-permute-start | bytes 983048 | tf_op jit(solution)/shard_map/ppermute | solution.py:347
  30.0 22.9 %all-to-all-start = ((f32[8,96,128]{2,1,0:T(8,128)}), f32[8,96,128]{2,1,0:T(8,128)S(1)}, u32[]{:S(2)}, u32[]{:S(2)}) async-start(f32[8,96,128]{2,1,0:T(8,128)} %shard_map.82), calls=%async_computation | async-start | bytes 786432 | tf_op jit(solution)/shard_map/all_to_all | solution.py:357
  38.7 13.2 %collective-permute-start.2 = (f32[8,160,128]{2,1,0:T(8,128)S(1)}, f32[8,160,128]{2,1,0:T(8,128)S(1)}, u32[]{:S(2)}, u32[]{:S(2)}) collective-permute-start(f32[8,160,128]{2,1,0:T(8,128)S(1)} %get-tuple-element.40), channel_id=1, source_target_pairs={{0,8},{8,16},{16,24},{24,0},{1,9},{9,17},{17,25},{25,1},{2,10},{10... | collective-permute-start | bytes 1966088 | tf_op jit(solution)/shard_map/ppermute | solution.py:347
  40.0 12.0 %collective-permute-start.3 = (f32[8,160,128]{2,1,0:T(8,128)S(1)}, f32[8,160,128]{2,1,0:T(8,128)S(1)}, u32[]{:S(2)}, u32[]{:S(2)}) collective-permute-start(f32[8,160,128]{2,1,0:T(8,128)S(1)} %get-tuple-element.41), channel_id=1, source_target_pairs={{8,0},{16,8},{24,16},{0,24},{9,1},{17,9},{25,17},{1,25},{10,2},{18... | collective-permute-start | bytes 1966088 | tf_op jit(solution)/shard_map/ppermute | solution.py:347
  52.9 19.8 %all-to-all-start.1 = ((f32[8,160,128]{2,1,0:T(8,128)}), f32[8,160,128]{2,1,0:T(8,128)S(1)}, u32[]{:S(2)}, u32[]{:S(2)}) async-start(f32[8,160,128]{2,1,0:T(8,128)} %shard_map.80), calls=%async_computation.1 | async-start | bytes 1310720 | tf_op jit(solution)/shard_map/all_to_all | solution.py:360
  84.1 22.8 %collective-permute-start.8 = (f32[32,640]{1,0:T(8,128)S(1)}, f32[32,640]{1,0:T(8,128)S(1)}, u32[]{:S(2)}, u32[]{:S(2)}) collective-permute-start(f32[32,640]{1,0:T(8,128)S(1)} %get-tuple-element.54), channel_id=1, source_target_pairs={{1,0},{2,1},{3,2},{4,3},{5,4},{6,5},{7,6},{8,7},{9,8},{10,9},{11,1... | collective-permute-start | bytes 245768 | tf_op jit(solution)/shard_map/ppermute | solution.py:366
  88.5 18.4 %collective-permute-start.9 = (f32[32,640]{1,0:T(8,128)S(1)}, f32[32,640]{1,0:T(8,128)S(1)}, u32[]{:S(2)}, u32[]{:S(2)}) collective-permute-start(f32[32,640]{1,0:T(8,128)S(1)} %get-tuple-element.55), channel_id=1, source_target_pairs={{0,1},{1,2},{2,3},{3,4},{4,5},{5,6},{6,7},{7,8},{8,9},{9,10},{10,1... | collective-permute-start | bytes 245768 | tf_op jit(solution)/shard_map/ppermute | solution.py:367

commit v3 on v2

--- a/solution.py
+++ b/solution.py
@@ -20,7 +20,7 @@
 epsilon = 1e-06
 
 HALO = 16
-FIRST = 96
+X_FIRST = 128
 LANES = 128
 BASE = 8
 
@@ -37,75 +37,107 @@
     return pltpu.CompilerParams(vmem_limit_bytes=mebibytes * 1024 * 1024)
 
 
-def back_project_kernel(marks, residual, weights, *outs, plan, splits, width, n_x, n_z):
-    own = lax.axis_index("col_0")
-    for o, (step, low, high) in enumerate(plan):
-        x = lax.rem(own + step, n_x)
-        for z in range(low, high, width):
+def turned(axis, steps):
+    return lax.rem(lax.axis_index(axis) + steps, lax.axis_size(axis))
+
+
+def marked_products(marks, residual, weights, angles, tile, width):
+    columns = pl.ds(pl.multiple_of(tile * LANES, width * LANES), width * LANES)
+    product = jnp.dot(
+        residual[slice(*angles)], weights[0, :, columns], preferred_element_type=jnp.float32
+    )
+    for t in range(width):
+        yield t, product[:, t * LANES:(t + 1) * LANES] * marks[0, tile + t].astype(jnp.float32)
+
+
+def far_products_kernel(marks, residual, weights, x_up, x_down, z_up, z_down, *, n_x, n_z):
+    split = x_up.shape[1]
+    x, z = turned("col_0", n_x // 2), turned("col_1", n_z // 2)
+    width = n_z // 2
+    for half, out in enumerate((x_up, x_down)):
+        tile = x * n_z + half * width
+        for t, value in marked_products(marks, residual, weights, (0, split), tile, width):
+            out[t] = value
+    for half, out in enumerate((z_up, z_down)):
+        for k in range(n_x // 2):
+            tile = (half * (n_x // 2) + k) * n_z + z
+            for _, value in marked_products(marks, residual, weights, (split, None), tile, 1):
+                out[k] = value
+
+
+def near_products_kernel(marks, residual, weights, by_x, by_z, *, n_x, n_z):
+    split = by_x.shape[2]
+    width = n_z // 2
+    for step in range(n_x):
+        if step == n_x // 2:
+            continue
+        for z in range(0, n_z, width):
+            tile = turned("col_0", step) * n_z + z
+            for t, value in marked_products(marks, residual, weights, (0, split), tile, width):
+                by_x[step, z + t] = value
+    for x in range(n_x):
+        for z in range(0, n_z, width):
             tile = x * n_z + z
-            columns = pl.ds(pl.multiple_of(tile * LANES, width * LANES), width * LANES)
-            product = jnp.dot(
-                residual[...], weights[0, :, columns], preferred_element_type=jnp.float32
-            )
-            for t in range(width):
-                mark = marks[0, tile + t].astype(jnp.float32)
-                marked = product[:, t * LANES:(t + 1) * LANES] * mark
-                for s, (first, last) in enumerate(splits):
-                    outs[o * len(splits) + s][z - low + t] = marked[first:last]
-
-
-def back_project(residual, weights, marks, plan, splits, n_x, n_z):
-    outs = pl.pallas_call(
-        functools.partial(
-            back_project_kernel, plan=plan, splits=splits, width=4, n_x=n_x, n_z=n_z
-        ),
+            for t, value in marked_products(marks, residual, weights, (split, None), tile, width):
+                steps = lax.rem(z + t + n_z - lax.axis_index("col_1"), n_z)
+                by_z[steps, x] = value
+
+
+def back_project(kernel, residual, weights, marks, shapes, n_x, n_z):
+    return pl.pallas_call(
+        functools.partial(kernel, n_x=n_x, n_z=n_z),
         in_specs=[smem(), vmem(), vmem()],
-        out_specs=[vmem()] * (len(plan) * len(splits)),
-        out_shape=[
-            jax.ShapeDtypeStruct((high - low, last - first, LANES), jnp.float32)
-            for _, low, high in plan for first, last in splits
-        ],
+        out_specs=[vmem()] * len(shapes),
+        out_shape=[jax.ShapeDtypeStruct(shape + (LANES,), jnp.float32) for shape in shapes],
         compiler_params=params(32),
     )(marks, residual, weights)
-    return [outs[i:i + len(splits)] for i in range(0, len(outs), len(splits))]
-
-
-def relay_kernel(ahead, behind, from_behind, from_ahead, to_ahead, to_behind):
-    half = ahead.shape[0] // 2
-    for k in range(half):
-        to_ahead[k] = ahead[k] + from_behind[k]
-        to_ahead[half + k] = ahead[half + k]
-        to_behind[k] = behind[k]
-        to_behind[half + k] = behind[half + k] + from_ahead[k]
-
-
-def relay(ahead, behind, from_behind, from_ahead):
-    shape = jax.ShapeDtypeStruct(ahead.shape, jnp.float32)
-    return pl.pallas_call(
-        relay_kernel,
-        in_specs=[vmem()] * 4,
+
+
+def relay_kernel(chunks, from_behind, from_ahead, to_ahead, to_behind, *, step):
+    ahead, behind = chunks.at[step], chunks.at[chunks.shape[0] - step]
+    count = to_ahead.shape[0]
+    brought = from_behind.shape[0]
+    for k in range(count):
+        value = ahead[k]
+        to_ahead[k] = value + from_behind[k] if k < brought else value
+        value = behind[k]
+        here = k - (count - brought)
+        to_behind[k] = value + from_ahead[here] if here >= 0 else value
+
+
+def relay(chunks, from_behind, from_ahead, step):
+    shape = jax.ShapeDtypeStruct(chunks.shape[1:], jnp.float32)
+    return pl.pallas_call(
+        functools.partial(relay_kernel, step=step),
+        in_specs=[vmem()] * 3,
         out_specs=[vmem()] * 2,
         out_shape=[shape, shape],
         compiler_params=params(8),
-    )(ahead, behind, from_behind, from_ahead)
-
-
-def add_up_kernel(*refs):
-    *parts, out = refs
-    total = parts[0][...]
-    for part in parts[1:]:
-        total = total + part[...]
-    out[...] = total
-
-
-def add_up(*parts):
-    return pl.pallas_call(
-        add_up_kernel,
-        in_specs=[vmem()] * len(parts),
-        out_specs=vmem(),
-        out_shape=jax.ShapeDtypeStruct(parts[0].shape, jnp.float32),
+    )(chunks, from_behind, from_ahead)
+
+
+def collect_kernel(chunks, from_behind, from_ahead, up, down, out, *, axis):
+    n = chunks.shape[1]
+    half = up.shape[1]
+    for step in range(n):
+        k = turned(axis, step)
+        total = chunks[0, k] + from_behind[k] + from_ahead[k]
+        if step == n // 2:
+            up[0], down[0] = total[:half], total[half:]
+        else:
+            out[step, 0], out[step, 1] = total[:half], total[half:]
+
+
+def collect(chunks, from_behind, from_ahead, axis):
+    _, n, angles, _ = chunks.shape
+    half = jax.ShapeDtypeStruct((1, angles // 2, LANES), jnp.float32)
+    return pl.pallas_call(
+        functools.partial(collect_kernel, axis=axis),
+        in_specs=[vmem()] * 3,
+        out_specs=[vmem()] * 3,
+        out_shape=[half, half, jax.ShapeDtypeStruct((n, 2, angles // 2, LANES), jnp.float32)],
         compiler_params=params(8),
-    )(*parts)
+    )(chunks, from_behind, from_ahead)
 
 
 def exact_parts(value):
@@ -119,11 +151,10 @@
 def gradient_kernel(*refs, n_row):
     *groups, strip, precond, image, step_dir, slots = refs
     sums = []
-    for parts in groups:
-        total = parts[0]
-        for k in range(1, parts.shape[0]):
-            total = total + parts[k]
-        sums.append(total)
+    for k in range(0, len(groups), 3):
+        chunks, from_behind, from_ahead = groups[k:k + 3]
+        for half in range(2):
+            sums.append(chunks[0, half] + from_behind[half] + from_ahead[half])
     summed = jnp.concatenate(sums, axis=0)
     gradient = None
     for piece in reversed(exact_parts(summed)):
@@ -333,39 +364,69 @@
     n_x = lax.axis_size("col_0")
     n_z = lax.axis_size("col_1")
     angles = residual.shape[0]
-    splits = ((0, FIRST), (FIRST, angles))
-    half = n_z // 2
     marks = touched[0]
+    others = angles - X_FIRST
     far = back_project(
-        residual, bin_weights, marks, ((2, 0, half), (2, half, n_z)), splits, n_x, n_z
+        far_products_kernel, residual, bin_weights, marks,
+        ((n_z // 2, X_FIRST), (n_z // 2, X_FIRST), (n_x // 2, others), (n_x // 2, others)),
+        n_x, n_z,
     )
     far, residual = lax.optimization_barrier((far, residual))
-    ring = [(i, (i + 1) % n_x) for i in range(n_x)]
-    back = [(j, i) for i, j in ring]
-
-    def both_ways(forward, backward):
-        return lax.ppermute(forward, "col_0", ring), lax.ppermute(backward, "col_0", back)
-
-    relayed = [both_ways(far[0][c], far[1][c]) for c in range(2)]
-    ahead, behind, own = back_project(
-        residual, bin_weights, marks,
-        ((1, 0, n_z), (n_x - 1, 0, n_z), (0, 0, n_z)), splits, n_x, n_z,
-    )
-    outgoing = [relay(ahead[c], behind[c], *relayed[c]) for c in range(2)]
-    incoming = [both_ways(*outgoing[c]) for c in range(2)]
-    first = add_up(own[0], *incoming[0])
-    by_z = [lax.all_to_all(first, "col_1", 0, 0, tiled=True)]
-    last = add_up(own[1], *incoming[1])
-    last, by_z[0] = lax.optimization_barrier((last, by_z[0]))
-    by_z.append(lax.all_to_all(last, "col_1", 0, 0, tiled=True))
+    flight = {}
+
+    def send(name, pair):
+        axis = "col_0" if name.endswith("x") else "col_1"
+        n = lax.axis_size(axis)
+        ring = [(i, (i + 1) % n) for i in range(n)]
+        flight[name] = (
+            lax.ppermute(pair[0], axis, ring),
+            lax.ppermute(pair[1], axis, [(j, i) for i, j in ring]),
+        )
+
+    send("first_x", far[:2])
+    send("first_z", far[2:])
+    x_chunks, z_chunks = back_project(
+        near_products_kernel, residual, bin_weights, marks,
+        ((n_x, n_z, X_FIRST), (n_z, n_x, others)), n_x, n_z,
+    )
+    chunks = {"first_x": x_chunks, "first_z": z_chunks}
+    waiting = []
+
+    def flush(here):
+        if waiting:
+            name, pair = waiting.pop()
+            pair, here = lax.optimization_barrier((pair, here))
+            send(name, pair)
+        return here
+
+    def onward(name, step):
+        here = flush(chunks[name])
+        waiting.append((name, relay(here, *flight[name], step)))
+
+    def turn(name, then, axis):
+        here = flush(chunks[name])
+        up, down, chunks[then] = collect(here, *flight[name], axis)
+        waiting.append((then, (up, down)))
+
+    onward("first_z", 3)
+    onward("first_x", 1)
+    onward("first_z", 2)
+    onward("first_z", 1)
+    turn("first_x", "then_z", "col_1")
+    turn("first_z", "then_x", "col_0")
+    onward("then_z", 3)
+    onward("then_x", 1)
+    onward("then_z", 2)
+    onward("then_z", 1)
+    groups = [flush(chunks["then_z"]), *flight["then_z"], chunks["then_x"], *flight["then_x"]]
     strip = strip_weights.T
-    step_dir, row_slots = make_gradient(by_z, strip, precond, image, n_row)
+    step_dir, row_slots = make_gradient(groups, strip, precond, image, n_row)
     received = lax.all_to_all(row_slots, ROW, 0, 0, tiled=True)
     leftward, rightward, sum_slots = make_edges(received, step_dir, image, n_row, n_col)
     later, earlier = neighbours(n_col)
+    sums = lax.all_to_all(sum_slots, COL, 0, 0, tiled=True)
     from_right = lax.ppermute(leftward, COL, earlier)
     from_left = lax.ppermute(rightward, COL, later)
-    sums = lax.all_to_all(sum_slots, COL, 0, 0, tiled=True)
     updated, change_slots = denoise(
         sums, received, step_dir, image, from_right, from_left, n_row, n_col
     )

time: 138 us -> 131 us (0.949)
  waiting for transfers between devices: 30.7 us -> 21.5 us
  starting transfers between devices: 35.2 us -> 38.7 us
  Pallas kernels: 13.9 us -> 12.1 us
  blocking collectives: 46 us -> 47.7 us
    ppermute x8 -> x24, starting transfers between devices: 13.1 us -> 32.9 us  [the longest x12 19.3 us: send(): lax.ppermute(pair[0], axis, ring)]
    all_to_all x2 -> x0, starting transfers between devices: 15.8 us -> none  [the longest x1 8.57 us: step(): by_z = [lax.all_to_all(first, 'col_1', 0, 0, tiled=True)]]
    all_to_all x2 -> x0, waiting for transfers between devices: 11.5 us -> none  [the longest x1 11.5 us: step(): by_z.append(lax.all_to_all(last, 'col_1', 0, 0, tiled=True))]
    ppermute x8 -> x24, waiting for transfers between devices: 19.2 us -> 21.5 us  [the longest x12 12 us: send(): lax.ppermute(pair[0], axis, ring)]
    all_to_all x1, blocking collectives: 16.5 us -> 18.2 us  [step(): sums = lax.all_to_all(sum_slots, COL, 0, 0, tiled=True)]
    pallas_call x6 -> x12, Pallas kernels: 6.32 us -> 4.59 us  [the longest x2 4.16 us: back_project(): pl.pallas_call(functools.partial(kernel, n_x=n_x, n_z=n_z), in_specs=[sme...]
    ppermute x1, starting transfers between devices: 4.39 us -> 2.67 us  [step(): from_right = lax.ppermute(leftward, COL, earlier)]
    unnamed x11 -> x13, local copies, waits for them, and re-layouts: 6.16 us -> 5.22 us
  transfers between devices with their start and end apart: 12 -> 26, of which waited for: 5 -> 11; matrix products, arithmetic and copies ran while one was open for 1% -> 0% of each run, Pallas kernels for 3% -> 2%
where the time goes in v3:
time: 131 us; the launch traced here: 129 us
  blocking collectives  47.7 us (36%)
  starting transfers between devices  38.7 us (30%)
  waiting for transfers between devices  21.5 us (16%)
  Pallas kernels  12.1 us (9%)
  local copies, waits for them, and re-layouts  5.22 us (4%)
  between operations  2.63 us (2%)
    ppermute x12, starting transfers between devices, send(): lax.ppermute(pair[0], axis, ring)  19.3 us
    all_to_all x1, blocking collectives, step(): changes = lax.all_to_all(change_slots, ROW_COL, 0, 0, tiled=True)  18.8 us
    all_to_all x1, blocking collectives, step(): sums = lax.all_to_all(sum_slots, COL, 0, 0, tiled=True)  18.2 us
    ppermute x12, starting transfers between devices, send(): lax.ppermute(pair[1], axis, [(j, i) for i, j in ring])  13.6 us
    ppermute x12, waiting for transfers between devices, send(): lax.ppermute(pair[0], axis, ring)  12 us
    all_to_all x1, blocking collectives, step(): received = lax.all_to_all(row_slots, ROW, 0, 0, tiled=True)  10.7 us
    ppermute x12, waiting for transfers between devices, send(): lax.ppermute(pair[1], axis, [(j, i) for i, j in ring])  9.48 us
    pallas_call x1, Pallas kernels, denoise(): pl.pallas_call(functools.partial(denoise_kernel, n_row=n_row, n_col=n_col...  6.92 us
  transfers between devices with their start and end apart: 26, of which 11 were waited for; matrix products, arithmetic and copies ran while one was open for 0% of the time, Pallas kernels for 2%

profile of v3, /device:TPU:32, one launch (start us, length us, event | category | flops | bytes accessed | tf_op | source)
XLA Modules:
  0.0 128.8 jit_solution(12326607456884829280)
XLA Ops:
  0.6 3.4 %copy-done = bf16[1,1024,4096]{2,1,0:T(8,128)(2,1)S(1)} copy-done((bf16[1,1024,4096]{2,1,0:T(8,128)(2,1)S(1)}, bf16[1,1024,4096]{2,1,0:T(8,128)(2,1)}, u32[]{:S(2)}) %copy-start) | copy-done | bytes 8388632
  4.0 1.0 copy-done.2
  5.7 1.3 %shard_map.77 = (f32[4,128,128]{2,1,0:T(8,128)S(1)}, f32[4,128,128]{2,1,0:T(8,128)S(1)}, f32[2,128,128]{2,1,0:T(8,128)S(1)}, f32[2,128,128]{2,1,0:T(8,128)S(1)}) custom-call(s32[1,32]{1,0:T(1,128)S(1)} %bitcast.3, bf16[256,1024]{1,0:T(8,128)(2,1)S(1)} %copy-done.2, bf16[1,1024,4096]{2,1,0:T(8,128)(2,1)S(1)} %copy-done), custom_call_target="tpu_custom_call" | custom-call | tf_op jit(solution)/shard_map/pallas_call | solution.py:87
  7.1 2.0 %collective-permute-start = (f32[2,128,128]{2,1,0:T(8,128)S(1)}, f32[2,128,128]{2,1,0:T(8,128)S(1)}, u32[]{:S(2)}, u32[]{:S(2)}) collective-permute-start(f32[2,128,128]{2,1,0:T(8,128)S(1)} %get-tuple-element.78), channel_id=1, source_target_pairs={{0,1},{1,2},{2,3},{3,4},{4,5},{5,6},{6,7},{7,0},{8,9},{9,10},{10,1... | collective-permute-start | bytes 393224 | tf_op jit(solution)/shard_map/ppermute | solution.py:382
  9.2 1.5 %collective-permute-start.2 = (f32[4,128,128]{2,1,0:T(8,128)S(1)}, f32[4,128,128]{2,1,0:T(8,128)S(1)}, u32[]{:S(2)}, u32[]{:S(2)}) collective-permute-start(f32[4,128,128]{2,1,0:T(8,128)S(1)} %get-tuple-element.84), channel_id=1, source_target_pairs={{0,8},{8,16},{16,24},{24,0},{1,9},{9,17},{17,25},{25,1},{2,10},{10... | collective-permute-start | bytes 786440 | tf_op jit(solution)/shard_map/ppermute | solution.py:382
  10.7 1.7 %collective-permute-start.3 = (f32[4,128,128]{2,1,0:T(8,128)S(1)}, f32[4,128,128]{2,1,0:T(8,128)S(1)}, u32[]{:S(2)}, u32[]{:S(2)}) collective-permute-start(f32[4,128,128]{2,1,0:T(8,128)S(1)} %get-tuple-element.85), channel_id=1, source_target_pairs={{8,0},{16,8},{24,16},{0,24},{9,1},{17,9},{25,17},{1,25},{10,2},{18... | collective-permute-start | bytes 786440 | tf_op jit(solution)/shard_map/ppermute | solution.py:383
  12.4 2.8 %shard_map.78 = (f32[4,8,128,128]{3,2,1,0:T(8,128)S(1)}, f32[8,4,128,128]{3,2,1,0:T(8,128)S(1)}) custom-call(s32[1,32]{1,0:T(1,128)S(1)} %bitcast.4, bf16[256,1024]{1,0:T(8,128)(2,1)S(1)} %copy-done.2, bf16[1,1024,4096]{2,1,0:T(8,128)(2,1)S(1)} %copy-done), custom_call_target="tpu_custom_call" | custom-call | tf_op jit(solution)/shard_map/pallas_call | solution.py:87
  15.3 2.1 %collective-permute-start.4 = (f32[4,128,128]{2,1,0:T(8,128)S(1)}, f32[4,128,128]{2,1,0:T(8,128)S(1)}, u32[]{:S(2)}, u32[]{:S(2)}) collective-permute-start(f32[4,128,128]{2,1,0:T(8,128)S(1)} %get-tuple-element.89), channel_id=1, source_target_pairs={{0,1},{1,2},{2,3},{3,4},{4,5},{5,6},{6,7},{7,0},{8,9},{9,10},{10,1... | collective-permute-start | bytes 786440 | tf_op jit(solution)/shard_map/ppermute | solution.py:382
  17.4 2.1 %collective-permute-start.5 = (f32[4,128,128]{2,1,0:T(8,128)S(1)}, f32[4,128,128]{2,1,0:T(8,128)S(1)}, u32[]{:S(2)}, u32[]{:S(2)}) collective-permute-start(f32[4,128,128]{2,1,0:T(8,128)S(1)} %get-tuple-element.90), channel_id=1, source_target_pairs={{1,0},{2,1},{3,2},{4,3},{5,4},{6,5},{7,6},{0,7},{9,8},{10,9},{11,1... | collective-permute-start | bytes 786440 | tf_op jit(solution)/shard_map/ppermute | solution.py:383
  20.0 3.0 %collective-permute-start.9 = (f32[8,128,128]{2,1,0:T(8,128)S(1)}, f32[8,128,128]{2,1,0:T(8,128)S(1)}, u32[]{:S(2)}, u32[]{:S(2)}) collective-permute-start(f32[8,128,128]{2,1,0:T(8,128)S(1)} %get-tuple-element.100), channel_id=1, source_target_pairs={{8,0},{16,8},{24,16},{0,24},{9,1},{17,9},{25,17},{1,25},{10,2},{18... | collective-permute-start | bytes 1572872 | tf_op jit(solution)/shard_map/ppermute | solution.py:383
  22.9 2.0 %collective-permute-done.4.from_behind = f32[4,128,128]{2,1,0:T(8,128)S(1)} collective-permute-done((f32[4,128,128]{2,1,0:T(8,128)S(1)}, f32[4,128,128]{2,1,0:T(8,128)S(1)}, u32[]{:S(2)}, u32[]{:S(2)}) %collective-permute-start.4) | collective-permute-done | bytes 262176 | tf_op jit(solution)/shard_map/ppermute | solution.py:382
  25.5 3.0 %collective-permute-start.6 = (f32[4,128,128]{2,1,0:T(8,128)S(1)}, f32[4,128,128]{2,1,0:T(8,128)S(1)}, u32[]{:S(2)}, u32[]{:S(2)}) collective-permute-start(f32[4,128,128]{2,1,0:T(8,128)S(1)} %get-tuple-element.94), channel_id=1, source_target_pairs={{0,1},{1,2},{2,3},{3,4},{4,5},{5,6},{6,7},{7,0},{8,9},{9,10},{10,1... | collective-permute-start | bytes 786440 | tf_op jit(solution)/shard_map/ppermute | solution.py:382
  28.6 4.0 %collective-permute-done.6.from_behind = f32[4,128,128]{2,1,0:T(8,128)S(1)} collective-permute-done((f32[4,128,128]{2,1,0:T(8,128)S(1)}, f32[4,128,128]{2,1,0:T(8,128)S(1)}, u32[]{:S(2)}, u32[]{:S(2)}) %collective-permute-start.6) | collective-permute-done | bytes 262176 | tf_op jit(solution)/shard_map/ppermute | solution.py:382
  32.6 3.3 %collective-permute-done.7.from_ahead = f32[4,128,128]{2,1,0:T(8,128)S(1)} collective-permute-done((f32[4,128,128]{2,1,0:T(8,128)S(1)}, f32[4,128,128]{2,1,0:T(8,128)S(1)}, u32[]{:S(2)}, u32[]{:S(2)}) %collective-permute-start.7) | collective-permute-done | bytes 262176 | tf_op jit(solution)/shard_map/ppermute | solution.py:383
  35.9 2.1 %collective-permute-start.10 = (f32[4,128,128]{2,1,0:T(8,128)S(1)}, f32[4,128,128]{2,1,0:T(8,128)S(1)}, u32[]{:S(2)}, u32[]{:S(2)}) collective-permute-start(f32[4,128,128]{2,1,0:T(8,128)S(1)} %get-tuple-element.104), channel_id=1, source_target_pairs={{0,1},{1,2},{2,3},{3,4},{4,5},{5,6},{6,7},{7,0},{8,9},{9,10},{10,1... | collective-permute-start | bytes 786440 | tf_op jit(solution)/shard_map/ppermute | solution.py:382
  38.2 2.1 %collective-permute-start.12 = (f32[1,64,128]{2,1,0:T(8,128)S(1)}, f32[1,64,128]{2,1,0:T(8,128)S(1)}, u32[]{:S(2)}, u32[]{:S(2)}) collective-permute-start(f32[1,64,128]{2,1,0:T(8,128)S(1)} %get-tuple-element.110), channel_id=1, source_target_pairs={{0,1},{1,2},{2,3},{3,4},{4,5},{5,6},{6,7},{7,0},{8,9},{9,10},{10,1... | collective-permute-start | bytes 98312 | tf_op jit(solution)/shard_map/ppermute | solution.py:382
  40.3 2.1 %collective-permute-done.10.from_behind = f32[4,128,128]{2,1,0:T(8,128)S(1)} collective-permute-done((f32[4,128,128]{2,1,0:T(8,128)S(1)}, f32[4,128,128]{2,1,0:T(8,128)S(1)}, u32[]{:S(2)}, u32[]{:S(2)}) %collective-permute-start.10) | collective-permute-done | bytes 262176 | tf_op jit(solution)/shard_map/ppermute | solution.py:382
  42.4 2.2 %collective-permute-done.11.from_ahead = f32[4,128,128]{2,1,0:T(8,128)S(1)} collective-permute-done((f32[4,128,128]{2,1,0:T(8,128)S(1)}, f32[4,128,128]{2,1,0:T(8,128)S(1)}, u32[]{:S(2)}, u32[]{:S(2)}) %collective-permute-start.11) | collective-permute-done | bytes 262176 | tf_op jit(solution)/shard_map/ppermute | solution.py:383
  45.3 1.5 %collective-permute-start.16 = (f32[2,64,128]{2,1,0:T(8,128)S(1)}, f32[2,64,128]{2,1,0:T(8,128)S(1)}, u32[]{:S(2)}, u32[]{:S(2)}) collective-permute-start(f32[2,64,128]{2,1,0:T(8,128)S(1)} %get-tuple-element.121), channel_id=1, source_target_pairs={{0,1},{1,2},{2,3},{3,4},{4,5},{5,6},{6,7},{7,0},{8,9},{9,10},{10,1... | collective-permute-start | bytes 196616 | tf_op jit(solution)/shard_map/ppermute | solution.py:382
  47.9 2.8 %collective-permute-start.15 = (f32[1,64,128]{2,1,0:T(8,128)S(1)}, f32[1,64,128]{2,1,0:T(8,128)S(1)}, u32[]{:S(2)}, u32[]{:S(2)}) collective-permute-start(f32[1,64,128]{2,1,0:T(8,128)S(1)} %get-tuple-element.117), channel_id=1, source_target_pairs={{8,0},{16,8},{24,16},{0,24},{9,1},{17,9},{25,17},{1,25},{10,2},{18... | collective-permute-start | bytes 98312 | tf_op jit(solution)/shard_map/ppermute | solution.py:383
  50.6 1.9 %collective-permute-done.14.from_behind = f32[1,64,128]{2,1,0:T(8,128)S(1)} collective-permute-done((f32[1,64,128]{2,1,0:T(8,128)S(1)}, f32[1,64,128]{2,1,0:T(8,128)S(1)}, u32[]{:S(2)}, u32[]{:S(2)}) %collective-permute-start.14) | collective-permute-done | bytes 32800 | tf_op jit(solution)/shard_map/ppermute | solution.py:382
  52.6 1.5 %collective-permute-start.18 = (f32[2,64,128]{2,1,0:T(8,128)S(1)}, f32[2,64,128]{2,1,0:T(8,128)S(1)}, u32[]{:S(2)}, u32[]{:S(2)}) collective-permute-start(f32[2,64,128]{2,1,0:T(8,128)S(1)} %get-tuple-element.126), channel_id=1, source_target_pairs={{0,1},{1,2},{2,3},{3,4},{4,5},{5,6},{6,7},{7,0},{8,9},{9,10},{10,1... | collective-permute-start | bytes 196616 | tf_op jit(solution)/shard_map/ppermute | solution.py:382
  55.4 2.5 %collective-permute-start.23 = (f32[2,64,128]{2,1,0:T(8,128)S(1)}, f32[2,64,128]{2,1,0:T(8,128)S(1)}, u32[]{:S(2)}, u32[]{:S(2)}) collective-permute-start(f32[2,64,128]{2,1,0:T(8,128)S(1)} %get-tuple-element.134), channel_id=1, source_target_pairs={{8,0},{16,8},{24,16},{0,24},{9,1},{17,9},{25,17},{1,25},{10,2},{18... | collective-permute-start | bytes 196616 | tf_op jit(solution)/shard_map/ppermute | solution.py:383
  58.4 1.8 %collective-permute-start.20 = (f32[2,64,128]{2,1,0:T(8,128)S(1)}, f32[2,64,128]{2,1,0:T(8,128)S(1)}, u32[]{:S(2)}, u32[]{:S(2)}) collective-permute-start(f32[2,64,128]{2,1,0:T(8,128)S(1)} %get-tuple-element.131), channel_id=1, source_target_pairs={{0,1},{1,2},{2,3},{3,4},{4,5},{5,6},{6,7},{7,0},{8,9},{9,10},{10,1... | collective-permute-start | bytes 196616 | tf_op jit(solution)/shard_map/ppermute | solution.py:382
  60.7 2.1 %collective-permute-done.20.refs_1_ = f32[2,64,128]{2,1,0:T(8,128)S(1)} collective-permute-done((f32[2,64,128]{2,1,0:T(8,128)S(1)}, f32[2,64,128]{2,1,0:T(8,128)S(1)}, u32[]{:S(2)}, u32[]{:S(2)}) %collective-permute-start.20) | collective-permute-done | bytes 65568 | tf_op jit(solution)/shard_map/ppermute | solution.py:382
  62.7 2.3 %collective-permute-done.21.refs_2_ = f32[2,64,128]{2,1,0:T(8,128)S(1)} collective-permute-done((f32[2,64,128]{2,1,0:T(8,128)S(1)}, f32[2,64,128]{2,1,0:T(8,128)S(1)}, u32[]{:S(2)}, u32[]{:S(2)}) %collective-permute-start.21) | collective-permute-done | bytes 65568 | tf_op jit(solution)/shard_map/ppermute | solution.py:383
  65.4 10.7 %all_to_all.15.received = f32[8,40,128]{2,1,0:T(8,128)S(1)} all-to-all(f32[8,40,128]{2,1,0:T(8,128)S(1)} %get-tuple-element.135), channel_id=1, replica_groups=mesh['row_0'=4,'row_1'=2,'col_0'=4,'col_1'=8] {'row_0','row_1'}, dimensions={0} | all-to-all | bytes 327680 | tf_op jit(solution)/shard_map/all_to_all | solution.py:424
  76.4 2.7 %collective-permute-start.24 = (f32[32,640]{1,0:T(8,128)S(1)}, f32[32,640]{1,0:T(8,128)S(1)}, u32[]{:S(2)}, u32[]{:S(2)}) collective-permute-start(f32[32,640]{1,0:T(8,128)S(1)} %get-tuple-element.138), channel_id=1, source_target_pairs={{1,0},{2,1},{3,2},{4,3},{5,4},{6,5},{7,6},{8,7},{9,8},{10,9},{11,1... | collective-permute-start | bytes 245768 | tf_op jit(solution)/shard_map/ppermute | solution.py:428
  79.1 3.2 %collective-permute-start.25 = (f32[32,640]{1,0:T(8,128)S(1)}, f32[32,640]{1,0:T(8,128)S(1)}, u32[]{:S(2)}, u32[]{:S(2)}) collective-permute-start(f32[32,640]{1,0:T(8,128)S(1)} %get-tuple-element.139), channel_id=1, source_target_pairs={{0,1},{1,2},{2,3},{3,4},{4,5},{5,6},{6,7},{7,8},{8,9},{9,10},{10,1... | collective-permute-start | bytes 245768 | tf_op jit(solution)/shard_map/ppermute | solution.py:429
  82.3 18.2 %all_to_all.16.sums = f32[32,1,128]{2,1,0:T(1,128)S(1)} all-to-all(f32[32,1,128]{2,1,0:T(1,128)S(1)} %get-tuple-element.137), channel_id=1, replica_groups=mesh['row_0'=4,'row_1'=2,'col_0'=4,'col_1'=8] {'col_0','col_1'}, dimensions={0} | all-to-all | bytes 32768 | tf_op jit(solution)/shard_map/all_to_all | solution.py:427
  100.5 6.9 %shard_map.91 = (f32[512,128]{1,0:T(8,128)}, f32[256,1,128]{2,1,0:T(1,128)S(1)}) custom-call(f32[32,1,128]{2,1,0:T(1,128)S(1)} %all_to_all.16.sums, f32[8,40,128]{2,1,0:T(8,128)S(1)} %all_to_all.15.received, f32[512,128]{1,0:T(8,128)S(1)} %get-tuple-element.136.step_dir, f32[512,128]{1,0:T(8,128)S(1)} %copy-done.1, ...), custom_call_target="tpu_custom_call" | custom-call | tf_op jit(solution)/shard_map/pallas_call | solution.py:343
  107.4 18.8 %all_to_all.17 = f32[256,1,128]{2,1,0:T(1,128)S(1)} all-to-all(f32[256,1,128]{2,1,0:T(1,128)S(1)} %get-tuple-element.141), channel_id=1, replica_groups=mesh['row_0'=4,'row_1'=2,'col_0'=4,'col_1'=8] {'row_0','row_1','col_0','..., dimensions={0} | all-to-all | bytes 262144 | tf_op jit(solution)/shard_map/all_to_all | solution.py:433
  (52 shorter events, 7.6 us)
Async XLA Ops:
  0.6 3.4 %copy-start = (bf16[1,1024,4096]{2,1,0:T(8,128)(2,1)S(1)}, bf16[1,1024,4096]{2,1,0:T(8,128)(2,1)}, u32[]{:S(2)}) copy-start(bf16[1,1024,4096]{2,1,0:T(8,128)(2,1)} %weights.3) | copy-start | bytes 25165828
  4.0 1.0 copy-start.2
  5.1 0.7 copy-start.4
  7.1 8.2 %collective-permute-start = (f32[2,128,128]{2,1,0:T(8,128)S(1)}, f32[2,128,128]{2,1,0:T(8,128)S(1)}, u32[]{:S(2)}, u32[]{:S(2)}) collective-permute-start(f32[2,128,128]{2,1,0:T(8,128)S(1)} %get-tuple-element.78), channel_id=1, source_target_pairs={{0,1},{1,2},{2,3},{3,4},{4,5},{5,6},{6,7},{7,0},{8,9},{9,10},{10,1... | collective-permute-start | bytes 393224 | tf_op jit(solution)/shard_map/ppermute | solution.py:382
  9.1 6.2 %collective-permute-start.1 = (f32[2,128,128]{2,1,0:T(8,128)S(1)}, f32[2,128,128]{2,1,0:T(8,128)S(1)}, u32[]{:S(2)}, u32[]{:S(2)}) collective-permute-start(f32[2,128,128]{2,1,0:T(8,128)S(1)} %get-tuple-element.79), channel_id=1, source_target_pairs={{1,0},{2,1},{3,2},{4,3},{5,4},{6,5},{7,6},{0,7},{9,8},{10,9},{11,1... | collective-permute-start | bytes 393224 | tf_op jit(solution)/shard_map/ppermute | solution.py:383
  9.2 10.4 %collective-permute-start.2 = (f32[4,128,128]{2,1,0:T(8,128)S(1)}, f32[4,128,128]{2,1,0:T(8,128)S(1)}, u32[]{:S(2)}, u32[]{:S(2)}) collective-permute-start(f32[4,128,128]{2,1,0:T(8,128)S(1)} %get-tuple-element.84), channel_id=1, source_target_pairs={{0,8},{8,16},{16,24},{24,0},{1,9},{9,17},{17,25},{25,1},{2,10},{10... | collective-permute-start | bytes 786440 | tf_op jit(solution)/shard_map/ppermute | solution.py:382
  10.7 8.9 %collective-permute-start.3 = (f32[4,128,128]{2,1,0:T(8,128)S(1)}, f32[4,128,128]{2,1,0:T(8,128)S(1)}, u32[]{:S(2)}, u32[]{:S(2)}) collective-permute-start(f32[4,128,128]{2,1,0:T(8,128)S(1)} %get-tuple-element.85), channel_id=1, source_target_pairs={{8,0},{16,8},{24,16},{0,24},{9,1},{17,9},{25,17},{1,25},{10,2},{18... | collective-permute-start | bytes 786440 | tf_op jit(solution)/shard_map/ppermute | solution.py:383
  15.3 9.6 %collective-permute-start.4 = (f32[4,128,128]{2,1,0:T(8,128)S(1)}, f32[4,128,128]{2,1,0:T(8,128)S(1)}, u32[]{:S(2)}, u32[]{:S(2)}) collective-permute-start(f32[4,128,128]{2,1,0:T(8,128)S(1)} %get-tuple-element.89), channel_id=1, source_target_pairs={{0,1},{1,2},{2,3},{3,4},{4,5},{5,6},{6,7},{7,0},{8,9},{9,10},{10,1... | collective-permute-start | bytes 786440 | tf_op jit(solution)/shard_map/ppermute | solution.py:382
  17.4 8.1 %collective-permute-start.5 = (f32[4,128,128]{2,1,0:T(8,128)S(1)}, f32[4,128,128]{2,1,0:T(8,128)S(1)}, u32[]{:S(2)}, u32[]{:S(2)}) collective-permute-start(f32[4,128,128]{2,1,0:T(8,128)S(1)} %get-tuple-element.90), channel_id=1, source_target_pairs={{1,0},{2,1},{3,2},{4,3},{5,4},{6,5},{7,6},{0,7},{9,8},{10,9},{11,1... | collective-permute-start | bytes 786440 | tf_op jit(solution)/shard_map/ppermute | solution.py:383
  19.6 18.4 %collective-permute-start.8 = (f32[8,128,128]{2,1,0:T(8,128)S(1)}, f32[8,128,128]{2,1,0:T(8,128)S(1)}, u32[]{:S(2)}, u32[]{:S(2)}) collective-permute-start(f32[8,128,128]{2,1,0:T(8,128)S(1)} %get-tuple-element.99), channel_id=1, source_target_pairs={{0,8},{8,16},{16,24},{24,0},{1,9},{9,17},{17,25},{25,1},{2,10},{10... | collective-permute-start | bytes 1572872 | tf_op jit(solution)/shard_map/ppermute | solution.py:382
  20.0 18.1 %collective-permute-start.9 = (f32[8,128,128]{2,1,0:T(8,128)S(1)}, f32[8,128,128]{2,1,0:T(8,128)S(1)}, u32[]{:S(2)}, u32[]{:S(2)}) collective-permute-start(f32[8,128,128]{2,1,0:T(8,128)S(1)} %get-tuple-element.100), channel_id=1, source_target_pairs={{8,0},{16,8},{24,16},{0,24},{9,1},{17,9},{25,17},{1,25},{10,2},{18... | collective-permute-start | bytes 1572872 | tf_op jit(solution)/shard_map/ppermute | solution.py:383
  25.5 7.0 %collective-permute-start.6 = (f32[4,128,128]{2,1,0:T(8,128)S(1)}, f32[4,128,128]{2,1,0:T(8,128)S(1)}, u32[]{:S(2)}, u32[]{:S(2)}) collective-permute-start(f32[4,128,128]{2,1,0:T(8,128)S(1)} %get-tuple-element.94), channel_id=1, source_target_pairs={{0,1},{1,2},{2,3},{3,4},{4,5},{5,6},{6,7},{7,0},{8,9},{9,10},{10,1... | collective-permute-start | bytes 786440 | tf_op jit(solution)/shard_map/ppermute | solution.py:382
  28.6 7.3 %collective-permute-start.7 = (f32[4,128,128]{2,1,0:T(8,128)S(1)}, f32[4,128,128]{2,1,0:T(8,128)S(1)}, u32[]{:S(2)}, u32[]{:S(2)}) collective-permute-start(f32[4,128,128]{2,1,0:T(8,128)S(1)} %get-tuple-element.95), channel_id=1, source_target_pairs={{1,0},{2,1},{3,2},{4,3},{5,4},{6,5},{7,6},{0,7},{9,8},{10,9},{11,1... | collective-permute-start | bytes 786440 | tf_op jit(solution)/shard_map/ppermute | solution.py:383
  35.9 6.4 %collective-permute-start.10 = (f32[4,128,128]{2,1,0:T(8,128)S(1)}, f32[4,128,128]{2,1,0:T(8,128)S(1)}, u32[]{:S(2)}, u32[]{:S(2)}) collective-permute-start(f32[4,128,128]{2,1,0:T(8,128)S(1)} %get-tuple-element.104), channel_id=1, source_target_pairs={{0,1},{1,2},{2,3},{3,4},{4,5},{5,6},{6,7},{7,0},{8,9},{9,10},{10,1... | collective-permute-start | bytes 786440 | tf_op jit(solution)/shard_map/ppermute | solution.py:382
  38.0 6.5 %collective-permute-start.11 = (f32[4,128,128]{2,1,0:T(8,128)S(1)}, f32[4,128,128]{2,1,0:T(8,128)S(1)}, u32[]{:S(2)}, u32[]{:S(2)}) collective-permute-start(f32[4,128,128]{2,1,0:T(8,128)S(1)} %get-tuple-element.105), channel_id=1, source_target_pairs={{1,0},{2,1},{3,2},{4,3},{5,4},{6,5},{7,6},{0,7},{9,8},{10,9},{11,1... | collective-permute-start | bytes 786440 | tf_op jit(solution)/shard_map/ppermute | solution.py:383
  38.1 22.4 %copy-start.5 = (bf16[256,512]{1,0:T(8,128)(2,1)S(1)}, bf16[256,512]{1,0:T(8,128)(2,1)}, u32[]{:S(2)}) copy-start(bf16[256,512]{1,0:T(8,128)(2,1)} %param.7) | copy-start | bytes 786436
  38.2 26.9 %copy-start.1 = (f32[512,128]{1,0:T(8,128)S(1)}, f32[512,128]{1,0:T(8,128)}, u32[]{:S(2)}) copy-start(f32[512,128]{1,0:T(8,128)} %image.3) | copy-start | bytes 786436
  38.2 26.9 %copy-start.3 = (f32[512,128]{1,0:T(8,128)S(1)}, f32[512,128]{1,0:T(8,128)}, u32[]{:S(2)}) copy-start(f32[512,128]{1,0:T(8,128)} %refs_7_.1) | copy-start | bytes 786436
  38.2 6.4 %collective-permute-start.12 = (f32[1,64,128]{2,1,0:T(8,128)S(1)}, f32[1,64,128]{2,1,0:T(8,128)S(1)}, u32[]{:S(2)}, u32[]{:S(2)}) collective-permute-start(f32[1,64,128]{2,1,0:T(8,128)S(1)} %get-tuple-element.110), channel_id=1, source_target_pairs={{0,1},{1,2},{2,3},{3,4},{4,5},{5,6},{6,7},{7,0},{8,9},{9,10},{10,1... | collective-permute-start | bytes 98312 | tf_op jit(solution)/shard_map/ppermute | solution.py:382
  40.3 5.0 %collective-permute-start.13 = (f32[1,64,128]{2,1,0:T(8,128)S(1)}, f32[1,64,128]{2,1,0:T(8,128)S(1)}, u32[]{:S(2)}, u32[]{:S(2)}) collective-permute-start(f32[1,64,128]{2,1,0:T(8,128)S(1)} %get-tuple-element.111), channel_id=1, source_target_pairs={{1,0},{2,1},{3,2},{4,3},{5,4},{6,5},{7,6},{0,7},{9,8},{10,9},{11,1... | collective-permute-start | bytes 98312 | tf_op jit(solution)/shard_map/ppermute | solution.py:383
  45.3 7.3 %collective-permute-start.16 = (f32[2,64,128]{2,1,0:T(8,128)S(1)}, f32[2,64,128]{2,1,0:T(8,128)S(1)}, u32[]{:S(2)}, u32[]{:S(2)}) collective-permute-start(f32[2,64,128]{2,1,0:T(8,128)S(1)} %get-tuple-element.121), channel_id=1, source_target_pairs={{0,1},{1,2},{2,3},{3,4},{4,5},{5,6},{6,7},{7,0},{8,9},{9,10},{10,1... | collective-permute-start | bytes 196616 | tf_op jit(solution)/shard_map/ppermute | solution.py:382
  46.8 5.7 %collective-permute-start.17 = (f32[2,64,128]{2,1,0:T(8,128)S(1)}, f32[2,64,128]{2,1,0:T(8,128)S(1)}, u32[]{:S(2)}, u32[]{:S(2)}) collective-permute-start(f32[2,64,128]{2,1,0:T(8,128)S(1)} %get-tuple-element.122), channel_id=1, source_target_pairs={{1,0},{2,1},{3,2},{4,3},{5,4},{6,5},{7,6},{0,7},{9,8},{10,9},{11,1... | collective-permute-start | bytes 196616 | tf_op jit(solution)/shard_map/ppermute | solution.py:383
  47.4 5.1 %collective-permute-start.14 = (f32[1,64,128]{2,1,0:T(8,128)S(1)}, f32[1,64,128]{2,1,0:T(8,128)S(1)}, u32[]{:S(2)}, u32[]{:S(2)}) collective-permute-start(f32[1,64,128]{2,1,0:T(8,128)S(1)} %get-tuple-element.116), channel_id=1, source_target_pairs={{0,8},{8,16},{16,24},{24,0},{1,9},{9,17},{17,25},{25,1},{2,10},{10... | collective-permute-start | bytes 98312 | tf_op jit(solution)/shard_map/ppermute | solution.py:382
  47.9 4.7 %collective-permute-start.15 = (f32[1,64,128]{2,1,0:T(8,128)S(1)}, f32[1,64,128]{2,1,0:T(8,128)S(1)}, u32[]{:S(2)}, u32[]{:S(2)}) collective-permute-start(f32[1,64,128]{2,1,0:T(8,128)S(1)} %get-tuple-element.117), channel_id=1, source_target_pairs={{8,0},{16,8},{24,16},{0,24},{9,1},{17,9},{25,17},{1,25},{10,2},{18... | collective-permute-start | bytes 98312 | tf_op jit(solution)/shard_map/ppermute | solution.py:383
  52.6 5.3 %collective-permute-start.18 = (f32[2,64,128]{2,1,0:T(8,128)S(1)}, f32[2,64,128]{2,1,0:T(8,128)S(1)}, u32[]{:S(2)}, u32[]{:S(2)}) collective-permute-start(f32[2,64,128]{2,1,0:T(8,128)S(1)} %get-tuple-element.126), channel_id=1, source_target_pairs={{0,1},{1,2},{2,3},{3,4},{4,5},{5,6},{6,7},{7,0},{8,9},{9,10},{10,1... | collective-permute-start | bytes 196616 | tf_op jit(solution)/shard_map/ppermute | solution.py:382
  54.1 4.3 %collective-permute-start.19 = (f32[2,64,128]{2,1,0:T(8,128)S(1)}, f32[2,64,128]{2,1,0:T(8,128)S(1)}, u32[]{:S(2)}, u32[]{:S(2)}) collective-permute-start(f32[2,64,128]{2,1,0:T(8,128)S(1)} %get-tuple-element.127), channel_id=1, source_target_pairs={{1,0},{2,1},{3,2},{4,3},{5,4},{6,5},{7,6},{0,7},{9,8},{10,9},{11,1... | collective-permute-start | bytes 196616 | tf_op jit(solution)/shard_map/ppermute | solution.py:383
  54.7 6.0 %collective-permute-start.22 = (f32[2,64,128]{2,1,0:T(8,128)S(1)}, f32[2,64,128]{2,1,0:T(8,128)S(1)}, u32[]{:S(2)}, u32[]{:S(2)}) collective-permute-start(f32[2,64,128]{2,1,0:T(8,128)S(1)} %get-tuple-element.133), channel_id=1, source_target_pairs={{0,8},{8,16},{16,24},{24,0},{1,9},{9,17},{17,25},{25,1},{2,10},{10... | collective-permute-start | bytes 196616 | tf_op jit(solution)/shard_map/ppermute | solution.py:382
  55.4 5.2 %collective-permute-start.23 = (f32[2,64,128]{2,1,0:T(8,128)S(1)}, f32[2,64,128]{2,1,0:T(8,128)S(1)}, u32[]{:S(2)}, u32[]{:S(2)}) collective-permute-start(f32[2,64,128]{2,1,0:T(8,128)S(1)} %get-tuple-element.134), channel_id=1, source_target_pairs={{8,0},{16,8},{24,16},{0,24},{9,1},{17,9},{25,17},{1,25},{10,2},{18... | collective-permute-start | bytes 196616 | tf_op jit(solution)/shard_map/ppermute | solution.py:383
  58.4 4.3 %collective-permute-start.20 = (f32[2,64,128]{2,1,0:T(8,128)S(1)}, f32[2,64,128]{2,1,0:T(8,128)S(1)}, u32[]{:S(2)}, u32[]{:S(2)}) collective-permute-start(f32[2,64,128]{2,1,0:T(8,128)S(1)} %get-tuple-element.131), channel_id=1, source_target_pairs={{0,1},{1,2},{2,3},{3,4},{4,5},{5,6},{6,7},{7,0},{8,9},{9,10},{10,1... | collective-permute-start | bytes 196616 | tf_op jit(solution)/shard_map/ppermute | solution.py:382
  60.2 4.9 %collective-permute-start.21 = (f32[2,64,128]{2,1,0:T(8,128)S(1)}, f32[2,64,128]{2,1,0:T(8,128)S(1)}, u32[]{:S(2)}, u32[]{:S(2)}) collective-permute-start(f32[2,64,128]{2,1,0:T(8,128)S(1)} %get-tuple-element.132), channel_id=1, source_target_pairs={{1,0},{2,1},{3,2},{4,3},{5,4},{6,5},{7,6},{0,7},{9,8},{10,9},{11,1... | collective-permute-start | bytes 196616 | tf_op jit(solution)/shard_map/ppermute | solution.py:383
  76.4 24.1 %collective-permute-start.24 = (f32[32,640]{1,0:T(8,128)S(1)}, f32[32,640]{1,0:T(8,128)S(1)}, u32[]{:S(2)}, u32[]{:S(2)}) collective-permute-start(f32[32,640]{1,0:T(8,128)S(1)} %get-tuple-element.138), channel_id=1, source_target_pairs={{1,0},{2,1},{3,2},{4,3},{5,4},{6,5},{7,6},{8,7},{9,8},{10,9},{11,1... | collective-permute-start | bytes 245768 | tf_op jit(solution)/shard_map/ppermute | solution.py:428
  79.1 21.4 %collective-permute-start.25 = (f32[32,640]{1,0:T(8,128)S(1)}, f32[32,640]{1,0:T(8,128)S(1)}, u32[]{:S(2)}, u32[]{:S(2)}) collective-permute-start(f32[32,640]{1,0:T(8,128)S(1)} %get-tuple-element.139), channel_id=1, source_target_pairs={{0,1},{1,2},{2,3},{3,4},{4,5},{5,6},{6,7},{7,8},{8,9},{9,10},{10,1... | collective-permute-start | bytes 245768 | tf_op jit(solution)/shard_map/ppermute | solution.py:429

commit v4 on v3

--- a/solution.py
+++ b/solution.py
@@ -93,7 +93,8 @@
     )(marks, residual, weights)
 
 
-def relay_kernel(chunks, from_behind, from_ahead, to_ahead, to_behind, *, step):
+def relay_kernel(chunks, *refs, step):
+    from_behind, *from_ahead, to_ahead, to_behind = refs
     ahead, behind = chunks.at[step], chunks.at[chunks.shape[0] - step]
     count = to_ahead.shape[0]
     brought = from_behind.shape[0]
@@ -102,40 +103,40 @@
         to_ahead[k] = value + from_behind[k] if k < brought else value
         value = behind[k]
         here = k - (count - brought)
-        to_behind[k] = value + from_ahead[here] if here >= 0 else value
-
-
-def relay(chunks, from_behind, from_ahead, step):
+        to_behind[k] = value + from_ahead[0][here] if from_ahead and here >= 0 else value
+
+
+def relay(chunks, brought, step):
     shape = jax.ShapeDtypeStruct(chunks.shape[1:], jnp.float32)
     return pl.pallas_call(
         functools.partial(relay_kernel, step=step),
-        in_specs=[vmem()] * 3,
+        in_specs=[vmem()] * (1 + len(brought)),
         out_specs=[vmem()] * 2,
         out_shape=[shape, shape],
         compiler_params=params(8),
-    )(chunks, from_behind, from_ahead)
-
-
-def collect_kernel(chunks, from_behind, from_ahead, up, down, out, *, axis):
+    )(chunks, *brought)
+
+
+def collect_kernel(chunks, from_behind, from_ahead, far, out, *, axis):
     n = chunks.shape[1]
-    half = up.shape[1]
+    half = far.shape[1]
     for step in range(n):
         k = turned(axis, step)
         total = chunks[0, k] + from_behind[k] + from_ahead[k]
         if step == n // 2:
-            up[0], down[0] = total[:half], total[half:]
+            far[0], far[1] = total[:half], total[half:]
         else:
             out[step, 0], out[step, 1] = total[:half], total[half:]
 
 
 def collect(chunks, from_behind, from_ahead, axis):
     _, n, angles, _ = chunks.shape
-    half = jax.ShapeDtypeStruct((1, angles // 2, LANES), jnp.float32)
+    far = jax.ShapeDtypeStruct((2, angles // 2, LANES), jnp.float32)
     return pl.pallas_call(
         functools.partial(collect_kernel, axis=axis),
         in_specs=[vmem()] * 3,
-        out_specs=[vmem()] * 3,
-        out_shape=[half, half, jax.ShapeDtypeStruct((n, 2, angles // 2, LANES), jnp.float32)],
+        out_specs=[vmem()] * 2,
+        out_shape=[far, jax.ShapeDtypeStruct((n, 2, angles // 2, LANES), jnp.float32)],
         compiler_params=params(8),
     )(chunks, from_behind, from_ahead)
 
@@ -378,10 +379,8 @@
         axis = "col_0" if name.endswith("x") else "col_1"
         n = lax.axis_size(axis)
         ring = [(i, (i + 1) % n) for i in range(n)]
-        flight[name] = (
-            lax.ppermute(pair[0], axis, ring),
-            lax.ppermute(pair[1], axis, [(j, i) for i, j in ring]),
-        )
+        ways = (ring, [(j, i) for i, j in ring])
+        flight[name] = [lax.ppermute(part, axis, way) for part, way in zip(pair, ways)]
 
     send("first_x", far[:2])
     send("first_z", far[2:])
@@ -401,18 +400,18 @@
 
     def onward(name, step):
         here = flush(chunks[name])
-        waiting.append((name, relay(here, *flight[name], step)))
+        waiting.append((name, relay(here, flight[name], step)))
 
     def turn(name, then, axis):
         here = flush(chunks[name])
-        up, down, chunks[then] = collect(here, *flight[name], axis)
-        waiting.append((then, (up, down)))
+        far, chunks[then] = collect(here, *flight[name], axis)
+        waiting.append((then, (far,)))
 
     onward("first_z", 3)
     onward("first_x", 1)
     onward("first_z", 2)
+    turn("first_x", "then_z", "col_1")
     onward("first_z", 1)
-    turn("first_x", "then_z", "col_1")
     turn("first_z", "then_x", "col_0")
     onward("then_z", 3)
     onward("then_x", 1)

time: 131 us -> 129 us (0.985)
  starting transfers between devices: 38.7 us -> 33.1 us
  waiting for transfers between devices: 21.5 us -> 26.2 us
    ppermute x24 -> x22, starting transfers between devices: 32.9 us -> 27.2 us  [send(): lax.ppermute(part, axis, way)]
    ppermute x24 -> x22, waiting for transfers between devices: 21.5 us -> 26.2 us  [send(): lax.ppermute(part, axis, way)]
  transfers between devices with their start and end apart: 26 -> 24, of which waited for: 11 -> 14; matrix products, arithmetic and copies ran while one was open for 0% -> 0% of each run, Pallas kernels for 2% -> 2%
where the time goes in v4:
time: 129 us; the launch traced here: 127 us
  blocking collectives  47 us (36%)
  starting transfers between devices  33.1 us (26%)
  waiting for transfers between devices  26.2 us (20%)
  Pallas kernels  12.1 us (9%)
  local copies, waits for them, and re-layouts  5.22 us (4%)
  between operations  2.59 us (2%)
    ppermute x22, starting transfers between devices, send(): lax.ppermute(part, axis, way)  27.2 us
    ppermute x22, waiting for transfers between devices, send(): lax.ppermute(part, axis, way)  26.2 us
    all_to_all x1, blocking collectives, step(): changes = lax.all_to_all(change_slots, ROW_COL, 0, 0, tiled=True)  18.8 us
    all_to_all x1, blocking collectives, step(): sums = lax.all_to_all(sum_slots, COL, 0, 0, tiled=True)  17.5 us
    all_to_all x1, blocking collectives, step(): received = lax.all_to_all(row_slots, ROW, 0, 0, tiled=True)  10.7 us
    pallas_call x1, Pallas kernels, denoise(): pl.pallas_call(functools.partial(denoise_kernel, n_row=n_row, n_col=n_col...  6.92 us
    unnamed x13, local copies, waits for them, and re-layouts  5.22 us
    pallas_call x2, Pallas kernels, back_project(): pl.pallas_call(functools.partial(kernel, n_x=n_x, n_z=n_z), in_specs=[sme...  4.16 us
  transfers between devices with their start and end apart: 24, of which 14 were waited for; matrix products, arithmetic and copies ran while one was open for 0% of the time, Pallas kernels for 2%

profile of v4, /device:TPU:32, one launch (start us, length us, event | category | flops | bytes accessed | tf_op | source)
XLA Modules:
  0.0 127.1 jit_solution(11770698064595563489)
XLA Ops:
  0.6 3.4 %copy-done = bf16[1,1024,4096]{2,1,0:T(8,128)(2,1)S(1)} copy-done((bf16[1,1024,4096]{2,1,0:T(8,128)(2,1)S(1)}, bf16[1,1024,4096]{2,1,0:T(8,128)(2,1)}, u32[]{:S(2)}) %copy-start) | copy-done | bytes 8388632
  4.0 1.0 copy-done.2
  5.7 1.3 %shard_map.77 = (f32[4,128,128]{2,1,0:T(8,128)S(1)}, f32[4,128,128]{2,1,0:T(8,128)S(1)}, f32[2,128,128]{2,1,0:T(8,128)S(1)}, f32[2,128,128]{2,1,0:T(8,128)S(1)}) custom-call(s32[1,32]{1,0:T(1,128)S(1)} %bitcast.3, bf16[256,1024]{1,0:T(8,128)(2,1)S(1)} %copy-done.2, bf16[1,1024,4096]{2,1,0:T(8,128)(2,1)S(1)} %copy-done), custom_call_target="tpu_custom_call" | custom-call | tf_op jit(solution)/shard_map/pallas_call | solution.py:87
  7.1 1.6 %collective-permute-start.2 = (f32[4,128,128]{2,1,0:T(8,128)S(1)}, f32[4,128,128]{2,1,0:T(8,128)S(1)}, u32[]{:S(2)}, u32[]{:S(2)}) collective-permute-start(f32[4,128,128]{2,1,0:T(8,128)S(1)} %get-tuple-element.80), channel_id=1, source_target_pairs={{0,8},{8,16},{16,24},{24,0},{1,9},{9,17},{17,25},{25,1},{2,10},{10... | collective-permute-start | bytes 786440 | tf_op jit(solution)/shard_map/ppermute | solution.py:383
  8.6 1.7 %collective-permute-start.3 = (f32[4,128,128]{2,1,0:T(8,128)S(1)}, f32[4,128,128]{2,1,0:T(8,128)S(1)}, u32[]{:S(2)}, u32[]{:S(2)}) collective-permute-start(f32[4,128,128]{2,1,0:T(8,128)S(1)} %get-tuple-element.81), channel_id=1, source_target_pairs={{8,0},{16,8},{24,16},{0,24},{9,1},{17,9},{25,17},{1,25},{10,2},{18... | collective-permute-start | bytes 786440 | tf_op jit(solution)/shard_map/ppermute | solution.py:383
  10.4 1.9 %collective-permute-start = (f32[2,128,128]{2,1,0:T(8,128)S(1)}, f32[2,128,128]{2,1,0:T(8,128)S(1)}, u32[]{:S(2)}, u32[]{:S(2)}) collective-permute-start(f32[2,128,128]{2,1,0:T(8,128)S(1)} %get-tuple-element.74), channel_id=1, source_target_pairs={{0,1},{1,2},{2,3},{3,4},{4,5},{5,6},{6,7},{7,0},{8,9},{9,10},{10,1... | collective-permute-start | bytes 393224 | tf_op jit(solution)/shard_map/ppermute | solution.py:383
  12.4 2.8 %shard_map.78 = (f32[4,8,128,128]{3,2,1,0:T(8,128)S(1)}, f32[8,4,128,128]{3,2,1,0:T(8,128)S(1)}) custom-call(s32[1,32]{1,0:T(1,128)S(1)} %bitcast.4, bf16[256,1024]{1,0:T(8,128)(2,1)S(1)} %copy-done.2, bf16[1,1024,4096]{2,1,0:T(8,128)(2,1)S(1)} %copy-done), custom_call_target="tpu_custom_call" | custom-call | tf_op jit(solution)/shard_map/pallas_call | solution.py:87
  15.3 1.9 %collective-permute-done.1.refs_1_ = f32[2,128,128]{2,1,0:T(8,128)S(1)} collective-permute-done((f32[2,128,128]{2,1,0:T(8,128)S(1)}, f32[2,128,128]{2,1,0:T(8,128)S(1)}, u32[]{:S(2)}, u32[]{:S(2)}) %collective-permute-start.1) | collective-permute-done | bytes 131104 | tf_op jit(solution)/shard_map/ppermute | solution.py:383
  17.3 3.1 %collective-permute-start.4 = (f32[4,128,128]{2,1,0:T(8,128)S(1)}, f32[4,128,128]{2,1,0:T(8,128)S(1)}, u32[]{:S(2)}, u32[]{:S(2)}) collective-permute-start(f32[4,128,128]{2,1,0:T(8,128)S(1)} %get-tuple-element.85), channel_id=1, source_target_pairs={{0,1},{1,2},{2,3},{3,4},{4,5},{5,6},{6,7},{7,0},{8,9},{9,10},{10,1... | collective-permute-start | bytes 786440 | tf_op jit(solution)/shard_map/ppermute | solution.py:383
  20.9 3.0 %collective-permute-start.7 = (f32[8,128,128]{2,1,0:T(8,128)S(1)}, f32[8,128,128]{2,1,0:T(8,128)S(1)}, u32[]{:S(2)}, u32[]{:S(2)}) collective-permute-start(f32[8,128,128]{2,1,0:T(8,128)S(1)} %get-tuple-element.91), channel_id=1, source_target_pairs={{8,0},{16,8},{24,16},{0,24},{9,1},{17,9},{25,17},{1,25},{10,2},{18... | collective-permute-start | bytes 1572872 | tf_op jit(solution)/shard_map/ppermute | solution.py:383
  24.8 3.2 %collective-permute-done.5.refs_1_ = f32[4,128,128]{2,1,0:T(8,128)S(1)} collective-permute-done((f32[4,128,128]{2,1,0:T(8,128)S(1)}, f32[4,128,128]{2,1,0:T(8,128)S(1)}, u32[]{:S(2)}, u32[]{:S(2)}) %collective-permute-start.5) | collective-permute-done | bytes 262176 | tf_op jit(solution)/shard_map/ppermute | solution.py:383
  28.0 2.1 %collective-permute-start.8 = (f32[4,128,128]{2,1,0:T(8,128)S(1)}, f32[4,128,128]{2,1,0:T(8,128)S(1)}, u32[]{:S(2)}, u32[]{:S(2)}) collective-permute-start(f32[4,128,128]{2,1,0:T(8,128)S(1)} %get-tuple-element.94), channel_id=1, source_target_pairs={{0,1},{1,2},{2,3},{3,4},{4,5},{5,6},{6,7},{7,0},{8,9},{9,10},{10,1... | collective-permute-start | bytes 786440 | tf_op jit(solution)/shard_map/ppermute | solution.py:383
  30.1 3.4 %collective-permute-done.6.from_behind = f32[8,128,128]{2,1,0:T(8,128)S(1)} collective-permute-done((f32[8,128,128]{2,1,0:T(8,128)S(1)}, f32[8,128,128]{2,1,0:T(8,128)S(1)}, u32[]{:S(2)}, u32[]{:S(2)}) %collective-permute-start.6) | collective-permute-done | bytes 524320 | tf_op jit(solution)/shard_map/ppermute | solution.py:383
  34.5 2.0 %collective-permute-done.9.refs_1_ = f32[4,128,128]{2,1,0:T(8,128)S(1)} collective-permute-done((f32[4,128,128]{2,1,0:T(8,128)S(1)}, f32[4,128,128]{2,1,0:T(8,128)S(1)}, u32[]{:S(2)}, u32[]{:S(2)}) %collective-permute-start.9) | collective-permute-done | bytes 262176 | tf_op jit(solution)/shard_map/ppermute | solution.py:383
  36.6 1.5 %collective-permute-start.10 = (f32[4,128,128]{2,1,0:T(8,128)S(1)}, f32[4,128,128]{2,1,0:T(8,128)S(1)}, u32[]{:S(2)}, u32[]{:S(2)}) collective-permute-start(f32[4,128,128]{2,1,0:T(8,128)S(1)} %get-tuple-element.99), channel_id=1, source_target_pairs={{0,1},{1,2},{2,3},{3,4},{4,5},{5,6},{6,7},{7,0},{8,9},{9,10},{10,1... | collective-permute-start | bytes 786440 | tf_op jit(solution)/shard_map/ppermute | solution.py:383
  38.7 1.4 %collective-permute-start.12 = (f32[2,64,128]{2,1,0:T(8,128)S(1)}, f32[2,64,128]{2,1,0:T(8,128)S(1)}, u32[]{:S(2)}, u32[]{:S(2)}) collective-permute-start(f32[2,64,128]{2,1,0:T(8,128)S(1)} %get-tuple-element.104), channel_id=1, source_target_pairs={{0,1},{1,2},{2,3},{3,4},{4,5},{5,6},{6,7},{7,0},{8,9},{9,10},{10,1... | collective-permute-start | bytes 196616 | tf_op jit(solution)/shard_map/ppermute | solution.py:383
  40.1 3.6 %collective-permute-done.10.from_behind = f32[4,128,128]{2,1,0:T(8,128)S(1)} collective-permute-done((f32[4,128,128]{2,1,0:T(8,128)S(1)}, f32[4,128,128]{2,1,0:T(8,128)S(1)}, u32[]{:S(2)}, u32[]{:S(2)}) %collective-permute-start.10) | collective-permute-done | bytes 262176 | tf_op jit(solution)/shard_map/ppermute | solution.py:383
  44.9 1.6 %collective-permute-start.14 = (f32[2,64,128]{2,1,0:T(8,128)S(1)}, f32[2,64,128]{2,1,0:T(8,128)S(1)}, u32[]{:S(2)}, u32[]{:S(2)}) collective-permute-start(f32[2,64,128]{2,1,0:T(8,128)S(1)} %get-tuple-element.113), channel_id=1, source_target_pairs={{0,1},{1,2},{2,3},{3,4},{4,5},{5,6},{6,7},{7,0},{8,9},{9,10},{10,1... | collective-permute-start | bytes 196616 | tf_op jit(solution)/shard_map/ppermute | solution.py:383
  47.0 3.1 %collective-permute-done.13.refs_0_ = f32[2,64,128]{2,1,0:T(8,128)S(1)} collective-permute-done((f32[2,64,128]{2,1,0:T(8,128)S(1)}, f32[2,64,128]{2,1,0:T(8,128)S(1)}, u32[]{:S(2)}, u32[]{:S(2)}) %collective-permute-start.13) | collective-permute-done | bytes 65568 | tf_op jit(solution)/shard_map/ppermute | solution.py:383
  50.9 2.0 %collective-permute-start.16 = (f32[2,64,128]{2,1,0:T(8,128)S(1)}, f32[2,64,128]{2,1,0:T(8,128)S(1)}, u32[]{:S(2)}, u32[]{:S(2)}) collective-permute-start(f32[2,64,128]{2,1,0:T(8,128)S(1)} %get-tuple-element.118), channel_id=1, source_target_pairs={{0,1},{1,2},{2,3},{3,4},{4,5},{5,6},{6,7},{7,0},{8,9},{9,10},{10,1... | collective-permute-start | bytes 196616 | tf_op jit(solution)/shard_map/ppermute | solution.py:383
  53.0 1.3 %collective-permute-start.20 = (f32[2,64,128]{2,1,0:T(8,128)S(1)}, f32[2,64,128]{2,1,0:T(8,128)S(1)}, u32[]{:S(2)}, u32[]{:S(2)}) collective-permute-start(f32[2,64,128]{2,1,0:T(8,128)S(1)} %get-tuple-element.125), channel_id=1, source_target_pairs={{0,8},{8,16},{16,24},{24,0},{1,9},{9,17},{17,25},{25,1},{2,10},{10... | collective-permute-start | bytes 196616 | tf_op jit(solution)/shard_map/ppermute | solution.py:383
  54.3 1.9 %collective-permute-start.21 = (f32[2,64,128]{2,1,0:T(8,128)S(1)}, f32[2,64,128]{2,1,0:T(8,128)S(1)}, u32[]{:S(2)}, u32[]{:S(2)}) collective-permute-start(f32[2,64,128]{2,1,0:T(8,128)S(1)} %get-tuple-element.126), channel_id=1, source_target_pairs={{8,0},{16,8},{24,16},{0,24},{9,1},{17,9},{25,17},{1,25},{10,2},{18... | collective-permute-start | bytes 196616 | tf_op jit(solution)/shard_map/ppermute | solution.py:383
  56.3 1.4 %collective-permute-done.17.refs_1_ = f32[2,64,128]{2,1,0:T(8,128)S(1)} collective-permute-done((f32[2,64,128]{2,1,0:T(8,128)S(1)}, f32[2,64,128]{2,1,0:T(8,128)S(1)}, u32[]{:S(2)}, u32[]{:S(2)}) %collective-permute-start.17) | collective-permute-done | bytes 65568 | tf_op jit(solution)/shard_map/ppermute | solution.py:383
  57.6 2.1 %collective-permute-start.18 = (f32[2,64,128]{2,1,0:T(8,128)S(1)}, f32[2,64,128]{2,1,0:T(8,128)S(1)}, u32[]{:S(2)}, u32[]{:S(2)}) collective-permute-start(f32[2,64,128]{2,1,0:T(8,128)S(1)} %get-tuple-element.123), channel_id=1, source_target_pairs={{0,1},{1,2},{2,3},{3,4},{4,5},{5,6},{6,7},{7,0},{8,9},{9,10},{10,1... | collective-permute-start | bytes 196616 | tf_op jit(solution)/shard_map/ppermute | solution.py:383
  59.9 2.1 %collective-permute-done.18.refs_1_ = f32[2,64,128]{2,1,0:T(8,128)S(1)} collective-permute-done((f32[2,64,128]{2,1,0:T(8,128)S(1)}, f32[2,64,128]{2,1,0:T(8,128)S(1)}, u32[]{:S(2)}, u32[]{:S(2)}) %collective-permute-start.18) | collective-permute-done | bytes 65568 | tf_op jit(solution)/shard_map/ppermute | solution.py:383
  62.0 2.0 %collective-permute-done.19.refs_2_ = f32[2,64,128]{2,1,0:T(8,128)S(1)} collective-permute-done((f32[2,64,128]{2,1,0:T(8,128)S(1)}, f32[2,64,128]{2,1,0:T(8,128)S(1)}, u32[]{:S(2)}, u32[]{:S(2)}) %collective-permute-start.19) | collective-permute-done | bytes 65568 | tf_op jit(solution)/shard_map/ppermute | solution.py:383
  64.4 10.7 %all_to_all.15.received = f32[8,40,128]{2,1,0:T(8,128)S(1)} all-to-all(f32[8,40,128]{2,1,0:T(8,128)S(1)} %get-tuple-element.127), channel_id=1, replica_groups=mesh['row_0'=4,'row_1'=2,'col_0'=4,'col_1'=8] {'row_0','row_1'}, dimensions={0} | all-to-all | bytes 327680 | tf_op jit(solution)/shard_map/all_to_all | solution.py:423
  75.4 1.9 %collective-permute-start.22 = (f32[32,640]{1,0:T(8,128)S(1)}, f32[32,640]{1,0:T(8,128)S(1)}, u32[]{:S(2)}, u32[]{:S(2)}) collective-permute-start(f32[32,640]{1,0:T(8,128)S(1)} %get-tuple-element.130), channel_id=1, source_target_pairs={{1,0},{2,1},{3,2},{4,3},{5,4},{6,5},{7,6},{8,7},{9,8},{10,9},{11,1... | collective-permute-start | bytes 245768 | tf_op jit(solution)/shard_map/ppermute | solution.py:427
  77.3 3.9 %collective-permute-start.23 = (f32[32,640]{1,0:T(8,128)S(1)}, f32[32,640]{1,0:T(8,128)S(1)}, u32[]{:S(2)}, u32[]{:S(2)}) collective-permute-start(f32[32,640]{1,0:T(8,128)S(1)} %get-tuple-element.131), channel_id=1, source_target_pairs={{0,1},{1,2},{2,3},{3,4},{4,5},{5,6},{6,7},{7,8},{8,9},{9,10},{10,1... | collective-permute-start | bytes 245768 | tf_op jit(solution)/shard_map/ppermute | solution.py:428
  81.2 17.5 %all_to_all.16.sums = f32[32,1,128]{2,1,0:T(1,128)S(1)} all-to-all(f32[32,1,128]{2,1,0:T(1,128)S(1)} %get-tuple-element.129), channel_id=1, replica_groups=mesh['row_0'=4,'row_1'=2,'col_0'=4,'col_1'=8] {'col_0','col_1'}, dimensions={0} | all-to-all | bytes 32768 | tf_op jit(solution)/shard_map/all_to_all | solution.py:426
  98.7 6.9 %shard_map.91 = (f32[512,128]{1,0:T(8,128)}, f32[256,1,128]{2,1,0:T(1,128)S(1)}) custom-call(f32[32,1,128]{2,1,0:T(1,128)S(1)} %all_to_all.16.sums, f32[8,40,128]{2,1,0:T(8,128)S(1)} %all_to_all.15.received, f32[512,128]{1,0:T(8,128)S(1)} %get-tuple-element.128.step_dir, f32[512,128]{1,0:T(8,128)S(1)} %copy-done.1, ...), custom_call_target="tpu_custom_call" | custom-call | tf_op jit(solution)/shard_map/pallas_call | solution.py:344
  105.6 18.8 %all_to_all.17 = f32[256,1,128]{2,1,0:T(1,128)S(1)} all-to-all(f32[256,1,128]{2,1,0:T(1,128)S(1)} %get-tuple-element.133), channel_id=1, replica_groups=mesh['row_0'=4,'row_1'=2,'col_0'=4,'col_1'=8] {'row_0','row_1','col_0','..., dimensions={0} | all-to-all | bytes 262144 | tf_op jit(solution)/shard_map/all_to_all | solution.py:432
  (48 shorter events, 8.4 us)
Async XLA Ops:
  0.6 3.4 %copy-start = (bf16[1,1024,4096]{2,1,0:T(8,128)(2,1)S(1)}, bf16[1,1024,4096]{2,1,0:T(8,128)(2,1)}, u32[]{:S(2)}) copy-start(bf16[1,1024,4096]{2,1,0:T(8,128)(2,1)} %weights.3) | copy-start | bytes 25165828
  4.0 1.0 copy-start.2
  5.1 0.7 copy-start.4
  7.1 13.3 %collective-permute-start.2 = (f32[4,128,128]{2,1,0:T(8,128)S(1)}, f32[4,128,128]{2,1,0:T(8,128)S(1)}, u32[]{:S(2)}, u32[]{:S(2)}) collective-permute-start(f32[4,128,128]{2,1,0:T(8,128)S(1)} %get-tuple-element.80), channel_id=1, source_target_pairs={{0,8},{8,16},{16,24},{24,0},{1,9},{9,17},{17,25},{25,1},{2,10},{10... | collective-permute-start | bytes 786440 | tf_op jit(solution)/shard_map/ppermute | solution.py:383
  8.6 11.8 %collective-permute-start.3 = (f32[4,128,128]{2,1,0:T(8,128)S(1)}, f32[4,128,128]{2,1,0:T(8,128)S(1)}, u32[]{:S(2)}, u32[]{:S(2)}) collective-permute-start(f32[4,128,128]{2,1,0:T(8,128)S(1)} %get-tuple-element.81), channel_id=1, source_target_pairs={{8,0},{16,8},{24,16},{0,24},{9,1},{17,9},{25,17},{1,25},{10,2},{18... | collective-permute-start | bytes 786440 | tf_op jit(solution)/shard_map/ppermute | solution.py:383
  10.4 5.0 %collective-permute-start = (f32[2,128,128]{2,1,0:T(8,128)S(1)}, f32[2,128,128]{2,1,0:T(8,128)S(1)}, u32[]{:S(2)}, u32[]{:S(2)}) collective-permute-start(f32[2,128,128]{2,1,0:T(8,128)S(1)} %get-tuple-element.74), channel_id=1, source_target_pairs={{0,1},{1,2},{2,3},{3,4},{4,5},{5,6},{6,7},{7,0},{8,9},{9,10},{10,1... | collective-permute-start | bytes 393224 | tf_op jit(solution)/shard_map/ppermute | solution.py:383
  12.3 5.0 %collective-permute-start.1 = (f32[2,128,128]{2,1,0:T(8,128)S(1)}, f32[2,128,128]{2,1,0:T(8,128)S(1)}, u32[]{:S(2)}, u32[]{:S(2)}) collective-permute-start(f32[2,128,128]{2,1,0:T(8,128)S(1)} %get-tuple-element.75), channel_id=1, source_target_pairs={{1,0},{2,1},{3,2},{4,3},{5,4},{6,5},{7,6},{0,7},{9,8},{10,9},{11,1... | collective-permute-start | bytes 393224 | tf_op jit(solution)/shard_map/ppermute | solution.py:383
  17.3 7.5 %collective-permute-start.4 = (f32[4,128,128]{2,1,0:T(8,128)S(1)}, f32[4,128,128]{2,1,0:T(8,128)S(1)}, u32[]{:S(2)}, u32[]{:S(2)}) collective-permute-start(f32[4,128,128]{2,1,0:T(8,128)S(1)} %get-tuple-element.85), channel_id=1, source_target_pairs={{0,1},{1,2},{2,3},{3,4},{4,5},{5,6},{6,7},{7,0},{8,9},{9,10},{10,1... | collective-permute-start | bytes 786440 | tf_op jit(solution)/shard_map/ppermute | solution.py:383
  20.4 7.6 %collective-permute-start.5 = (f32[4,128,128]{2,1,0:T(8,128)S(1)}, f32[4,128,128]{2,1,0:T(8,128)S(1)}, u32[]{:S(2)}, u32[]{:S(2)}) collective-permute-start(f32[4,128,128]{2,1,0:T(8,128)S(1)} %get-tuple-element.86), channel_id=1, source_target_pairs={{1,0},{2,1},{3,2},{4,3},{5,4},{6,5},{7,6},{0,7},{9,8},{10,9},{11,1... | collective-permute-start | bytes 786440 | tf_op jit(solution)/shard_map/ppermute | solution.py:383
  20.5 13.0 %collective-permute-start.6 = (f32[8,128,128]{2,1,0:T(8,128)S(1)}, f32[8,128,128]{2,1,0:T(8,128)S(1)}, u32[]{:S(2)}, u32[]{:S(2)}) collective-permute-start(f32[8,128,128]{2,1,0:T(8,128)S(1)} %get-tuple-element.90), channel_id=1, source_target_pairs={{0,8},{8,16},{16,24},{24,0},{1,9},{9,17},{17,25},{25,1},{2,10},{10... | collective-permute-start | bytes 1572872 | tf_op jit(solution)/shard_map/ppermute | solution.py:383
  20.9 12.7 %collective-permute-start.7 = (f32[8,128,128]{2,1,0:T(8,128)S(1)}, f32[8,128,128]{2,1,0:T(8,128)S(1)}, u32[]{:S(2)}, u32[]{:S(2)}) collective-permute-start(f32[8,128,128]{2,1,0:T(8,128)S(1)} %get-tuple-element.91), channel_id=1, source_target_pairs={{8,0},{16,8},{24,16},{0,24},{9,1},{17,9},{25,17},{1,25},{10,2},{18... | collective-permute-start | bytes 1572872 | tf_op jit(solution)/shard_map/ppermute | solution.py:383
  28.0 6.4 %collective-permute-start.8 = (f32[4,128,128]{2,1,0:T(8,128)S(1)}, f32[4,128,128]{2,1,0:T(8,128)S(1)}, u32[]{:S(2)}, u32[]{:S(2)}) collective-permute-start(f32[4,128,128]{2,1,0:T(8,128)S(1)} %get-tuple-element.94), channel_id=1, source_target_pairs={{0,1},{1,2},{2,3},{3,4},{4,5},{5,6},{6,7},{7,0},{8,9},{9,10},{10,1... | collective-permute-start | bytes 786440 | tf_op jit(solution)/shard_map/ppermute | solution.py:383
  30.1 6.4 %collective-permute-start.9 = (f32[4,128,128]{2,1,0:T(8,128)S(1)}, f32[4,128,128]{2,1,0:T(8,128)S(1)}, u32[]{:S(2)}, u32[]{:S(2)}) collective-permute-start(f32[4,128,128]{2,1,0:T(8,128)S(1)} %get-tuple-element.95), channel_id=1, source_target_pairs={{1,0},{2,1},{3,2},{4,3},{5,4},{6,5},{7,6},{0,7},{9,8},{10,9},{11,1... | collective-permute-start | bytes 786440 | tf_op jit(solution)/shard_map/ppermute | solution.py:383
  36.6 23.2 %copy-start.5 = (bf16[256,512]{1,0:T(8,128)(2,1)S(1)}, bf16[256,512]{1,0:T(8,128)(2,1)}, u32[]{:S(2)}) copy-start(bf16[256,512]{1,0:T(8,128)(2,1)} %param.7) | copy-start | bytes 786436
  36.6 27.4 %copy-start.1 = (f32[512,128]{1,0:T(8,128)S(1)}, f32[512,128]{1,0:T(8,128)}, u32[]{:S(2)}) copy-start(f32[512,128]{1,0:T(8,128)} %image.3) | copy-start | bytes 786436
  36.6 27.4 %copy-start.3 = (f32[512,128]{1,0:T(8,128)S(1)}, f32[512,128]{1,0:T(8,128)}, u32[]{:S(2)}) copy-start(f32[512,128]{1,0:T(8,128)} %refs_7_.1) | copy-start | bytes 786436
  36.6 7.2 %collective-permute-start.10 = (f32[4,128,128]{2,1,0:T(8,128)S(1)}, f32[4,128,128]{2,1,0:T(8,128)S(1)}, u32[]{:S(2)}, u32[]{:S(2)}) collective-permute-start(f32[4,128,128]{2,1,0:T(8,128)S(1)} %get-tuple-element.99), channel_id=1, source_target_pairs={{0,1},{1,2},{2,3},{3,4},{4,5},{5,6},{6,7},{7,0},{8,9},{9,10},{10,1... | collective-permute-start | bytes 786440 | tf_op jit(solution)/shard_map/ppermute | solution.py:383
  38.1 6.4 %collective-permute-start.11 = (f32[4,128,128]{2,1,0:T(8,128)S(1)}, f32[4,128,128]{2,1,0:T(8,128)S(1)}, u32[]{:S(2)}, u32[]{:S(2)}) collective-permute-start(f32[4,128,128]{2,1,0:T(8,128)S(1)} %get-tuple-element.100), channel_id=1, source_target_pairs={{1,0},{2,1},{3,2},{4,3},{5,4},{6,5},{7,6},{0,7},{9,8},{10,9},{11,1... | collective-permute-start | bytes 786440 | tf_op jit(solution)/shard_map/ppermute | solution.py:383
  38.7 6.1 %collective-permute-start.12 = (f32[2,64,128]{2,1,0:T(8,128)S(1)}, f32[2,64,128]{2,1,0:T(8,128)S(1)}, u32[]{:S(2)}, u32[]{:S(2)}) collective-permute-start(f32[2,64,128]{2,1,0:T(8,128)S(1)} %get-tuple-element.104), channel_id=1, source_target_pairs={{0,1},{1,2},{2,3},{3,4},{4,5},{5,6},{6,7},{7,0},{8,9},{9,10},{10,1... | collective-permute-start | bytes 196616 | tf_op jit(solution)/shard_map/ppermute | solution.py:383
  44.5 5.6 %collective-permute-start.13 = (f32[2,64,128]{2,1,0:T(8,128)S(1)}, f32[2,64,128]{2,1,0:T(8,128)S(1)}, u32[]{:S(2)}, u32[]{:S(2)}) collective-permute-start(f32[2,64,128]{2,1,0:T(8,128)S(1)} %get-tuple-element.109), channel_id=1, source_target_pairs={{0,8},{8,16},{16,24},{24,0},{1,9},{9,17},{17,25},{25,1},{2,10},{10... | collective-permute-start | bytes 196616 | tf_op jit(solution)/shard_map/ppermute | solution.py:383
  44.9 5.2 %collective-permute-start.14 = (f32[2,64,128]{2,1,0:T(8,128)S(1)}, f32[2,64,128]{2,1,0:T(8,128)S(1)}, u32[]{:S(2)}, u32[]{:S(2)}) collective-permute-start(f32[2,64,128]{2,1,0:T(8,128)S(1)} %get-tuple-element.113), channel_id=1, source_target_pairs={{0,1},{1,2},{2,3},{3,4},{4,5},{5,6},{6,7},{7,0},{8,9},{9,10},{10,1... | collective-permute-start | bytes 196616 | tf_op jit(solution)/shard_map/ppermute | solution.py:383
  46.4 4.5 %collective-permute-start.15 = (f32[2,64,128]{2,1,0:T(8,128)S(1)}, f32[2,64,128]{2,1,0:T(8,128)S(1)}, u32[]{:S(2)}, u32[]{:S(2)}) collective-permute-start(f32[2,64,128]{2,1,0:T(8,128)S(1)} %get-tuple-element.114), channel_id=1, source_target_pairs={{1,0},{2,1},{3,2},{4,3},{5,4},{6,5},{7,6},{0,7},{9,8},{10,9},{11,1... | collective-permute-start | bytes 196616 | tf_op jit(solution)/shard_map/ppermute | solution.py:383
  50.9 5.3 %collective-permute-start.16 = (f32[2,64,128]{2,1,0:T(8,128)S(1)}, f32[2,64,128]{2,1,0:T(8,128)S(1)}, u32[]{:S(2)}, u32[]{:S(2)}) collective-permute-start(f32[2,64,128]{2,1,0:T(8,128)S(1)} %get-tuple-element.118), channel_id=1, source_target_pairs={{0,1},{1,2},{2,3},{3,4},{4,5},{5,6},{6,7},{7,0},{8,9},{9,10},{10,1... | collective-permute-start | bytes 196616 | tf_op jit(solution)/shard_map/ppermute | solution.py:383
  52.9 4.7 %collective-permute-start.17 = (f32[2,64,128]{2,1,0:T(8,128)S(1)}, f32[2,64,128]{2,1,0:T(8,128)S(1)}, u32[]{:S(2)}, u32[]{:S(2)}) collective-permute-start(f32[2,64,128]{2,1,0:T(8,128)S(1)} %get-tuple-element.119), channel_id=1, source_target_pairs={{1,0},{2,1},{3,2},{4,3},{5,4},{6,5},{7,6},{0,7},{9,8},{10,9},{11,1... | collective-permute-start | bytes 196616 | tf_op jit(solution)/shard_map/ppermute | solution.py:383
  53.0 6.9 %collective-permute-start.20 = (f32[2,64,128]{2,1,0:T(8,128)S(1)}, f32[2,64,128]{2,1,0:T(8,128)S(1)}, u32[]{:S(2)}, u32[]{:S(2)}) collective-permute-start(f32[2,64,128]{2,1,0:T(8,128)S(1)} %get-tuple-element.125), channel_id=1, source_target_pairs={{0,8},{8,16},{16,24},{24,0},{1,9},{9,17},{17,25},{25,1},{2,10},{10... | collective-permute-start | bytes 196616 | tf_op jit(solution)/shard_map/ppermute | solution.py:383
  54.3 5.6 %collective-permute-start.21 = (f32[2,64,128]{2,1,0:T(8,128)S(1)}, f32[2,64,128]{2,1,0:T(8,128)S(1)}, u32[]{:S(2)}, u32[]{:S(2)}) collective-permute-start(f32[2,64,128]{2,1,0:T(8,128)S(1)} %get-tuple-element.126), channel_id=1, source_target_pairs={{8,0},{16,8},{24,16},{0,24},{9,1},{17,9},{25,17},{1,25},{10,2},{18... | collective-permute-start | bytes 196616 | tf_op jit(solution)/shard_map/ppermute | solution.py:383
  57.6 4.3 %collective-permute-start.18 = (f32[2,64,128]{2,1,0:T(8,128)S(1)}, f32[2,64,128]{2,1,0:T(8,128)S(1)}, u32[]{:S(2)}, u32[]{:S(2)}) collective-permute-start(f32[2,64,128]{2,1,0:T(8,128)S(1)} %get-tuple-element.123), channel_id=1, source_target_pairs={{0,1},{1,2},{2,3},{3,4},{4,5},{5,6},{6,7},{7,0},{8,9},{9,10},{10,1... | collective-permute-start | bytes 196616 | tf_op jit(solution)/shard_map/ppermute | solution.py:383
  59.7 4.3 %collective-permute-start.19 = (f32[2,64,128]{2,1,0:T(8,128)S(1)}, f32[2,64,128]{2,1,0:T(8,128)S(1)}, u32[]{:S(2)}, u32[]{:S(2)}) collective-permute-start(f32[2,64,128]{2,1,0:T(8,128)S(1)} %get-tuple-element.124), channel_id=1, source_target_pairs={{1,0},{2,1},{3,2},{4,3},{5,4},{6,5},{7,6},{0,7},{9,8},{10,9},{11,1... | collective-permute-start | bytes 196616 | tf_op jit(solution)/shard_map/ppermute | solution.py:383
  75.4 23.4 %collective-permute-start.22 = (f32[32,640]{1,0:T(8,128)S(1)}, f32[32,640]{1,0:T(8,128)S(1)}, u32[]{:S(2)}, u32[]{:S(2)}) collective-permute-start(f32[32,640]{1,0:T(8,128)S(1)} %get-tuple-element.130), channel_id=1, source_target_pairs={{1,0},{2,1},{3,2},{4,3},{5,4},{6,5},{7,6},{8,7},{9,8},{10,9},{11,1... | collective-permute-start | bytes 245768 | tf_op jit(solution)/shard_map/ppermute | solution.py:427
  77.3 21.4 %collective-permute-start.23 = (f32[32,640]{1,0:T(8,128)S(1)}, f32[32,640]{1,0:T(8,128)S(1)}, u32[]{:S(2)}, u32[]{:S(2)}) collective-permute-start(f32[32,640]{1,0:T(8,128)S(1)} %get-tuple-element.131), channel_id=1, source_target_pairs={{0,1},{1,2},{2,3},{3,4},{4,5},{5,6},{6,7},{7,8},{8,9},{9,10},{10,1... | collective-permute-start | bytes 245768 | tf_op jit(solution)/shard_map/ppermute | solution.py:428
